TPU v7x, 32 devices: a whole 2x2x4 slice. The times are simulated.
32 devices in a mesh: section: 2 (over core), dp: 4 (over y, x), tensor: 4 (over z).
Axes of the slice: x: 2, y: 2, z: 4, core: 2. Of those that a mesh axis runs over, the one named last changes fastest.
Arguments:
- inputs: bfloat16 [2, 1536, 1536], P(None, ('dp', 'tensor')), may hold values from -7 to 7
- cotangent: bfloat16 [2, 1536, 1536], P(None, ('dp', 'tensor')), may hold values from -6 to 6
- seq_lengths: int32 [4, 2, 4], P('dp'), may hold values from 0 to 384, as said below
- gain_attn: bfloat16 [2, 1536], P('section'), may hold values from 0.5 to 1.5
- w_query: bfloat16 [2, 1536, 1536], P('section', None, 'tensor'), may hold values from -0.15309311 to 0.15309311
- w_key: bfloat16 [2, 1536, 768], P('section', None, 'tensor'), may hold values from -0.15309311 to 0.15309311
- w_value: bfloat16 [2, 1536, 768], P('section', None, 'tensor'), may hold values from -0.15625 to 0.15625
- w_out: bfloat16 [2, 1536, 1536], P('section', 'tensor'), may hold values from -0.625 to 0.625
- gain_ffn: bfloat16 [2, 1536], P('section'), may hold values from 0.5 to 1.5
- w_gate: bfloat16 [2, 1536, 4096], P('section', None, 'tensor'), may hold values from -0.15625 to 0.15625
- w_up: bfloat16 [2, 1536, 4096], P('section', None, 'tensor'), may hold values from -0.15625 to 0.15625
- w_down: bfloat16 [2, 4096, 1536], P('section', 'tensor'), may hold values from -0.09375 to 0.09375
Outputs:
- section_out: bfloat16 [2, 2, 1536, 1536], P('section', None, ('dp', 'tensor'))
- in_grad: bfloat16 [2, 2, 1536, 1536], P('section', None, ('dp', 'tensor'))
- grad_gain_attn: float32 [2, 1536], P('section')
- grad_w_query: float32 [2, 1536, 1536], P('section', None, 'tensor')
- grad_w_key: float32 [2, 1536, 768], P('section', None, 'tensor')
- grad_w_value: float32 [2, 1536, 768], P('section', None, 'tensor')
- grad_w_out: float32 [2, 1536, 1536], P('section', 'tensor')
- grad_gain_ffn: float32 [2, 1536], P('section')
- grad_w_gate: float32 [2, 1536, 4096], P('section', None, 'tensor')
- grad_w_up: float32 [2, 1536, 4096], P('section', None, 'tensor')
- grad_w_down: float32 [2, 4096, 1536], P('section', 'tensor')
Inputs may be any that keep to these rules, and one draw needn't show every extreme that they name: seq_lengths[d, m, :] are the lengths of the sequences of block (m, d) in order, zeros for unused entries; their sum is at most 384, and in every draw some block holds a single sequence of exactly 384 rows.
All inputs are finite; a program needn't handle non-finite values.
Results may differ from a plain program's by a relative error of at most 0.022.
Values may be sent and summed in bfloat16 or wider, within the bound.
A program may use at most 192 MiB of HBM per device.

v0:
```python
import jax
import jax.numpy as jnp
from jax import lax
from jax.sharding import PartitionSpec as P

HEAD = 96


eps = 1e-05
rope_base = 100000.0
neg_fill = -1e30


def passed_along(shard, axis, by):
    count = lax.axis_size(axis)
    pairs = [(i, i + by) for i in range(count) if 0 <= i + by < count]
    return lax.ppermute(shard, axis, pairs)


def rms_scale(values):
    return lax.rsqrt(jnp.mean(values * values, axis=-1, keepdims=True) + eps)


def matmul_f32(left, right):
    return jnp.dot(left, right, preferred_element_type=jnp.float32)


def rows_product(left, right):
    return lax.dot_general(
        left, right, (((0,), (0,)), ((), ())), preferred_element_type=jnp.float32
    )


def against_product(left, right):
    return lax.dot_general(
        left, right, (((1,), (1,)), ((), ())), preferred_element_type=jnp.float32
    )


def rotate(values, position, direction):
    half_size = values.shape[-1] // 2
    inverse = rope_base ** (-jnp.arange(half_size, dtype=jnp.float32) * 2.0 / values.shape[-1])
    angle = position.astype(jnp.float32)[:, None] * inverse[None, :]
    cosine = jnp.cos(angle)[:, None, :]
    sine = direction * jnp.sin(angle)[:, None, :]
    first = values[..., :half_size]
    second = values[..., half_size:]
    return jnp.concatenate(
        [first * cosine - second * sine, second * cosine + first * sine], axis=-1
    )


def segment_info(lengths_row, row_count):
    slot_count = lengths_row.shape[0]
    seq_ends = jnp.cumsum(lengths_row)
    seq_starts = jnp.concatenate([seq_ends - lengths_row, seq_ends[-1:]])
    row_index = jnp.arange(row_count, dtype=jnp.int32)
    segment = jnp.sum((row_index[:, None] >= seq_ends[None, :]).astype(jnp.int32), axis=1)
    pick = segment[:, None] == jnp.arange(slot_count + 1, dtype=jnp.int32)[None, :]
    position = row_index - jnp.sum(jnp.where(pick, seq_starts[None, :], 0), axis=1)
    allowed = (
        (segment[:, None] == segment[None, :])
        & (row_index[None, :] <= row_index[:, None])
        & (segment[:, None] < slot_count)
    )
    allowed = allowed | (row_index[:, None] == row_index[None, :])
    return (position, allowed)


def collect_rows(values):
    return lax.all_gather(values, "tensor", axis=0, tiled=True)


def collect_again(values):
    return lax.all_gather(values, "tensor", axis=0, tiled=True)


def collect_grads(values):
    return lax.all_gather(values, "tensor", axis=0, tiled=True)


def spread_rows(left, right, share_rows):

    def term(start, count):
        return matmul_f32(left, right)

    return lax.psum_scatter(
        term(jnp.int32(0), share_rows * lax.axis_size("tensor")),
        "tensor",
        scatter_dimension=0,
        tiled=True,
    )


def spread_grads(operand_pairs, share_rows):

    def term(start, count):
        summed = None
        for left, right in operand_pairs:
            part_term = against_product(left, right)
            summed = part_term if summed is None else summed + part_term
        return summed

    return lax.psum_scatter(
        term(jnp.int32(0), share_rows * lax.axis_size("tensor")),
        "tensor",
        scatter_dimension=0,
        tiled=True,
    )


def norm_back(d_normed, resid, scale_rows, gain):
    unit_rows = resid * scale_rows
    gain_part = jnp.sum(d_normed * unit_rows, axis=0)
    d_unit = d_normed * gain
    d_resid = scale_rows * (
        d_unit - unit_rows * jnp.mean(d_unit * unit_rows, axis=-1, keepdims=True)
    )
    return (d_resid, gain_part)


def attend(queries, key_rows, value_rows, allowed):
    full_rows, query_heads, head_size = queries.shape
    kv_count = key_rows.shape[1]
    grouped = queries.reshape(full_rows, kv_count, query_heads // kv_count, head_size)
    scores = jnp.einsum(
        "rkgd,skd->kgrs", grouped, key_rows, preferred_element_type=jnp.float32
    ) * head_size ** (-0.5)
    masked = jnp.where(allowed, scores, neg_fill)
    row_max = jnp.max(masked, axis=-1, keepdims=True)
    exp_scores = jnp.exp(masked - row_max)
    row_total = jnp.sum(exp_scores, axis=-1, keepdims=True)
    probs_low = (exp_scores / row_total).astype(jnp.bfloat16)
    attended = jnp.einsum(
        "kgrs,skd->rkgd", probs_low, value_rows, preferred_element_type=jnp.float32
    )
    return (attended.reshape(full_rows, query_heads * head_size), row_max + jnp.log(row_total))


def attend_back(queries, key_rows, value_rows, log_total, allowed, d_attended):
    full_rows, query_heads, head_size = queries.shape
    kv_count = key_rows.shape[1]
    group_size = query_heads // kv_count
    score_scale = head_size ** (-0.5)
    grouped = queries.reshape(full_rows, kv_count, group_size, head_size)
    scores = (
        jnp.einsum("rkgd,skd->kgrs", grouped, key_rows, preferred_element_type=jnp.float32)
        * score_scale
    )
    probs = jnp.exp(jnp.where(allowed, scores, neg_fill) - log_total)
    d_out = d_attended.reshape(full_rows, kv_count, group_size, head_size)
    d_probs = jnp.einsum("rkgd,skd->kgrs", d_out, value_rows, preferred_element_type=jnp.float32)
    d_scores = (probs * (d_probs - jnp.sum(probs * d_probs, axis=-1, keepdims=True))).astype(
        jnp.bfloat16
    )
    d_values = jnp.einsum(
        "kgrs,rkgd->skd", probs.astype(jnp.bfloat16), d_out, preferred_element_type=jnp.float32
    )
    d_grouped = (
        jnp.einsum("kgrs,skd->rkgd", d_scores, key_rows, preferred_element_type=jnp.float32)
        * score_scale
    )
    d_keys = (
        jnp.einsum("kgrs,rkgd->skd", d_scores, grouped, preferred_element_type=jnp.float32)
        * score_scale
    )
    return (d_grouped.reshape(full_rows, query_heads, head_size), d_keys, d_values)


def layer_forward(resid, position, allowed, weights):
    gain_attn, w_query, w_key, w_value, w_out, gain_ffn, w_gate, w_up, w_down = weights
    share_rows = resid.shape[0]
    scale_attn = rms_scale(resid)
    normed = (resid * scale_attn * gain_attn).astype(jnp.bfloat16)
    normed_all = collect_rows(normed)
    full_rows = normed_all.shape[0]
    queries = rotate(
        matmul_f32(normed_all, w_query).reshape(full_rows, -1, HEAD), position, 1.0
    ).astype(jnp.bfloat16)
    key_rows = rotate(
        matmul_f32(normed_all, w_key).reshape(full_rows, -1, HEAD), position, 1.0
    ).astype(jnp.bfloat16)
    value_rows = matmul_f32(normed_all, w_value).astype(jnp.bfloat16).reshape(full_rows, -1, HEAD)
    attended, log_total = attend(queries, key_rows, value_rows, allowed)
    attended_low = attended.astype(jnp.bfloat16)
    hidden_in = resid + spread_rows(attended_low, w_out, share_rows)
    scale_ffn = rms_scale(hidden_in)
    normed_ffn = (hidden_in * scale_ffn * gain_ffn).astype(jnp.bfloat16)
    normed_ffn_all = collect_rows(normed_ffn)
    gate = matmul_f32(normed_ffn_all, w_gate)
    up_proj = matmul_f32(normed_ffn_all, w_up)
    hidden_low = (jax.nn.silu(gate) * up_proj).astype(jnp.bfloat16)
    result = hidden_in + spread_rows(hidden_low, w_down, share_rows)
    kept = {
        "resid": resid,
        "scale_attn": scale_attn,
        "normed": normed,
        "queries": queries,
        "key_rows": key_rows,
        "value_rows": value_rows,
        "log_total": log_total,
        "attended_low": attended_low,
        "hidden_in": hidden_in,
        "scale_ffn": scale_ffn,
        "normed_ffn": normed_ffn,
        "gate": gate,
        "up_proj": up_proj,
        "hidden_low": hidden_low,
        "position": position,
        "allowed": allowed,
    }
    return (result, kept)


def layer_backward(upstream, kept, weights, accum):
    gain_attn, w_query, w_key, w_value, w_out, gain_ffn, w_gate, w_up, w_down = weights
    (
        acc_gain_attn,
        acc_query,
        acc_key,
        acc_value,
        acc_out,
        acc_gain_ffn,
        acc_gate,
        acc_up,
        acc_down,
    ) = accum
    share_rows = upstream.shape[0]
    ffn_grad_all = collect_grads(upstream.astype(jnp.bfloat16))
    acc_down = acc_down + rows_product(kept["hidden_low"], ffn_grad_all)
    d_hidden = against_product(ffn_grad_all, w_down)
    gate = kept["gate"]
    sigmoid_gate = jax.nn.sigmoid(gate)
    d_gate = (
        d_hidden * kept["up_proj"] * sigmoid_gate * (1.0 + gate * (1.0 - sigmoid_gate))
    ).astype(jnp.bfloat16)
    d_up = (d_hidden * gate * sigmoid_gate).astype(jnp.bfloat16)
    normed_ffn_all = collect_again(kept["normed_ffn"])
    acc_gate = acc_gate + rows_product(normed_ffn_all, d_gate)
    acc_up = acc_up + rows_product(normed_ffn_all, d_up)
    d_normed_ffn = spread_grads(((d_gate, w_gate), (d_up, w_up)), share_rows)
    d_hidden_in, gain_part = norm_back(d_normed_ffn, kept["hidden_in"], kept["scale_ffn"], gain_ffn)
    acc_gain_ffn = acc_gain_ffn + gain_part
    d_hidden_in = upstream + d_hidden_in
    attn_grad_all = collect_grads(d_hidden_in.astype(jnp.bfloat16))
    acc_out = acc_out + rows_product(kept["attended_low"], attn_grad_all)
    d_attended = against_product(attn_grad_all, w_out).astype(jnp.bfloat16)
    d_query, d_keys, d_values = attend_back(
        kept["queries"],
        kept["key_rows"],
        kept["value_rows"],
        kept["log_total"],
        kept["allowed"],
        d_attended,
    )
    full_rows = d_query.shape[0]
    d_query_low = (
        rotate(d_query, kept["position"], -1.0).reshape(full_rows, -1).astype(jnp.bfloat16)
    )
    d_keys_low = rotate(d_keys, kept["position"], -1.0).reshape(full_rows, -1).astype(jnp.bfloat16)
    d_values_low = d_values.reshape(full_rows, -1).astype(jnp.bfloat16)
    normed_all = collect_again(kept["normed"])
    acc_query = acc_query + rows_product(normed_all, d_query_low)
    acc_key = acc_key + rows_product(normed_all, d_keys_low)
    acc_value = acc_value + rows_product(normed_all, d_values_low)
    d_normed = spread_grads(
        ((d_query_low, w_query), (d_keys_low, w_key), (d_values_low, w_value)), share_rows
    )
    d_resid, gain_part = norm_back(d_normed, kept["resid"], kept["scale_attn"], gain_attn)
    acc_gain_attn = acc_gain_attn + gain_part
    d_resid = d_hidden_in + d_resid
    accum = (
        acc_gain_attn,
        acc_query,
        acc_key,
        acc_value,
        acc_out,
        acc_gain_ffn,
        acc_gate,
        acc_up,
        acc_down,
    )
    return (d_resid, accum)


def shards(
    inputs,
    cotangent,
    seq_lengths,
    gain_attn,
    w_query,
    w_key,
    w_value,
    w_out,
    gain_ffn,
    w_gate,
    w_up,
    w_down,
):
    section_index = lax.axis_index("section")
    micro_count = inputs.shape[0]
    share_rows = inputs.shape[1]
    full_rows = share_rows * lax.axis_size("tensor")
    weights = tuple(
        (
            stacked[0].astype(jnp.float32) if stacked.ndim == 2 else stacked[0]
            for stacked in (
                gain_attn,
                w_query,
                w_key,
                w_value,
                w_out,
                gain_ffn,
                w_gate,
                w_up,
                w_down,
            )
        )
    )
    lengths_here = seq_lengths[0]
    outputs_tick = []
    kept_tick = []
    received = jnp.zeros(inputs.shape[1:], jnp.bfloat16)
    for tick_num in range(micro_count + 1):
        batch_num = jnp.clip(tick_num - section_index, 0, micro_count - 1)
        lengths_row = lax.dynamic_index_in_dim(lengths_here, batch_num, 0, keepdims=False)
        position, allowed = segment_info(lengths_row, full_rows)
        entry = jnp.where(
            section_index == 0, inputs[min(tick_num, micro_count - 1)], received
        ).astype(jnp.float32)
        result, kept = layer_forward(entry, position, allowed, weights)
        result_low = result.astype(jnp.bfloat16)
        outputs_tick.append(result_low)
        kept_tick.append(kept)
        if tick_num < micro_count:
            received = passed_along(result_low, "section", 1)
    accum = tuple((jnp.zeros(weight.shape, jnp.float32) for weight in weights))
    grads_tick = []
    received_grad = jnp.zeros(inputs.shape[1:], jnp.bfloat16)
    for back_num in range(micro_count + 1):
        own_grad = cotangent[max(micro_count - 1 - back_num, 0)]
        if back_num == micro_count:
            own_grad = jnp.zeros_like(own_grad)
        upstream = jnp.where(section_index == 1, own_grad, received_grad).astype(jnp.float32)
        d_entry, accum = layer_backward(upstream, kept_tick[micro_count - back_num], weights, accum)
        d_low = d_entry.astype(jnp.bfloat16)
        grads_tick.append(d_low)
        if back_num < micro_count:
            received_grad = passed_along(d_low, "section", -1)
    (
        grad_gain_attn,
        grad_query,
        grad_key,
        grad_value,
        grad_out,
        grad_gain_ffn,
        grad_gate,
        grad_up,
        grad_down,
    ) = accum
    grad_query, grad_key, grad_value, grad_out, grad_gate, grad_up, grad_down = lax.psum(
        (grad_query, grad_key, grad_value, grad_out, grad_gate, grad_up, grad_down), "dp"
    )
    grad_gain_attn, grad_gain_ffn = lax.psum((grad_gain_attn, grad_gain_ffn), ("dp", "tensor"))
    section_out = jnp.stack(
        [
            jnp.where(section_index == 0, outputs_tick[batch_num], outputs_tick[batch_num + 1])
            for batch_num in range(micro_count)
        ]
    )[None]
    in_grad = jnp.stack(
        [
            jnp.where(
                section_index == 0,
                grads_tick[micro_count - batch_num],
                grads_tick[micro_count - 1 - batch_num],
            )
            for batch_num in range(micro_count)
        ]
    )[None]
    return (
        section_out,
        in_grad,
        grad_gain_attn[None],
        grad_query[None],
        grad_key[None],
        grad_value[None],
        grad_out[None],
        grad_gain_ffn[None],
        grad_gate[None],
        grad_up[None],
        grad_down[None],
    )


def solution(mesh):
    placed = (
        P(None, ("dp", "tensor"), None),
        P(None, ("dp", "tensor"), None),
        P("dp", None, None),
        P("section", None),
        P("section", None, "tensor"),
        P("section", None, "tensor"),
        P("section", None, "tensor"),
        P("section", "tensor", None),
        P("section", None),
        P("section", None, "tensor"),
        P("section", None, "tensor"),
        P("section", "tensor", None),
    )
    return jax.shard_map(
        shards,
        mesh=mesh,
        in_specs=placed,
        out_specs=(
            P("section", None, ("dp", "tensor"), None),
            P("section", None, ("dp", "tensor"), None),
            P("section", None),
            P("section", None, "tensor"),
            P("section", None, "tensor"),
            P("section", None, "tensor"),
            P("section", "tensor", None),
            P("section", None),
            P("section", None, "tensor"),
            P("section", None, "tensor"),
            P("section", "tensor", None),
        ),
        check_vma=False,
    )
```

profile of v0, /device:TPU:0, one launch (start us, length us, event | category | flops | bytes accessed | tf_op | source)
XLA Modules:
  0.0 1586.4 jit_solution(5963205858138941223)
XLA Ops:
  15.3 2.4 copy.51
  22.4 21.8 %all-gather.14.cloned.1.call-done = bf16[384,1536]{1,0:T(8,128)(2,1)} async-done(((bf16[96,1536]{1,0:T(8,128)(2,1)}), bf16[384,1536]{1,0:T(8,128)(2,1)}) %all-gather.14.cloned.1.call-update) | async-done | bytes 1179664 | tf_op jit(solution)/shard_map/all_gather | solution.py:71
  54.4 46.4 %reduce-scatter.13.cloned.1.call-done = f32[96,1536]{1,0:T(8,128)} async-done(((f32[384,1536]{1,0:T(8,128)}), f32[96,1536]{1,0:T(8,128)}) %reduce-scatter.13.cloned.1.call-update) | async-done | bytes 589840 | tf_op jit(solution)/shard_map/reduce_scatter | solution.py:87
  103.9 29.8 %all-gather.16.cloned.1.call-done = bf16[384,1536]{1,0:T(8,128)(2,1)} async-done(((bf16[96,1536]{1,0:T(8,128)(2,1)}), bf16[384,1536]{1,0:T(8,128)(2,1)}) %all-gather.16.cloned.1.call-update) | async-done | bytes 1179664 | tf_op jit(solution)/shard_map/all_gather | solution.py:71
  133.6 3.7 fusion.34
  137.4 2.7 multiply_convert_fusion.8
  141.0 2.8 fusion.10
  143.9 47.0 %reduce-scatter.15.cloned.1.call-done = f32[96,1536]{1,0:T(8,128)} async-done(((f32[384,1536]{1,0:T(8,128)}), f32[96,1536]{1,0:T(8,128)}) %reduce-scatter.15.cloned.1.call-update) | async-done | bytes 589840 | tf_op jit(solution)/shard_map/reduce_scatter | solution.py:87
  197.5 29.1 %all-gather.18.cloned.1.call-done = bf16[384,1536]{1,0:T(8,128)(2,1)} async-done(((bf16[96,1536]{1,0:T(8,128)(2,1)}), bf16[384,1536]{1,0:T(8,128)(2,1)}) %all-gather.18.cloned.1.call-update) | async-done | bytes 1179664 | tf_op jit(solution)/shard_map/all_gather | solution.py:71
  237.1 47.1 %reduce-scatter.17.cloned.1.call-done = f32[96,1536]{1,0:T(8,128)} async-done(((f32[384,1536]{1,0:T(8,128)}), f32[96,1536]{1,0:T(8,128)}) %reduce-scatter.17.cloned.1.call-update) | async-done | bytes 589840 | tf_op jit(solution)/shard_map/reduce_scatter | solution.py:87
  287.1 29.7 %all-gather.20.cloned.1.call-done = bf16[384,1536]{1,0:T(8,128)(2,1)} async-done(((bf16[96,1536]{1,0:T(8,128)(2,1)}), bf16[384,1536]{1,0:T(8,128)(2,1)}) %all-gather.20.cloned.1.call-update) | async-done | bytes 1179664 | tf_op jit(solution)/shard_map/all_gather | solution.py:71
  316.9 3.7 fusion.32
  320.6 2.7 multiply_convert_fusion.7
  324.2 2.8 fusion.8
  327.1 47.0 %reduce-scatter.19.cloned.1.call-done = f32[96,1536]{1,0:T(8,128)} async-done(((f32[384,1536]{1,0:T(8,128)}), f32[96,1536]{1,0:T(8,128)}) %reduce-scatter.19.cloned.1.call-update) | async-done | bytes 589840 | tf_op jit(solution)/shard_map/reduce_scatter | solution.py:87
  381.5 29.2 %all-gather.22.cloned.1.call-done = bf16[384,1536]{1,0:T(8,128)(2,1)} async-done(((bf16[96,1536]{1,0:T(8,128)(2,1)}), bf16[384,1536]{1,0:T(8,128)(2,1)}) %all-gather.22.cloned.1.call-update) | async-done | bytes 1179664 | tf_op jit(solution)/shard_map/all_gather | solution.py:71
  410.7 2.5 fusion.79
  422.6 45.3 %reduce-scatter.21.cloned.1.call-done = f32[96,1536]{1,0:T(8,128)} async-done(((f32[384,1536]{1,0:T(8,128)}), f32[96,1536]{1,0:T(8,128)}) %reduce-scatter.21.cloned.1.call-update) | async-done | bytes 589840 | tf_op jit(solution)/shard_map/reduce_scatter | solution.py:87
  471.4 28.3 %all-gather.36.cloned.1.call-done = bf16[1,384,1536]{2,1,0:T(8,128)(2,1)} async-done(((bf16[1,96,1536]{2,1,0:T(8,128)(2,1)}), bf16[1,384,1536]{2,1,0:T(8,128)(2,1)}) %all-gather.36.cloned.1.call-update) | async-done | bytes 1179664 | tf_op jit(solution)/shard_map/all_gather | solution.py:79
  499.7 4.8 fusion.4
  504.5 26.7 %all-gather.24.cloned.1.call-done = bf16[384,1536]{1,0:T(8,128)(2,1)} async-done(((bf16[96,1536]{1,0:T(8,128)(2,1)}), bf16[384,1536]{1,0:T(8,128)(2,1)}) %all-gather.24.cloned.1.call-update) | async-done | bytes 1179664 | tf_op jit(solution)/shard_map/all_gather | solution.py:71
  531.2 2.8 fusion.18
  534.3 3.0 multiply_convert_fusion.5
  538.7 2.8 fusion.41
  541.7 47.0 %reduce-scatter.25.cloned.1.call-done = f32[96,1536]{1,0:T(8,128)} async-done(((f32[384,1536]{1,0:T(8,128)}), f32[96,1536]{1,0:T(8,128)}) %reduce-scatter.25.cloned.1.call-update) | async-done | bytes 589840 | tf_op jit(solution)/shard_map/reduce_scatter | solution.py:104
  593.0 29.0 %all-gather.26.cloned.1.call-done = bf16[384,1536]{1,0:T(8,128)(2,1)} async-done(((bf16[96,1536]{1,0:T(8,128)(2,1)}), bf16[384,1536]{1,0:T(8,128)(2,1)}) %all-gather.26.cloned.1.call-update) | async-done | bytes 1179664 | tf_op jit(solution)/shard_map/all_gather | solution.py:79
  622.1 2.6 convolution_convert_fusion.2
  633.4 47.0 %reduce-scatter.27.cloned.1.call-done = f32[96,1536]{1,0:T(8,128)} async-done(((f32[384,1536]{1,0:T(8,128)}), f32[96,1536]{1,0:T(8,128)}) %reduce-scatter.27.cloned.1.call-update) | async-done | bytes 589840 | tf_op jit(solution)/shard_map/reduce_scatter | solution.py:104
  689.1 29.6 %all-gather.28.cloned.1.call-done = bf16[384,1536]{1,0:T(8,128)(2,1)} async-done(((bf16[96,1536]{1,0:T(8,128)(2,1)}), bf16[384,1536]{1,0:T(8,128)(2,1)}) %all-gather.28.cloned.1.call-update) | async-done | bytes 1179664 | tf_op jit(solution)/shard_map/all_gather | solution.py:79
  718.7 4.9 multiply_convert_fusion.3
  726.1 2.8 fusion.44
  729.0 47.0 %reduce-scatter.29.cloned.1.call-done = f32[96,1536]{1,0:T(8,128)} async-done(((f32[384,1536]{1,0:T(8,128)}), f32[96,1536]{1,0:T(8,128)}) %reduce-scatter.29.cloned.1.call-update) | async-done | bytes 589840 | tf_op jit(solution)/shard_map/reduce_scatter | solution.py:104
  780.9 29.0 %all-gather.30.cloned.1.call-done = bf16[384,1536]{1,0:T(8,128)(2,1)} async-done(((bf16[96,1536]{1,0:T(8,128)(2,1)}), bf16[384,1536]{1,0:T(8,128)(2,1)}) %all-gather.30.cloned.1.call-update) | async-done | bytes 1179664 | tf_op jit(solution)/shard_map/all_gather | solution.py:79
  809.9 2.6 convolution_convert_fusion.1
  821.2 47.0 %reduce-scatter.31.cloned.1.call-done = f32[96,1536]{1,0:T(8,128)} async-done(((f32[384,1536]{1,0:T(8,128)}), f32[96,1536]{1,0:T(8,128)}) %reduce-scatter.31.cloned.1.call-update) | async-done | bytes 589840 | tf_op jit(solution)/shard_map/reduce_scatter | solution.py:104
  870.1 2.6 select_bitcast_fusion
  877.0 29.8 %all-gather.32.cloned.1.call-done = bf16[384,1536]{1,0:T(8,128)(2,1)} async-done(((bf16[96,1536]{1,0:T(8,128)(2,1)}), bf16[384,1536]{1,0:T(8,128)(2,1)}) %all-gather.32.cloned.1.call-update) | async-done | bytes 1179664 | tf_op jit(solution)/shard_map/all_gather | solution.py:79
  906.8 4.9 multiply_convert_fusion.1
  914.2 2.8 fusion.47
  917.1 47.0 %reduce-scatter.33.cloned.1.call-done = f32[96,1536]{1,0:T(8,128)} async-done(((f32[384,1536]{1,0:T(8,128)}), f32[96,1536]{1,0:T(8,128)}) %reduce-scatter.33.cloned.1.call-update) | async-done | bytes 589840 | tf_op jit(solution)/shard_map/reduce_scatter | solution.py:104
  966.7 4.7 fusion.6
  972.6 5.7 fusion.76
  978.4 4.6 fusion.212
  983.0 4.5 fusion.214
  992.8 2.3 fusion.210
  995.1 4.5 fusion.216
  999.6 4.5 fusion.213
  1004.1 4.5 fusion.215
  1008.7 2.6 convolution_convert_fusion
  1020.9 2.9 convolution_add_fusion.8
  1025.4 3.8 convolution_add_fusion.1
  1029.2 2.5 convolution_add_fusion.3
  1031.7 9.0 add_bitcast_fusion
  1040.8 4.7 add_bitcast_fusion.2
  1045.6 4.7 add_bitcast_fusion.1
  1054.3 2.3 fusion.40
  1056.6 2.4 fusion.39
  1062.2 33.9 %reduce-scatter.35.cloned.1.call-done = f32[96,1536]{1,0:T(8,128)} async-done(((f32[384,1536]{1,0:T(8,128)}), f32[96,1536]{1,0:T(8,128)}) %reduce-scatter.35.cloned.1.call-update) | async-done | bytes 589840 | tf_op jit(solution)/shard_map/reduce_scatter | solution.py:104
  1097.5 77.1 %all-reduce = (f32[1,1536]{1,0:T(1,128)}, f32[1,1536]{1,0:T(1,128)}) all-reduce(f32[1,1536]{1,0:T(1,128)S(1)} %broadcast_in_dim.78, f32[1,1536]{1,0:T(1,128)S(1)} %broadcast_in_dim.83), channel_id=1, replica_groups=mesh['section'=2,'dp'=4,'tensor'=4] {'dp','tensor'}, use_global_device_ids=true, to_apply=%region_45.46 | all-reduce | flops 3072 | bytes 24576 | tf_op jit(solution)/shard_map/psum | solution.py:364
  1176.9 381.8 %all-reduce.4.cloned.1.call-done = (f32[1,1536,384]{2,1,0:T(8,128)}, f32[1,1536,192]{1,2,0:T(8,128)}, f32[1,1536,192]{1,2,0:T(8,128)}, f32[1,384,1536]{2,1,0:T(8...) async-done(((f32[1,1536,384]{2,1,0:T(8,128)}, f32[1,1536,192]{1,2,0:T(8,128)}, f32[1,1536,192]{1,2,0:T(8,128)}, ...) | async-done | bytes 25952272 | tf_op jit(solution)/shard_map/psum | solution.py:361
  1558.7 3.4 copy.95
  1567.4 3.2 copy.99
  1570.9 3.2 copy.100
  1575.5 3.2 copy.101
  (634 shorter events, 153.9 us)
Async XLA Ops:
  7.2 130.2 %copy-start = (bf16[1,1536,1024]{2,1,0:T(8,128)(2,1)S(1)}, bf16[1,1536,1024]{2,1,0:T(8,128)(2,1)}, u32[]{:S(2)}) copy-start(bf16[1,1536,1024]{2,1,0:T(8,128)(2,1)} %param.22) | copy-start | bytes 9437188
  7.2 37.1 %all-gather.14.cloned.1.call-start = ((), (), s32[]{:S(2)}) async-start(), calls=%async_computation.12 | async-start | bytes 1474560 | tf_op jit(solution)/shard_map/all_gather | solution.py:71
  11.1 89.7 %reduce-scatter.13.cloned.1.call-start = ((), (), s32[]{:S(2)}) async-start(), calls=%async_computation.13 | async-start | bytes 2949120 | tf_op jit(solution)/shard_map/reduce_scatter | solution.py:87
  53.7 79.9 %all-gather.16.cloned.1.call-start = ((), (), s32[]{:S(2)}) async-start(), calls=%async_computation.14 | async-start | bytes 1474560 | tf_op jit(solution)/shard_map/all_gather | solution.py:71
  103.8 87.0 %reduce-scatter.15.cloned.1.call-start = ((), (), s32[]{:S(2)}) async-start(), calls=%async_computation.15 | async-start | bytes 2949120 | tf_op jit(solution)/shard_map/reduce_scatter | solution.py:87
  143.8 82.8 %all-gather.18.cloned.1.call-start = ((), (), s32[]{:S(2)}) async-start(), calls=%async_computation.16 | async-start | bytes 1474560 | tf_op jit(solution)/shard_map/all_gather | solution.py:71
  192.3 2.5 collective-permute-start
  196.4 87.7 %reduce-scatter.17.cloned.1.call-start = ((), (), s32[]{:S(2)}) async-start(), calls=%async_computation.17 | async-start | bytes 2949120 | tf_op jit(solution)/shard_map/reduce_scatter | solution.py:87
  237.0 79.8 %all-gather.20.cloned.1.call-start = ((), (), s32[]{:S(2)}) async-start(), calls=%async_computation.18 | async-start | bytes 1474560 | tf_op jit(solution)/shard_map/all_gather | solution.py:71
  287.1 87.0 %reduce-scatter.19.cloned.1.call-start = ((), (), s32[]{:S(2)}) async-start(), calls=%async_computation.19 | async-start | bytes 2949120 | tf_op jit(solution)/shard_map/reduce_scatter | solution.py:87
  327.1 83.7 %all-gather.22.cloned.1.call-start = ((), (), s32[]{:S(2)}) async-start(), calls=%async_computation.20 | async-start | bytes 1474560 | tf_op jit(solution)/shard_map/all_gather | solution.py:71
  376.3 2.5 collective-permute-start.1
  380.6 87.3 %reduce-scatter.21.cloned.1.call-start = ((), (), s32[]{:S(2)}) async-start(), calls=%async_computation.21 | async-start | bytes 2949120 | tf_op jit(solution)/shard_map/reduce_scatter | solution.py:87
  420.8 78.9 %all-gather.36.cloned.1.call-start = ((), (), s32[]{:S(2)}) async-start(), calls=%async_computation.35 | async-start | bytes 1474560 | tf_op jit(solution)/shard_map/all_gather | solution.py:79
  422.6 108.7 %all-gather.24.cloned.1.call-start = ((), (), s32[]{:S(2)}) async-start(), calls=%async_computation.22 | async-start | bytes 1474560 | tf_op jit(solution)/shard_map/all_gather | solution.py:71
  469.2 121.1 %copy-start.172 = (f32[96]{0:T(128)}, f32[96]{0:T(128)S(1)}, u32[]{:S(2)}) copy-start(f32[96]{0:T(128)S(1)} %add_rsqrt_fusion) | copy-start | bytes 1156
  470.9 117.7 %reduce-scatter.25.cloned.1.call-start = ((), (), s32[]{:S(2)}) async-start(), calls=%async_computation.24 | async-start | bytes 2949120 | tf_op jit(solution)/shard_map/reduce_scatter | solution.py:104
  541.6 80.5 %all-gather.26.cloned.1.call-start = ((), (), s32[]{:S(2)}) async-start(), calls=%async_computation.25 | async-start | bytes 1474560 | tf_op jit(solution)/shard_map/all_gather | solution.py:79
  592.3 88.1 %reduce-scatter.27.cloned.1.call-start = ((), (), s32[]{:S(2)}) async-start(), calls=%async_computation.26 | async-start | bytes 2949120 | tf_op jit(solution)/shard_map/reduce_scatter | solution.py:104
  633.3 47.1 %copy-start.180 = (f32[96]{0:T(128)S(1)}, f32[96]{0:T(128)}, u32[]{:S(2)}) copy-start(f32[96]{0:T(128)} %copy-done.179) | copy-start | bytes 1156
  633.3 48.6 %copy-start.173 = (f32[96]{0:T(128)S(1)}, f32[96]{0:T(128)}, u32[]{:S(2)}) copy-start(f32[96]{0:T(128)} %copy-done.172) | copy-start | bytes 1156
  633.4 85.3 %all-gather.28.cloned.1.call-start = ((), (), s32[]{:S(2)}) async-start(), calls=%async_computation.27 | async-start | bytes 1474560 | tf_op jit(solution)/shard_map/all_gather | solution.py:79
  680.4 7.7 copy-start.65
  684.6 3.5 collective-permute-start.2
  688.9 87.2 %reduce-scatter.29.cloned.1.call-start = ((), (), s32[]{:S(2)}) async-start(), calls=%async_computation.28 | async-start | bytes 2949120 | tf_op jit(solution)/shard_map/reduce_scatter | solution.py:104
  728.9 47.1 %copy-start.170 = (f32[96]{0:T(128)S(1)}, f32[96]{0:T(128)}, u32[]{:S(2)}) copy-start(f32[96]{0:T(128)} %copy-done.169) | copy-start | bytes 1156
  728.9 80.9 %all-gather.30.cloned.1.call-start = ((), (), s32[]{:S(2)}) async-start(), calls=%async_computation.29 | async-start | bytes 1474560 | tf_op jit(solution)/shard_map/all_gather | solution.py:79
  780.1 88.1 %reduce-scatter.31.cloned.1.call-start = ((), (), s32[]{:S(2)}) async-start(), calls=%async_computation.30 | async-start | bytes 2949120 | tf_op jit(solution)/shard_map/reduce_scatter | solution.py:104
  821.1 47.1 %copy-start.178 = (f32[96]{0:T(128)S(1)}, f32[96]{0:T(128)}, u32[]{:S(2)}) copy-start(f32[96]{0:T(128)} %copy-done.177) | copy-start | bytes 1156
  821.1 49.0 %copy-start.171 = (f32[96]{0:T(128)S(1)}, f32[96]{0:T(128)}, u32[]{:S(2)}) copy-start(f32[96]{0:T(128)} %copy-done.169) | copy-start | bytes 1156
  821.1 85.7 %all-gather.32.cloned.1.call-start = ((), (), s32[]{:S(2)}) async-start(), calls=%async_computation.31 | async-start | bytes 1474560 | tf_op jit(solution)/shard_map/all_gather | solution.py:79
  872.7 3.5 collective-permute-start.3
  876.2 89.4 %copy-start.61 = (bf16[96,1536]{1,0:T(8,128)(2,1)}, bf16[96,1536]{1,0:T(8,128)(2,1)S(1)}, u32[]{:S(2)}) copy-start(bf16[96,1536]{1,0:T(8,128)(2,1)S(1)} %collective-permute-done.3) | copy-start | bytes 884740
  877.0 87.2 %reduce-scatter.33.cloned.1.call-start = ((), (), s32[]{:S(2)}) async-start(), calls=%async_computation.32 | async-start | bytes 2949120 | tf_op jit(solution)/shard_map/reduce_scatter | solution.py:104
  917.0 47.1 %copy-start.14 = (f32[96,1536]{1,0:T(8,128)S(1)}, f32[96,1536]{1,0:T(8,128)}, u32[]{:S(2)}) copy-start(f32[96,1536]{1,0:T(8,128)} %copy-done.13) | copy-start | bytes 1769476
  917.0 47.1 %copy-start.175 = (f32[96]{0:T(128)S(1)}, f32[96]{0:T(128)}, u32[]{:S(2)}) copy-start(f32[96]{0:T(128)} %copy-done.174) | copy-start | bytes 1156
  917.1 49.6 %copy-start.121 = (bf16[384,1024]{1,0:T(8,128)(2,1)S(1)}, bf16[384,1024]{1,0:T(8,128)(2,1)}, u32[]{:S(2)}) copy-start(bf16[384,1024]{1,0:T(8,128)(2,1)} %get-tuple-element.51) | copy-start | bytes 2359300
  917.1 49.5 %copy-start.163 = (f32[2,2,384]{2,1,0:T(2,128)S(1)}, f32[2,2,384]{2,1,0:T(2,128)}, u32[]{:S(2)}) copy-start(f32[2,2,384]{2,1,0:T(2,128)} %copy-done.162) | copy-start | bytes 18436
  917.1 49.5 %copy-start.165 = (f32[2,2,384]{2,1,0:T(2,128)S(1)}, f32[2,2,384]{2,1,0:T(2,128)}, u32[]{:S(2)}) copy-start(f32[2,2,384]{2,1,0:T(2,128)} %copy-done.164) | copy-start | bytes 18436
  917.1 91.6 %all-gather.34.cloned.1.call-start = ((), (), s32[]{:S(2)}) async-start(), calls=%async_computation.33 | async-start | bytes 1474560 | tf_op jit(solution)/shard_map/all_gather | solution.py:79
  966.6 92.6 %reduce-scatter.23.cloned.1.call-start = ((), (), s32[]{:S(2)}) async-start(), calls=%async_computation.23 | async-start | bytes 2949120 | tf_op jit(solution)/shard_map/reduce_scatter | solution.py:87
  971.4 7.0 copy-start.42
  971.4 124.7 %reduce-scatter.35.cloned.1.call-start = ((), (), s32[]{:S(2)}) async-start(), calls=%async_computation.34 | async-start | bytes 2949120 | tf_op jit(solution)/shard_map/reduce_scatter | solution.py:104
  1019.7 539.0 %all-reduce.4.cloned.1.call-start = ((), (), s32[]{:S(2)}) async-start(), calls=%async_computation.36 | async-start | bytes 51904512 | tf_op jit(solution)/shard_map/psum | solution.py:361
  1023.8 7.8 slice-start.8
  1025.3 6.3 slice-start.9
  1025.3 6.3 copy-start.83
  1025.3 6.3 copy-start.106
  1029.1 11.6 slice-start.2
  1029.1 11.6 slice-start.6
  1031.6 9.1 slice-start.3
  1031.7 9.1 slice-start.7
  1031.7 9.1 copy-start.55
  1031.7 9.1 copy-start.110
  1031.7 13.8 slice-start
  1031.7 13.8 slice-start.4
  1059.0 37.0 %copy-start.38 = (bf16[2,96,1536]{2,1,0:T(8,128)(2,1)S(1)}, bf16[2,96,1536]{2,1,0:T(8,128)(2,1)}, u32[]{:S(2)}) copy-start(bf16[2,96,1536]{2,1,0:T(8,128)(2,1)} %param.12) | copy-start | bytes 1769476
  1059.1 37.0 %copy-start.182 = (f32[96]{0:T(128)S(1)}, f32[96]{0:T(128)}, u32[]{:S(2)}) copy-start(f32[96]{0:T(128)} %copy-done.181) | copy-start | bytes 1156
  1059.1 38.4 %copy-start.161 = (f32[1536]{0:T(1024)S(1)}, f32[1536]{0:T(1024)}, u32[]{:S(2)}) copy-start(f32[1536]{0:T(1024)} %get-tuple-element.19) | copy-start | bytes 18436
  1059.1 115.5 %copy-start.46 = (f32[96,1536]{1,0:T(8,128)S(1)}, f32[96,1536]{1,0:T(8,128)}, u32[]{:S(2)}) copy-start(f32[96,1536]{1,0:T(8,128)} %reduce-scatter.33.cloned.1.call-done) | copy-start | bytes 1769476
  1059.1 115.5 %copy-start.62 = (bf16[96,1536]{1,0:T(8,128)(2,1)S(1)}, bf16[96,1536]{1,0:T(8,128)(2,1)}, u32[]{:S(2)}) copy-start(bf16[96,1536]{1,0:T(8,128)(2,1)} %copy-done.61) | copy-start | bytes 884740
  1097.5 78.6 %copy-start.88 = (bf16[1,96,1536]{2,1,0:T(8,128)(2,1)S(1)}, bf16[1,96,1536]{2,1,0:T(8,128)(2,1)}, u32[]{:S(2)}) copy-start(bf16[1,96,1536]{2,1,0:T(8,128)(2,1)} %get-tuple-element.32) | copy-start | bytes 884740
  1564.4 6.2 slice-start.12
  1567.4 7.0 slice-start.10
  (172 other events, 351.0 us)
Sparse Core Ops, SparseCore 0:
  11.2 32.9 all-gather.13
  53.8 46.9 reduce-scatter.12
  104.0 29.6 all-gather.15
  143.9 46.9 reduce-scatter.14
  196.5 29.9 all-gather.17
  237.2 46.9 reduce-scatter.16
  287.2 29.6 all-gather.19
  327.2 46.9 reduce-scatter.18
  380.7 29.9 all-gather.21
  420.9 46.9 reduce-scatter.20
  470.0 29.6 all-gather.35
  501.7 29.4 all-gather.23
  541.7 46.9 reduce-scatter.24
  592.4 29.6 all-gather.25
  633.5 46.9 reduce-scatter.26
  689.0 29.6 all-gather.27
  729.1 46.9 reduce-scatter.28
  780.2 29.6 all-gather.29
  821.3 46.9 reduce-scatter.30
  877.1 29.6 all-gather.31
  917.2 46.9 reduce-scatter.32
  966.7 29.6 all-gather.33
  999.3 46.9 reduce-scatter.22
  1049.0 47.0 reduce-scatter.34
  1102.1 456.5 all-reduce.3
where the time goes:
time: 1600 us; the launch traced here: 1590 us
  waiting for transfers between devices  1200 us (75%)
  matrix products  173 us (11%)
  blocking collectives  77.1 us (5%)
  other arithmetic  56.3 us (4%)
  local copies, waits for them, and re-layouts  53.3 us (3%)
  between operations  16.5 us (1%)
    psum x1, waiting for transfers between devices, shards(): lax.psum((grad_query, grad_key, grad_value, grad_out, grad_gate, grad_up,...  382 us
    reduce_scatter x6, waiting for transfers between devices, spread_grads(): lax.psum_scatter(term(jnp.int32(0), share_rows * lax.axis_size('tensor'))...  269 us
    reduce_scatter x6, waiting for transfers between devices, spread_rows(): lax.psum_scatter(term(jnp.int32(0), share_rows * lax.axis_size('tensor'))...  233 us
    all_gather x6, waiting for transfers between devices, collect_rows(): return lax.all_gather(values, 'tensor', axis=0, tiled=True)  166 us
    all_gather x6, waiting for transfers between devices, collect_grads(): return lax.all_gather(values, 'tensor', axis=0, tiled=True)  146 us
    psum x1, blocking collectives, shards(): lax.psum((grad_gain_attn, grad_gain_ffn), ('dp', 'tensor'))  77.1 us
    dot_general x21, matrix products, rows_product(): lax.dot_general(left, right, (((0,), (0,)), ((), ())), preferred_element_...  72.7 us
    unnamed x422, local copies, waits for them, and re-layouts  50.7 us
  transfers between devices with their start and end apart: 29, of which 27 were waited for; matrix products, arithmetic and copies ran while one was open for 7% of the time, Pallas kernels for 0%

commit v1 on v0

--- a/solution.py
+++ b/solution.py
@@ -85,11 +85,11 @@
         return matmul_f32(left, right)
 
     return lax.psum_scatter(
-        term(jnp.int32(0), share_rows * lax.axis_size("tensor")),
+        term(jnp.int32(0), share_rows * lax.axis_size("tensor")).astype(jnp.bfloat16),
         "tensor",
         scatter_dimension=0,
         tiled=True,
-    )
+    ).astype(jnp.float32)
 
 
 def spread_grads(operand_pairs, share_rows):
@@ -102,11 +102,11 @@
         return summed
 
     return lax.psum_scatter(
-        term(jnp.int32(0), share_rows * lax.axis_size("tensor")),
+        term(jnp.int32(0), share_rows * lax.axis_size("tensor")).astype(jnp.bfloat16),
         "tensor",
         scatter_dimension=0,
         tiled=True,
-    )
+    ).astype(jnp.float32)
 
 
 def norm_back(d_normed, resid, scale_rows, gain):
@@ -358,8 +358,17 @@
         grad_up,
         grad_down,
     ) = accum
-    grad_query, grad_key, grad_value, grad_out, grad_gate, grad_up, grad_down = lax.psum(
-        (grad_query, grad_key, grad_value, grad_out, grad_gate, grad_up, grad_down), "dp"
+    grad_query, grad_key, grad_value, grad_out, grad_gate, grad_up, grad_down = (
+        summed.astype(jnp.float32)
+        for summed in lax.psum(
+            tuple(
+                part.astype(jnp.bfloat16)
+                for part in (
+                    grad_query, grad_key, grad_value, grad_out, grad_gate, grad_up, grad_down
+                )
+            ),
+            "dp",
+        )
     )
     grad_gain_attn, grad_gain_ffn = lax.psum((grad_gain_attn, grad_gain_ffn), ("dp", "tensor"))
     section_out = jnp.stack(

time: 1600 us -> 1150 us (0.72)
  waiting for transfers between devices: 1200 us -> 775 us
  other arithmetic: 56.3 us -> 76.8 us
  matrix products: 173 us -> 156 us
  local copies, waits for them, and re-layouts: 53.3 us -> 36.5 us
    psum x1, waiting for transfers between devices: 382 us -> 172 us  [shards(): lax.psum(tuple((part.astype(jnp.bfloat16) for part in (grad_query, grad_k...]
    reduce_scatter x6, waiting for transfers between devices: 269 us -> 150 us  [spread_grads(): lax.psum_scatter(term(jnp.int32(0), share_rows * lax.axis_size('tensor'))...]
    reduce_scatter x6, waiting for transfers between devices: 233 us -> 141 us  [spread_rows(): lax.psum_scatter(term(jnp.int32(0), share_rows * lax.axis_size('tensor'))...]
    broadcast_in_dim x0 -> x7, other arithmetic: none -> 17.4 us  [the longest x1 3.58 us: shards(): grad_down[None]]
    unnamed x422 -> x377, local copies, waits for them, and re-layouts: 50.7 us -> 34 us
  transfers between devices with their start and end apart: 29 -> 29, of which waited for: 27 -> 27; matrix products, arithmetic and copies ran while one was open for 7% -> 9% of each run, Pallas kernels for 0% -> 0%
where the time goes in v1:
time: 1150 us; the launch traced here: 1140 us
  waiting for transfers between devices  775 us (67%)
  matrix products  156 us (14%)
  other arithmetic  76.8 us (7%)
  blocking collectives  76.4 us (7%)
  local copies, waits for them, and re-layouts  36.5 us (3%)
  between operations  16.4 us (1%)
    psum x1, waiting for transfers between devices, shards(): lax.psum(tuple((part.astype(jnp.bfloat16) for part in (grad_query, grad_k...  172 us
    all_gather x6, waiting for transfers between devices, collect_rows(): return lax.all_gather(values, 'tensor', axis=0, tiled=True)  163 us
    reduce_scatter x6, waiting for transfers between devices, spread_grads(): lax.psum_scatter(term(jnp.int32(0), share_rows * lax.axis_size('tensor'))...  150 us
    all_gather x6, waiting for transfers between devices, collect_grads(): return lax.all_gather(values, 'tensor', axis=0, tiled=True)  142 us
    reduce_scatter x6, waiting for transfers between devices, spread_rows(): lax.psum_scatter(term(jnp.int32(0), share_rows * lax.axis_size('tensor'))...  141 us
    psum x1, blocking collectives, shards(): lax.psum((grad_gain_attn, grad_gain_ffn), ('dp', 'tensor'))  76.4 us
    dot_general x21, matrix products, rows_product(): lax.dot_general(left, right, (((0,), (0,)), ((), ())), preferred_element_...  60.8 us
    dot_general x21, matrix products, matmul_f32(): return jnp.dot(left, right, preferred_element_type=jnp.float32)  44 us
  transfers between devices with their start and end apart: 29, of which 27 were waited for; matrix products, arithmetic and copies ran while one was open for 9% of the time, Pallas kernels for 0%

profile of v1, /device:TPU:0, one launch (start us, length us, event | category | flops | bytes accessed | tf_op | source)
XLA Modules:
  0.0 1144.8 jit_solution(15275083800491831807)
XLA Ops:
  15.7 2.4 copy.51
  23.0 21.8 %all-gather.14.cloned.1.call-done = bf16[384,1536]{1,0:T(8,128)(2,1)} async-done(((bf16[96,1536]{1,0:T(8,128)(2,1)}), bf16[384,1536]{1,0:T(8,128)(2,1)}) %all-gather.14.cloned.1.call-update) | async-done | bytes 1179664 | tf_op jit(solution)/shard_map/all_gather | solution.py:71
  44.8 2.5 fusion.121
  54.6 28.6 %reduce-scatter.13.cloned.1.call-done = bf16[96,1536]{1,0:T(8,128)(2,1)} async-done(((bf16[384,1536]{1,0:T(8,128)(2,1)}), bf16[96,1536]{1,0:T(8,128)(2,1)}) %reduce-scatter.13.cloned.1.call-update) | async-done | bytes 294928 | tf_op jit(solution)/shard_map/reduce_scatter | solution.py:87
  87.0 29.0 %all-gather.16.cloned.1.call-done = bf16[384,1536]{1,0:T(8,128)(2,1)} async-done(((bf16[96,1536]{1,0:T(8,128)(2,1)}), bf16[384,1536]{1,0:T(8,128)(2,1)}) %all-gather.16.cloned.1.call-update) | async-done | bytes 1179664 | tf_op jit(solution)/shard_map/all_gather | solution.py:71
  116.0 3.7 fusion.37
  119.8 2.7 multiply_convert_fusion.8
  123.4 2.4 fusion.65
  125.9 28.6 %reduce-scatter.15.cloned.1.call-done = bf16[96,1536]{1,0:T(8,128)(2,1)} async-done(((bf16[384,1536]{1,0:T(8,128)(2,1)}), bf16[96,1536]{1,0:T(8,128)(2,1)}) %reduce-scatter.15.cloned.1.call-update) | async-done | bytes 294928 | tf_op jit(solution)/shard_map/reduce_scatter | solution.py:87
  162.0 28.2 %all-gather.18.cloned.1.call-done = bf16[384,1536]{1,0:T(8,128)(2,1)} async-done(((bf16[96,1536]{1,0:T(8,128)(2,1)}), bf16[384,1536]{1,0:T(8,128)(2,1)}) %all-gather.18.cloned.1.call-update) | async-done | bytes 1179664 | tf_op jit(solution)/shard_map/all_gather | solution.py:71
  190.3 2.6 fusion.111
  200.0 28.6 %reduce-scatter.17.cloned.1.call-done = bf16[96,1536]{1,0:T(8,128)(2,1)} async-done(((bf16[384,1536]{1,0:T(8,128)(2,1)}), bf16[96,1536]{1,0:T(8,128)(2,1)}) %reduce-scatter.17.cloned.1.call-update) | async-done | bytes 294928 | tf_op jit(solution)/shard_map/reduce_scatter | solution.py:87
  232.2 29.0 %all-gather.20.cloned.1.call-done = bf16[384,1536]{1,0:T(8,128)(2,1)} async-done(((bf16[96,1536]{1,0:T(8,128)(2,1)}), bf16[384,1536]{1,0:T(8,128)(2,1)}) %all-gather.20.cloned.1.call-update) | async-done | bytes 1179664 | tf_op jit(solution)/shard_map/all_gather | solution.py:71
  261.2 3.7 fusion.35
  265.0 2.7 multiply_convert_fusion.7
  268.7 2.4 fusion.68
  271.1 28.6 %reduce-scatter.19.cloned.1.call-done = bf16[96,1536]{1,0:T(8,128)(2,1)} async-done(((bf16[384,1536]{1,0:T(8,128)(2,1)}), bf16[96,1536]{1,0:T(8,128)(2,1)}) %reduce-scatter.19.cloned.1.call-update) | async-done | bytes 294928 | tf_op jit(solution)/shard_map/reduce_scatter | solution.py:87
  307.0 28.4 %all-gather.22.cloned.1.call-done = bf16[384,1536]{1,0:T(8,128)(2,1)} async-done(((bf16[96,1536]{1,0:T(8,128)(2,1)}), bf16[384,1536]{1,0:T(8,128)(2,1)}) %all-gather.22.cloned.1.call-update) | async-done | bytes 1179664 | tf_op jit(solution)/shard_map/all_gather | solution.py:71
  335.5 2.5 fusion.107
  346.9 26.9 %reduce-scatter.21.cloned.1.call-done = bf16[96,1536]{1,0:T(8,128)(2,1)} async-done(((bf16[384,1536]{1,0:T(8,128)(2,1)}), bf16[96,1536]{1,0:T(8,128)(2,1)}) %reduce-scatter.21.cloned.1.call-update) | async-done | bytes 294928 | tf_op jit(solution)/shard_map/reduce_scatter | solution.py:87
  377.5 27.3 %all-gather.36.cloned.1.call-done = bf16[1,384,1536]{2,1,0:T(8,128)(2,1)} async-done(((bf16[1,96,1536]{2,1,0:T(8,128)(2,1)}), bf16[1,384,1536]{2,1,0:T(8,128)(2,1)}) %all-gather.36.cloned.1.call-update) | async-done | bytes 1179664 | tf_op jit(solution)/shard_map/all_gather | solution.py:79
  404.9 4.8 fusion.7
  409.7 26.7 %all-gather.24.cloned.1.call-done = bf16[384,1536]{1,0:T(8,128)(2,1)} async-done(((bf16[96,1536]{1,0:T(8,128)(2,1)}), bf16[384,1536]{1,0:T(8,128)(2,1)}) %all-gather.24.cloned.1.call-update) | async-done | bytes 1179664 | tf_op jit(solution)/shard_map/all_gather | solution.py:71
  436.4 2.8 fusion.21
  439.5 2.9 multiply_convert_fusion.5
  443.8 2.4 fusion.57
  446.4 28.7 %reduce-scatter.25.cloned.1.call-done = bf16[96,1536]{1,0:T(8,128)(2,1)} async-done(((bf16[384,1536]{1,0:T(8,128)(2,1)}), bf16[96,1536]{1,0:T(8,128)(2,1)}) %reduce-scatter.25.cloned.1.call-update) | async-done | bytes 294928 | tf_op jit(solution)/shard_map/reduce_scatter | solution.py:104
  476.6 2.2 fusion.249
  479.6 28.2 %all-gather.26.cloned.1.call-done = bf16[384,1536]{1,0:T(8,128)(2,1)} async-done(((bf16[96,1536]{1,0:T(8,128)(2,1)}), bf16[384,1536]{1,0:T(8,128)(2,1)}) %all-gather.26.cloned.1.call-update) | async-done | bytes 1179664 | tf_op jit(solution)/shard_map/all_gather | solution.py:79
  507.8 2.6 convolution_convert_fusion.5
  519.1 28.7 %reduce-scatter.27.cloned.1.call-done = bf16[96,1536]{1,0:T(8,128)(2,1)} async-done(((bf16[384,1536]{1,0:T(8,128)(2,1)}), bf16[96,1536]{1,0:T(8,128)(2,1)}) %reduce-scatter.27.cloned.1.call-update) | async-done | bytes 294928 | tf_op jit(solution)/shard_map/reduce_scatter | solution.py:104
  553.0 2.2 collective-permute-done.2
  556.2 28.8 %all-gather.28.cloned.1.call-done = bf16[384,1536]{1,0:T(8,128)(2,1)} async-done(((bf16[96,1536]{1,0:T(8,128)(2,1)}), bf16[384,1536]{1,0:T(8,128)(2,1)}) %all-gather.28.cloned.1.call-update) | async-done | bytes 1179664 | tf_op jit(solution)/shard_map/all_gather | solution.py:79
  585.0 4.9 multiply_convert_fusion.3
  592.4 2.4 fusion.54
  594.9 28.7 %reduce-scatter.29.cloned.1.call-done = bf16[96,1536]{1,0:T(8,128)(2,1)} async-done(((bf16[384,1536]{1,0:T(8,128)(2,1)}), bf16[96,1536]{1,0:T(8,128)(2,1)}) %reduce-scatter.29.cloned.1.call-update) | async-done | bytes 294928 | tf_op jit(solution)/shard_map/reduce_scatter | solution.py:104
  628.4 28.2 %all-gather.30.cloned.1.call-done = bf16[384,1536]{1,0:T(8,128)(2,1)} async-done(((bf16[96,1536]{1,0:T(8,128)(2,1)}), bf16[384,1536]{1,0:T(8,128)(2,1)}) %all-gather.30.cloned.1.call-update) | async-done | bytes 1179664 | tf_op jit(solution)/shard_map/all_gather | solution.py:79
  656.6 2.6 convolution_convert_fusion.4
  667.9 28.7 %reduce-scatter.31.cloned.1.call-done = bf16[96,1536]{1,0:T(8,128)(2,1)} async-done(((bf16[384,1536]{1,0:T(8,128)(2,1)}), bf16[96,1536]{1,0:T(8,128)(2,1)}) %reduce-scatter.31.cloned.1.call-update) | async-done | bytes 294928 | tf_op jit(solution)/shard_map/reduce_scatter | solution.py:104
  698.4 2.4 select_bitcast_fusion
  702.2 2.2 collective-permute-done.3
  705.9 29.0 %all-gather.32.cloned.1.call-done = bf16[384,1536]{1,0:T(8,128)(2,1)} async-done(((bf16[96,1536]{1,0:T(8,128)(2,1)}), bf16[384,1536]{1,0:T(8,128)(2,1)}) %all-gather.32.cloned.1.call-update) | async-done | bytes 1179664 | tf_op jit(solution)/shard_map/all_gather | solution.py:79
  734.8 4.9 multiply_convert_fusion.1
  742.2 2.4 fusion.51
  744.8 28.6 %reduce-scatter.33.cloned.1.call-done = bf16[96,1536]{1,0:T(8,128)(2,1)} async-done(((bf16[384,1536]{1,0:T(8,128)(2,1)}), bf16[96,1536]{1,0:T(8,128)(2,1)}) %reduce-scatter.33.cloned.1.call-update) | async-done | bytes 294928 | tf_op jit(solution)/shard_map/reduce_scatter | solution.py:104
  776.8 4.3 fusion.71
  782.4 3.0 fusion.258
  785.5 4.5 fusion.260
  790.0 4.5 fusion.104
  801.1 4.5 fusion.261
  805.7 4.5 fusion.262
  810.2 2.8 convolution_add_fusion.3
  816.0 2.2 convolution_add_fusion.1
  818.2 3.7 fusion
  821.9 2.6 convolution_convert_fusion.3
  833.6 8.6 fusion.1
  842.3 8.5 fusion.2
  861.4 6.5 reduce-scatter.35.cloned.1.call-done
  869.3 76.4 %all-reduce = (f32[1,1536]{1,0:T(1,128)}, f32[1,1536]{1,0:T(1,128)}) all-reduce(f32[1,1536]{1,0:T(1,128)S(1)} %broadcast_in_dim.99, f32[1,1536]{1,0:T(1,128)S(1)} %broadcast_in_dim.108), channel_id=1, replica_groups=mesh['section'=2,'dp'=4,'tensor'=4] {'dp','tensor'}, use_global_device_ids=true, to_apply=%region_45.46 | all-reduce | flops 3072 | bytes 24576 | tf_op jit(solution)/shard_map/psum | solution.py:373
  947.9 171.7 %all-reduce.4.cloned.1.call-done = (bf16[1,1536,384]{2,1,0:T(8,128)(2,1)}, bf16[1,1536,192]{1,2,0:T(8,128)(2,1)}, bf16[1,1536,192]{1,2,0:T(8,128)(2,1)}, bf16[1,...) async-done(((bf16[1,1536,384]{2,1,0:T(8,128)(2,1)}, bf16[1,1536,192]{1,2,0:T(8,128)(2,1)}, ...) | async-done | bytes 12976144 | tf_op jit(solution)/shard_map/psum | solution.py:363
  1119.6 2.9 broadcast_in_dim.101
  1127.6 3.5 broadcast_in_dim.110
  1131.0 3.5 broadcast_in_dim.112
  1134.5 3.6 broadcast_in_dim.114
  (589 shorter events, 147.8 us)
Async XLA Ops:
  7.2 112.5 %copy-start = (bf16[1,1536,1024]{2,1,0:T(8,128)(2,1)S(1)}, bf16[1,1536,1024]{2,1,0:T(8,128)(2,1)}, u32[]{:S(2)}) copy-start(bf16[1,1536,1024]{2,1,0:T(8,128)(2,1)} %param.22) | copy-start | bytes 9437188
  7.2 37.6 %all-gather.14.cloned.1.call-start = ((), (), s32[]{:S(2)}) async-start(), calls=%async_computation.12 | async-start | bytes 1474560 | tf_op jit(solution)/shard_map/all_gather | solution.py:71
  11.7 71.5 %reduce-scatter.13.cloned.1.call-start = ((), (), s32[]{:S(2)}) async-start(), calls=%async_computation.13 | async-start | bytes 1474560 | tf_op jit(solution)/shard_map/reduce_scatter | solution.py:87
  54.5 61.5 %all-gather.16.cloned.1.call-start = ((), (), s32[]{:S(2)}) async-start(), calls=%async_computation.14 | async-start | bytes 1474560 | tf_op jit(solution)/shard_map/all_gather | solution.py:71
  87.0 67.5 %reduce-scatter.15.cloned.1.call-start = ((), (), s32[]{:S(2)}) async-start(), calls=%async_computation.15 | async-start | bytes 1474560 | tf_op jit(solution)/shard_map/reduce_scatter | solution.py:87
  123.4 31.1 %copy-start.27 = (bf16[96,1536]{1,0:T(8,128)(2,1)S(1)}, bf16[96,1536]{1,0:T(8,128)(2,1)}, u32[]{:S(2)}) copy-start(bf16[96,1536]{1,0:T(8,128)(2,1)} %reduce-scatter.13.cloned.1.call-done) | copy-start | bytes 884740
  125.8 64.5 %all-gather.18.cloned.1.call-start = ((), (), s32[]{:S(2)}) async-start(), calls=%async_computation.16 | async-start | bytes 1474560 | tf_op jit(solution)/shard_map/all_gather | solution.py:71
  155.7 2.6 collective-permute-start
  160.9 67.7 %reduce-scatter.17.cloned.1.call-start = ((), (), s32[]{:S(2)}) async-start(), calls=%async_computation.17 | async-start | bytes 1474560 | tf_op jit(solution)/shard_map/reduce_scatter | solution.py:87
  200.0 61.3 %all-gather.20.cloned.1.call-start = ((), (), s32[]{:S(2)}) async-start(), calls=%async_computation.18 | async-start | bytes 1474560 | tf_op jit(solution)/shard_map/all_gather | solution.py:71
  232.2 67.6 %reduce-scatter.19.cloned.1.call-start = ((), (), s32[]{:S(2)}) async-start(), calls=%async_computation.19 | async-start | bytes 1474560 | tf_op jit(solution)/shard_map/reduce_scatter | solution.py:87
  271.1 64.4 %all-gather.22.cloned.1.call-start = ((), (), s32[]{:S(2)}) async-start(), calls=%async_computation.20 | async-start | bytes 1474560 | tf_op jit(solution)/shard_map/all_gather | solution.py:71
  299.8 4.6 copy-start.25
  301.9 2.5 collective-permute-start.1
  306.1 67.7 %reduce-scatter.21.cloned.1.call-start = ((), (), s32[]{:S(2)}) async-start(), calls=%async_computation.21 | async-start | bytes 1474560 | tf_op jit(solution)/shard_map/reduce_scatter | solution.py:87
  345.1 59.8 %all-gather.36.cloned.1.call-start = ((), (), s32[]{:S(2)}) async-start(), calls=%async_computation.35 | async-start | bytes 1474560 | tf_op jit(solution)/shard_map/all_gather | solution.py:79
  346.9 89.5 %all-gather.24.cloned.1.call-start = ((), (), s32[]{:S(2)}) async-start(), calls=%async_computation.22 | async-start | bytes 1474560 | tf_op jit(solution)/shard_map/all_gather | solution.py:71
  375.1 101.4 %copy-start.169 = (f32[96]{0:T(128)}, f32[96]{0:T(128)S(1)}, u32[]{:S(2)}) copy-start(f32[96]{0:T(128)S(1)} %add_rsqrt_fusion) | copy-start | bytes 1156
  377.0 98.0 %reduce-scatter.25.cloned.1.call-start = ((), (), s32[]{:S(2)}) async-start(), calls=%async_computation.24 | async-start | bytes 1474560 | tf_op jit(solution)/shard_map/reduce_scatter | solution.py:104
  446.3 61.5 %all-gather.26.cloned.1.call-start = ((), (), s32[]{:S(2)}) async-start(), calls=%async_computation.25 | async-start | bytes 1474560 | tf_op jit(solution)/shard_map/all_gather | solution.py:79
  478.8 69.0 %reduce-scatter.27.cloned.1.call-start = ((), (), s32[]{:S(2)}) async-start(), calls=%async_computation.26 | async-start | bytes 1474560 | tf_op jit(solution)/shard_map/reduce_scatter | solution.py:104
  517.2 30.6 %copy-start.177 = (f32[96]{0:T(128)S(1)}, f32[96]{0:T(128)}, u32[]{:S(2)}) copy-start(f32[96]{0:T(128)} %copy-done.176) | copy-start | bytes 1156
  519.0 30.2 %copy-start.170 = (f32[96]{0:T(128)S(1)}, f32[96]{0:T(128)}, u32[]{:S(2)}) copy-start(f32[96]{0:T(128)} %copy-done.169) | copy-start | bytes 1156
  519.1 65.9 %all-gather.28.cloned.1.call-start = ((), (), s32[]{:S(2)}) async-start(), calls=%async_computation.27 | async-start | bytes 1474560 | tf_op jit(solution)/shard_map/all_gather | solution.py:79
  547.8 7.4 copy-start.63
  551.7 3.5 collective-permute-start.2
  556.0 67.6 %reduce-scatter.29.cloned.1.call-start = ((), (), s32[]{:S(2)}) async-start(), calls=%async_computation.28 | async-start | bytes 1474560 | tf_op jit(solution)/shard_map/reduce_scatter | solution.py:104
  592.4 31.2 %copy-start.165 = (f32[96]{0:T(128)S(1)}, f32[96]{0:T(128)}, u32[]{:S(2)}) copy-start(f32[96]{0:T(128)} %copy-done.164) | copy-start | bytes 1156
  594.8 61.8 %all-gather.30.cloned.1.call-start = ((), (), s32[]{:S(2)}) async-start(), calls=%async_computation.29 | async-start | bytes 1474560 | tf_op jit(solution)/shard_map/all_gather | solution.py:79
  627.6 69.0 %reduce-scatter.31.cloned.1.call-start = ((), (), s32[]{:S(2)}) async-start(), calls=%async_computation.30 | async-start | bytes 1474560 | tf_op jit(solution)/shard_map/reduce_scatter | solution.py:104
  666.0 30.6 %copy-start.175 = (f32[96]{0:T(128)S(1)}, f32[96]{0:T(128)}, u32[]{:S(2)}) copy-start(f32[96]{0:T(128)} %copy-done.174) | copy-start | bytes 1156
  667.9 30.6 %copy-start.166 = (f32[96]{0:T(128)S(1)}, f32[96]{0:T(128)}, u32[]{:S(2)}) copy-start(f32[96]{0:T(128)} %copy-done.164) | copy-start | bytes 1156
  667.9 66.9 %all-gather.32.cloned.1.call-start = ((), (), s32[]{:S(2)}) async-start(), calls=%async_computation.31 | async-start | bytes 1474560 | tf_op jit(solution)/shard_map/all_gather | solution.py:79
  700.9 3.5 collective-permute-start.3
  705.8 67.6 %reduce-scatter.33.cloned.1.call-start = ((), (), s32[]{:S(2)}) async-start(), calls=%async_computation.32 | async-start | bytes 1474560 | tf_op jit(solution)/shard_map/reduce_scatter | solution.py:104
  742.2 31.2 %copy-start.26 = (bf16[2,96,1536]{2,1,0:T(8,128)(2,1)S(1)}, bf16[2,96,1536]{2,1,0:T(8,128)(2,1)}, u32[]{:S(2)}) copy-start(bf16[2,96,1536]{2,1,0:T(8,128)(2,1)} %param.12) | copy-start | bytes 1769476
  742.2 31.2 %copy-start.28 = (bf16[96,1536]{1,0:T(8,128)(2,1)S(1)}, bf16[96,1536]{1,0:T(8,128)(2,1)}, u32[]{:S(2)}) copy-start(bf16[96,1536]{1,0:T(8,128)(2,1)} %reduce-scatter.13.cloned.1.call-done) | copy-start | bytes 884740
  742.2 31.2 %copy-start.168 = (f32[96]{0:T(128)S(1)}, f32[96]{0:T(128)}, u32[]{:S(2)}) copy-start(f32[96]{0:T(128)} %copy-done.167) | copy-start | bytes 1156
  744.7 30.1 %copy-start.58 = (bf16[96,1536]{1,0:T(8,128)(2,1)S(1)}, bf16[96,1536]{1,0:T(8,128)(2,1)}, u32[]{:S(2)}) copy-start(bf16[96,1536]{1,0:T(8,128)(2,1)} %copy-done.57) | copy-start | bytes 884740
  744.7 32.1 %copy-start.158 = (f32[2,2,384]{2,1,0:T(2,128)S(1)}, f32[2,2,384]{2,1,0:T(2,128)}, u32[]{:S(2)}) copy-start(f32[2,2,384]{2,1,0:T(2,128)} %copy-done.157) | copy-start | bytes 18436
  744.7 32.1 %copy-start.160 = (f32[2,2,384]{2,1,0:T(2,128)S(1)}, f32[2,2,384]{2,1,0:T(2,128)}, u32[]{:S(2)}) copy-start(f32[2,2,384]{2,1,0:T(2,128)} %copy-done.159) | copy-start | bytes 18436
  744.7 32.1 %copy-start.113 = (bf16[384,1024]{1,0:T(8,128)(2,1)S(1)}, bf16[384,1024]{1,0:T(8,128)(2,1)}, u32[]{:S(2)}) copy-start(bf16[384,1024]{1,0:T(8,128)(2,1)} %get-tuple-element.45) | copy-start | bytes 2359300
  744.7 77.2 %all-gather.34.cloned.1.call-start = ((), (), s32[]{:S(2)}) async-start(), calls=%async_computation.33 | async-start | bytes 1474560 | tf_op jit(solution)/shard_map/all_gather | solution.py:79
  776.7 81.6 %reduce-scatter.23.cloned.1.call-start = ((), (), s32[]{:S(2)}) async-start(), calls=%async_computation.23 | async-start | bytes 1474560 | tf_op jit(solution)/shard_map/reduce_scatter | solution.py:87
  781.2 86.8 %reduce-scatter.35.cloned.1.call-start = ((), (), s32[]{:S(2)}) async-start(), calls=%async_computation.34 | async-start | bytes 1474560 | tf_op jit(solution)/shard_map/reduce_scatter | solution.py:104
  785.4 4.6 copy-start.89
  785.5 4.5 copy-start.114
  790.0 4.6 copy-start.24
  790.0 4.6 copy-start.62
  801.1 4.6 copy-start.91
  801.1 4.6 copy-start.112
  805.7 4.5 copy-start.54
  832.4 287.3 %all-reduce.4.cloned.1.call-start = ((), (), s32[]{:S(2)}) async-start(), calls=%async_computation.36 | async-start | bytes 25952256 | tf_op jit(solution)/shard_map/psum | solution.py:363
  833.6 8.6 copy-start.78
  833.6 8.6 copy-start.100
  842.2 8.5 copy-start.20
  842.3 8.5 copy-start.48
  842.3 8.5 copy-start.77
  858.3 9.6 copy-start.173
  858.3 10.9 copy-start.156
  858.3 87.3 %copy-start.59 = (bf16[96,1536]{1,0:T(8,128)(2,1)S(1)}, bf16[96,1536]{1,0:T(8,128)(2,1)}, u32[]{:S(2)}) copy-start(bf16[96,1536]{1,0:T(8,128)(2,1)} %copy-done.57) | copy-start | bytes 884740
  858.3 87.3 %copy-start.60 = (bf16[96,1536]{1,0:T(8,128)(2,1)S(1)}, bf16[96,1536]{1,0:T(8,128)(2,1)}, u32[]{:S(2)}) copy-start(bf16[96,1536]{1,0:T(8,128)(2,1)} %reduce-scatter.33.cloned.1.call-done) | copy-start | bytes 884740
  858.3 87.3 %copy-start.80 = (bf16[96,1536]{1,0:T(8,128)(2,1)S(1)}, bf16[96,1536]{1,0:T(8,128)(2,1)}, u32[]{:S(2)}) copy-start(bf16[96,1536]{1,0:T(8,128)(2,1)} %copy-done.79) | copy-start | bytes 884740
  861.4 85.7 %copy-start.88 = (bf16[1,96,1536]{2,1,0:T(8,128)(2,1)S(1)}, bf16[1,96,1536]{2,1,0:T(8,128)(2,1)}, u32[]{:S(2)}) copy-start(bf16[1,96,1536]{2,1,0:T(8,128)(2,1)} %get-tuple-element.32) | copy-start | bytes 884740
  (153 other events, 259.6 us)
Sparse Core Ops, SparseCore 0:
  11.8 32.9 all-gather.13
  54.6 28.5 reduce-scatter.12
  87.1 28.8 all-gather.15
  125.9 28.5 reduce-scatter.14
  161.0 29.1 all-gather.17
  200.1 28.5 reduce-scatter.16
  232.3 28.8 all-gather.19
  271.2 28.5 reduce-scatter.18
  306.2 29.1 all-gather.21
  345.2 28.5 reduce-scatter.20
  376.0 28.8 all-gather.35
  406.9 29.4 all-gather.23
  446.4 28.5 reduce-scatter.24
  478.9 28.8 all-gather.25
  519.2 28.5 reduce-scatter.26
  556.1 28.8 all-gather.27
  595.0 28.5 reduce-scatter.28
  627.7 28.8 all-gather.29
  668.0 28.5 reduce-scatter.30
  705.9 28.8 all-gather.31
  744.8 28.5 reduce-scatter.32
  776.9 28.8 all-gather.33
  808.7 28.5 reduce-scatter.22
  840.0 27.9 reduce-scatter.34
  873.9 245.6 all-reduce.3

commit v2 on v0

v2 whole, which is shorter than its diff:
```python
import functools

import jax
import jax.numpy as jnp
from jax import lax
from jax.experimental import pallas as pl
from jax.experimental.pallas import tpu as pltpu
from jax.sharding import PartitionSpec as P

HEAD = 96
HALF = HEAD // 2
LANES = 128
CHUNKS = 2
BF16 = jnp.bfloat16
F32 = jnp.float32
MESH = pl.DeviceIdType.MESH
VMEM = pltpu.VMEM
VMEM_SPEC = pl.BlockSpec(memory_space=pltpu.VMEM)
HBM_SPEC = pl.BlockSpec(memory_space=pltpu.HBM)
DMA = pltpu.SemaphoreType.DMA

eps = 1e-05
rope_base = 100000.0
neg_fill = -1e30


def dot_nn(left, right):
    return lax.dot_general(left, right, (((1,), (0,)), ((), ())), preferred_element_type=F32)


def dot_nt(left, right):
    return lax.dot_general(left, right, (((1,), (1,)), ((), ())), preferred_element_type=F32)


def dot_tn(left, right):
    return lax.dot_general(left, right, (((0,), (0,)), ((), ())), preferred_element_type=F32)


def rms_scale(values):
    return lax.rsqrt(jnp.mean(values * values, axis=-1, keepdims=True) + eps)


def norm_back(d_normed, resid, gain):
    scale_rows = rms_scale(resid)
    unit_rows = resid * scale_rows
    gain_part = jnp.sum(d_normed * unit_rows, axis=0, keepdims=True)
    d_unit = d_normed * gain
    inner = jnp.mean(d_unit * unit_rows, axis=-1, keepdims=True)
    return scale_rows * (d_unit - unit_rows * inner), gain_part


class Line:
    def __init__(self, count, full, rbuf, sbuf, gs, gr, ss, sr):
        self.n = count
        self.core = lax.axis_index("section")
        self.me = lax.axis_index("tensor")
        self.full, self.rbuf, self.sbuf = full, rbuf, sbuf
        self.gs, self.gr, self.ss, self.sr = gs, gr, ss, sr
        self.rows = full.shape[1] // CHUNKS

    def span(self, c):
        return pl.ds(c * self.rows, self.rows)

    def neighbour(self, d):
        return self.me + 1 if d == 0 else self.me - 1

    def enter(self, also=()):
        me, n = self.me, self.n
        barrier = pltpu.get_barrier_semaphore()
        for peer in ({"section": 1 - self.core}, *also):
            pl.semaphore_signal(barrier, 1, device_id=peer, device_id_type=MESH)
        for d, there in ((1, me > 0), (0, me < n - 1)):

            @pl.when(there)
            def _():
                pl.semaphore_signal(
                    barrier, 1, device_id={"tensor": self.neighbour(d)}, device_id_type=MESH
                )

        peers = 1 + len(also) + (me > 0).astype(jnp.int32) + (me < n - 1).astype(jnp.int32)
        pl.semaphore_wait(barrier, peers)

    def gather_copy(self, d, step, shard, c):
        ref = self.full.at[shard, self.span(c)]
        return pltpu.make_async_remote_copy(
            ref,
            ref,
            self.gs.at[d, step, c],
            self.gr.at[d, step, c],
            device_id={"tensor": self.neighbour(d)},
            device_id_type=MESH,
        )

    def gather_step(self, step):
        me, n = self.me, self.n
        for c in range(CHUNKS):
            for d in range(2):
                shard = me - step if d == 0 else me + step
                holds = (shard >= 0) & (shard < n)
                onward = (me + 1 < n) if d == 0 else (me > 0)

                @pl.when(holds & (step > 0))
                def _():
                    self.gather_copy(d, step - 1, shard, c).wait_recv()

                @pl.when(holds & onward)
                def _():
                    self.gather_copy(d, step, shard, c).start()

    def gather_end(self):
        me, n = self.me, self.n

        @pl.loop(0, n - 1)
        def _(step):
            for c in range(CHUNKS):
                for d in range(2):
                    shard = me - step if d == 0 else me + step
                    onward = (me + 1 < n) if d == 0 else (me > 0)

                    @pl.when((shard >= 0) & (shard < n) & onward)
                    def _():
                        self.gather_copy(d, step, shard, c).wait_send()

    def sum_copy(self, d, shard, c):
        return pltpu.make_async_remote_copy(
            self.sbuf.at[shard, self.span(c)],
            self.rbuf.at[d, shard, self.span(c)],
            self.ss.at[d, shard, c],
            self.sr.at[d, shard, c],
            device_id={"tensor": self.neighbour(d)},
            device_id_type=MESH,
        )

    def sum_step(self, d, shard, partial):
        me, n = self.me, self.n
        goes = (shard > me) & (shard < n) if d == 0 else (shard >= 0) & (shard < me)
        first = (me == 0) if d == 0 else (me == n - 1)

        @pl.when(goes & first)
        def _():
            mine = partial(shard)
            for c in range(CHUNKS):
                rows = slice(c * self.rows, (c + 1) * self.rows)
                self.sbuf[shard, self.span(c)] = mine[rows].astype(BF16)
                self.sum_copy(d, shard, c).start()

        @pl.when(goes & jnp.logical_not(first))
        def _():
            mine = partial(shard)
            for c in range(CHUNKS):
                rows = slice(c * self.rows, (c + 1) * self.rows)
                self.sum_copy(d, shard, c).wait_recv()
                arrived = self.rbuf[d, shard, self.span(c)].astype(F32)
                self.sbuf[shard, self.span(c)] = (mine[rows] + arrived).astype(BF16)
                self.sum_copy(d, shard, c).start()

    def sum_take(self, total):
        me, n = self.me, self.n
        for d, there in ((0, me > 0), (1, me < n - 1)):

            @pl.when(there)
            def _():
                for c in range(CHUNKS):
                    self.sum_copy(d, me, c).wait_recv()
                    total[self.span(c)] += self.rbuf[d, me, self.span(c)].astype(F32)

    def sum_end(self):
        me, n = self.me, self.n

        @pl.loop(0, n)
        def _(shard):
            for d, goes in ((0, shard > me), (1, shard < me)):

                @pl.when(goes)
                def _():
                    for c in range(CHUNKS):
                        self.sum_copy(d, shard, c).wait_send()


def line_scratch(count, rows, width):
    return [
        VMEM((count, rows, width), BF16),
        VMEM((2, count, rows, width), BF16),
        VMEM((count, rows, width), BF16),
        DMA((2, count, CHUNKS)),
        DMA((2, count, CHUNKS)),
        DMA((2, count, CHUNKS)),
        DMA((2, count, CHUNKS)),
    ]


def rows_then_sums(line, compute, partial, halfway=lambda: None):
    me, n = line.me, line.n

    @pl.loop(0, 2 * n - 1)
    def _(step):
        @pl.when((step > 0) & (step < n))
        def _():
            line.gather_step(step)

        @pl.when(step < n)
        def _():
            @pl.loop(0, 2)
            def _(side):
                shard = jnp.where(side == 0, me - step, me + step)

                @pl.when((shard >= 0) & (shard < n) & ((step > 0) | (side == 0)))
                def _():
                    compute(shard)

        line.sum_step(0, step - me, partial)
        line.sum_step(1, 2 * (n - 1) - step - me, partial)

        @pl.when(step == n - 1)
        def _():
            halfway()


def later_shards(line, compute):
    me, n = line.me, line.n

    @pl.loop(0, n)
    def _(step):
        @pl.when(step > 0)
        def _():
            line.gather_step(step)

        @pl.loop(0, 2)
        def _(side):
            shard = jnp.where(side == 0, me - step, me + step)

            @pl.when((shard >= 0) & (shard < n) & ((step > 0) | (side == 0)))
            def _():
                compute(shard)


def sums_after(line, partial):
    me, n = line.me, line.n

    @pl.loop(0, n - 1)
    def _(step):
        line.sum_step(0, me + n - 1 - step, partial)
        line.sum_step(1, step - (n - 1 - me), partial)


class Weights:
    def __init__(self, layer, sems):
        self.own = lax.axis_index("section") == layer
        self.sems = sems
        self.wanted = []

    def want(self, mine, theirs, target):
        self.wanted.append((mine, theirs, target))

    def start_own(self):
        @pl.when(self.own)
        def _():
            for index, (mine, _theirs, target) in enumerate(self.wanted):
                pltpu.make_async_copy(mine, target, self.sems.at[index]).start()

    def start_other(self, before=lambda: None):
        @pl.when(jnp.logical_not(self.own))
        def _():
            before()
            for index, (_mine, theirs, target) in enumerate(self.wanted):
                pltpu.make_async_copy(theirs, target, self.sems.at[index]).start()

    def start(self):
        self.start_own()
        self.start_other()

    def wait(self):
        for index, (mine, _theirs, target) in enumerate(self.wanted):
            pltpu.make_async_copy(mine, target, self.sems.at[index]).wait()


class Pair:
    def __init__(self, local_sems, send_sems, recv_sems):
        self.core = lax.axis_index("section")
        self.sems = local_sems, send_sems, recv_sems
        self.kept, self.sent = [], []

    def keep(self, source, target):
        copy = pltpu.make_async_copy(source, target, self.sems[0].at[len(self.kept)])
        copy.start()
        self.kept.append(copy)

    def copy(self, source, target, index):
        return pltpu.make_async_remote_copy(
            source,
            target,
            self.sems[1].at[index],
            self.sems[2].at[index],
            device_id={"section": 1 - self.core},
            device_id_type=MESH,
        )

    def send(self, source, target):
        copy = self.copy(source, target, len(self.sent))
        copy.start()
        self.sent.append(copy)

    def share(self, source, pair):
        self.keep(source, pair.at[0])
        self.send(source, pair.at[1])

    def share_half(self, halves, pair):
        self.keep(halves.at[self.core], pair.at[0])
        self.send(halves.at[1 - self.core], pair.at[1])

    def wait(self):
        for copy in self.kept:
            copy.wait()
        for copy in self.sent:
            copy.wait()


def pair_scratch(kept, sent):
    return [DMA((max(kept, 1),)), DMA((max(sent, 1),)), DMA((max(sent, 1),))]


class Cube:
    def __init__(self, layer, count):
        self.bits = count.bit_length() - 1
        assert count == 1 << self.bits
        self.me = lax.axis_index("dp")
        self.core = lax.axis_index("section")
        self.active = self.core == layer
        self.bit = [(self.me // (1 << b)) % 2 for b in range(self.bits)]
        self.down = list(range(self.bits - 1, -1, -1))

    def order(self, colour):
        return list(range(self.bits)) if colour == 0 else self.down

    def peer(self, b):
        return {"dp": self.me + (1 - 2 * self.bit[b]) * (1 << b)}

    def peers(self):
        return [self.peer(b) for b in range(self.bits)]


class Reduce(Cube):
    def __init__(self, layer, count, sources, outs, scratch):
        super().__init__(layer, count)
        self.sources, self.outs = sources, outs
        size = len(sources)
        self.accs = scratch[:size]
        self.recvs = [scratch[size * (t + 1) : size * (t + 2)] for t in range(self.bits)]
        self.local, self.ss, self.sr, self.fs, self.fr = scratch[size * (self.bits + 1) :]
        self.t = 0
        self.place = [
            {b: slice(None) for b in self.down if b != self.order(c)[0]} for c in range(2)
        ]

    def items(self):
        return [(a, c) for a in range(len(self.sources)) for c in range(2)]

    def spot(self, c, changed=()):
        place = {**self.place[c], **dict(changed)}
        return (c, *(place[b] for b in self.down if b in place))

    def first_half(self, a, c, value):
        b = self.order(c)[0]
        index = [slice(None)] * self.bits
        index[self.down.index(b)] = value
        return self.sources[a].at[(c, *index)]

    def copy(self, a, c, t, source):
        return pltpu.make_async_remote_copy(
            source,
            self.recvs[t][a].at[c],
            self.ss.at[a, c, t],
            self.sr.at[a, c, t],
            device_id=self.peer(self.order(c)[t]),
            device_id_type=MESH,
        )

    def kept(self, a, c):
        mine = self.first_half(a, c, self.bit[self.order(c)[0]])
        return pltpu.make_async_copy(mine, self.accs[a].at[c], self.local.at[a, c])

    def start(self):
        for a, c in self.items():
            other = self.first_half(a, c, 1 - self.bit[self.order(c)[0]])
            self.copy(a, c, 0, other).start()
            self.kept(a, c).start()

    def advance(self):
        t = self.t
        if t >= self.bits:
            return
        for a, c in self.items():
            if t == 0:
                self.kept(a, c).wait()
            self.copy(a, c, t, self.recvs[t][a].at[c]).wait_recv()
            acc, spot = self.accs[a], self.spot(c)
            acc[spot] = (acc[spot].astype(F32) + self.recvs[t][a][c].astype(F32)).astype(BF16)
            if t + 1 < self.bits:
                b = self.order(c)[t + 1]
                self.copy(a, c, t + 1, acc.at[self.spot(c, [(b, 1 - self.bit[b])])]).start()
        if t + 1 < self.bits:
            for c in range(2):
                b = self.order(c)[t + 1]
                self.place[c][b] = self.bit[b]
        self.t = t + 1

    def hand_over(self, a, c):
        return pltpu.make_async_remote_copy(
            self.accs[a].at[self.spot(c)],
            self.outs[a].at[self.core, c],
            self.fs.at[a, c],
            self.fr.at[a, c],
            device_id={"section": 1 - self.core},
            device_id_type=MESH,
        )

    def put_away(self, a, c):
        return pltpu.make_async_copy(
            self.accs[a].at[self.spot(c)], self.outs[a].at[self.core, c], self.fs.at[a, c]
        )

    def finish(self):
        while self.t < self.bits:
            self.advance()

        @pl.when(self.active)
        def _():
            for a, c in self.items():
                self.put_away(a, c).start()

        @pl.when(jnp.logical_not(self.active))
        def _():
            for a, c in self.items():
                self.hand_over(a, c).start()

        for a, c in self.items():
            for t in range(self.bits):
                self.copy(a, c, t, self.recvs[t][a].at[c]).wait_send()

        @pl.when(self.active)
        def _():
            for a, c in self.items():
                self.put_away(a, c).wait()
                self.hand_over(a, c).wait_recv()

        @pl.when(jnp.logical_not(self.active))
        def _():
            for a, c in self.items():
                self.hand_over(a, c).wait_send()


class Gather(Cube):
    def __init__(self, layer, count, blocks, outs, sems):
        super().__init__(layer, count)
        self.blocks, self.outs = blocks, outs
        self.keep, self.ss, self.sr = sems
        self.t = 0

    def items(self):
        return [(a, h, c) for a in range(len(self.blocks)) for h in range(2) for c in range(2)]

    def order(self, colour):
        return super().order(colour)[::-1]

    def region(self, a, h, c, t):
        free = self.order(c)[:t]
        index = (slice(None) if b in free else self.bit[b] for b in self.down)
        return self.outs[a].at[(h, c, *index)]

    def copy(self, a, h, c, t):
        target = self.region(a, h, c, t)
        return pltpu.make_async_remote_copy(
            self.blocks[a].at[h, c] if t == 0 else target,
            target,
            self.ss.at[a, h, c, t],
            self.sr.at[a, h, c, t],
            device_id=self.peer(self.order(c)[t]),
            device_id_type=MESH,
        )

    def kept(self, a, h, c):
        return pltpu.make_async_copy(
            self.blocks[a].at[h, c], self.region(a, h, c, 0), self.keep.at[a, h, c]
        )

    def start(self):
        @pl.when(self.active)
        def _():
            for a, h, c in self.items():
                self.copy(a, h, c, 0).start()
                self.kept(a, h, c).start()

    def advance(self):
        t = self.t
        if t >= self.bits:
            return

        @pl.when(self.active)
        def _():
            for a, h, c in self.items():
                if t == 0:
                    self.kept(a, h, c).wait()
                self.copy(a, h, c, t).wait_recv()
                if t + 1 < self.bits:
                    self.copy(a, h, c, t + 1).start()

        self.t = t + 1

    def finish(self):
        while self.t < self.bits:
            self.advance()

        @pl.when(self.active)
        def _():
            for a, h, c in self.items():
                for t in range(self.bits):
                    self.copy(a, h, c, t).wait_send()


def reduce_scratch(count, arrays):
    bits = count.bit_length() - 1
    scratch = []
    for level in (1, *range(1, bits + 1)):
        scratch += [VMEM((2,) + (2,) * (bits - level) + shape[-2:], BF16) for shape in arrays]
    size = len(arrays)
    return scratch + [
        DMA((size, 2)),
        DMA((size, 2, bits)),
        DMA((size, 2, bits)),
        DMA((size, 2)),
        DMA((size, 2)),
    ]


def gather_sems(count, size):
    bits = count.bit_length() - 1
    return [DMA((size, 2, 2)), DMA((size, 2, 2, bits)), DMA((size, 2, 2, bits))]


class Tasks:
    def __init__(self, count, plan):
        self.count = count
        self.reduce = plan.get("reduce")
        self.gather = plan.get("gather")

    def arguments(self):
        args = list(self.reduce[1]) if self.reduce else []
        return args + (list(self.gather[1]) if self.gather else [])

    def outputs(self):
        outs = []
        if self.reduce:
            outs += [((2, 2) + ref.shape[-2:], BF16, HBM_SPEC) for ref in self.reduce[1]]
        if self.gather:
            middle = (2,) * (self.count.bit_length() - 1)
            outs += [
                ((2, 2) + middle + ref.shape[-2:], BF16, HBM_SPEC) for ref in self.gather[1]
            ]
        return outs

    def scratch(self):
        scratch = []
        if self.reduce:
            scratch += reduce_scratch(self.count, [ref.shape for ref in self.reduce[1]])
        if self.gather:
            scratch += [VMEM(ref.shape, BF16) for ref in self.gather[1]]
            scratch += [DMA((len(self.gather[1]),))]
            scratch += gather_sems(self.count, len(self.gather[1]))
        return scratch

    def bind(self, args, outs, scratch):
        self.running = []
        self.loads = []
        count = self.count
        if self.reduce:
            size = len(self.reduce[1])
            used = len(reduce_scratch(count, [ref.shape for ref in self.reduce[1]]))
            self.running.append(
                Reduce(self.reduce[0], count, args[:size], outs[:size], scratch[:used])
            )
            args, outs, scratch = args[size:], outs[size:], scratch[used:]
        if self.gather:
            size = len(self.gather[1])
            blocks = scratch[:size]
            self.loads = [
                pltpu.make_async_copy(args[a], blocks[a], scratch[size].at[a]) for a in range(size)
            ]
            self.running.append(
                Gather(self.gather[0], count, blocks, outs, scratch[size + 1 : size + 4])
            )
        for load in self.loads:
            load.start()

    def peers(self):
        return self.running[0].peers() if self.running else []

    def start(self):
        for load in self.loads:
            load.wait()
        for task in self.running:
            task.start()

    def advance(self):
        for task in self.running:
            task.advance()

    def finish(self):
        for task in self.running:
            task.finish()


def pick_split(columns):
    heads = columns // HEAD
    col = lax.broadcasted_iota(jnp.int32, (columns, heads * LANES), 1)
    row = lax.broadcasted_iota(jnp.int32, (columns, heads * LANES), 0)
    inner = col & 63
    source = (col >> 7) * HEAD + ((col >> 6) & 1) * HALF + inner
    return ((row == source) & (inner < HALF)).astype(F32).astype(BF16)


def pick_plain(columns):
    heads = columns // HEAD
    col = lax.broadcasted_iota(jnp.int32, (columns, heads * LANES), 1)
    row = lax.broadcasted_iota(jnp.int32, (columns, heads * LANES), 0)
    inner = col & 127
    return ((row == (col >> 7) * HEAD + inner) & (inner < HEAD)).astype(F32).astype(BF16)


def rotated(values, cosine, sine):
    return values * cosine + pltpu.roll(values, LANES // 2, 1) * sine


def spread_qkv(wq, wk, wv, wqkv):
    q_wide = wq.shape[1] // HEAD * LANES
    k_wide = wk.shape[1] // HEAD * LANES
    wqkv[:, :q_wide] = dot_nn(wq[...], pick_split(wq.shape[1])).astype(BF16)
    wqkv[:, q_wide : q_wide + k_wide] = dot_nn(wk[...], pick_split(wk.shape[1])).astype(BF16)
    wqkv[:, q_wide + k_wide :] = dot_nn(wv[...], pick_plain(wv.shape[1])).astype(BF16)


def allowed_pairs(seg_col, seg_row):
    full_rows = seg_col.shape[0]
    row = lax.broadcasted_iota(jnp.int32, (full_rows, full_rows), 0)
    col = lax.broadcasted_iota(jnp.int32, (full_rows, full_rows), 1)
    return (seg_col[...] == seg_row[...]) & (col <= row)


def lane_block(index):
    return pl.ds(pl.multiple_of(index * LANES, LANES), LANES)


def head_rows(ref, index):
    return ref[:, :, lane_block(index)].reshape(-1, LANES)


def attn_weights(weights, wo, sources):
    wq0, wq1, wk0, wk1, wv0, wv1, wo0, wo1 = sources[:8]
    wq, wk, wv = sources[8:]
    weights.want(wq0.at[0], wq1.at[0], wq)
    weights.want(wk0.at[0], wk1.at[0], wk)
    weights.want(wv0.at[0], wv1.at[0], wv)
    for h in range(wo.shape[0]):
        rows = pl.ds(h * HEAD, HEAD)
        weights.want(wo0.at[0, rows], wo1.at[0, rows], wo.at[h, pl.ds(0, HEAD)])


def clear_pads(wo):
    for h in range(wo.shape[0]):
        wo[h, HEAD:] = jnp.zeros((LANES - HEAD, wo.shape[2]), BF16)


def probabilities(queries, keys, allowed):
    scores = jnp.where(allowed, dot_nt(queries, keys) * HEAD ** (-0.5), neg_fill)
    exp_scores = jnp.exp(scores - jnp.max(scores, axis=-1, keepdims=True))
    return exp_scores / jnp.sum(exp_scores, axis=-1, keepdims=True)


def attn_fwd_kernel(layer, n, heads, kv_heads, others, *refs):
    x, gain, cos, sin, seg_col, seg_row = refs[:6]
    own = refs[6 : 6 + others]
    at = 6 + others
    if layer == 0:
        h_out, n_out, qkv_out, o_out = refs[at : at + 4]
        other = refs[at + 4 : at + 4 + others]
    else:
        other = refs[at : at + others]
        h_out, n_out, qkv_out, o_out = refs[at + others : at + others + 4]
    at += 4 + others
    (wq, wk, wv, wo, wqkv, qkv, o, osmall, wsem) = refs[at : at + 9]
    pair = Pair(*refs[at + 9 : at + 12])
    line = Line(n, *refs[at + 12 :])
    me = line.me
    group = heads // kv_heads
    weights = Weights(layer, wsem)
    sources = [ref for both in zip(own[:4], other[:4]) for ref in both] + [wq, wk, wv]
    attn_weights(weights, wo, sources)
    resid = x[...].astype(F32)
    line.full[me] = (resid * rms_scale(resid) * gain[...]).astype(BF16)
    clear_pads(wo)
    if layer == 0:
        weights.start_own()
        line.enter()
        line.gather_step(0)
        for mine, theirs in zip(own, other):
            pair.send(mine, theirs)

        def arrived():
            for index in range(4):
                pair.copy(own[index], other[index], index).wait_recv()

        weights.start_other(arrived)
    else:
        weights.start()
        line.enter()
        line.gather_step(0)
    weights.wait()
    spread_qkv(wq, wk, wv, wqkv)

    def compute(shard):
        products = dot_nn(line.full[shard], wqkv[...])
        for head in range(heads + kv_heads):
            lanes = slice(head * LANES, (head + 1) * LANES)
            qkv[shard, :, lanes] = rotated(products[:, lanes], cos[shard], sin[shard]).astype(BF16)
        lanes = slice((heads + kv_heads) * LANES, None)
        qkv[shard, :, lanes] = products[:, lanes].astype(BF16)

    later_shards(line, compute)
    pair.share(line.full, n_out)
    pair.keep(qkv, qkv_out)
    allowed = allowed_pairs(seg_col, seg_row)

    @pl.loop(0, kv_heads)
    def _(g):
        keys = head_rows(qkv, heads + g)
        values = head_rows(qkv, heads + kv_heads + g)
        rows = []
        for member in range(group):
            h = g * group + member
            probs = probabilities(head_rows(qkv, h), keys, allowed)
            attended = dot_nn(probs.astype(BF16), values).astype(BF16)
            o[:, :, lane_block(h)] = attended.reshape(n, -1, LANES)
            rows.append(attended)
        small = dot_nt(jnp.concatenate(rows, axis=1), pick_plain(group * HEAD))
        osmall[g] = small.astype(BF16).reshape(osmall.shape[1:])

    pair.share_half(osmall, o_out)
    wide = wo.shape[0] * LANES

    def partial(shard):
        return dot_nn(o[shard], wo[...].reshape(wide, -1))

    sums_after(line, partial)
    h_out[...] = resid + partial(me)
    line.sum_take(h_out)
    line.gather_end()
    line.sum_end()
    if layer == 0:
        for index, copy in enumerate(pair.sent[:others]):
            copy.wait_send()
            if index >= 4:
                copy.wait_recv()

        @pl.when(weights.own)
        def _():
            for index in range(4):
                pair.copy(own[index], other[index], index).wait_recv()

        pair.sent = pair.sent[others:]
    pair.wait()


def bound(tasks, sizes, refs):
    groups, at = [], 0
    for own, extra in sizes:
        groups.append((refs[at : at + own], refs[at + own : at + own + extra]))
        at += own + extra
    tasks.bind(*(list(extra) for _, extra in groups))
    return [ref for own, _ in groups for ref in own]


def attn_bwd_kernel(layer, n, heads, kv_heads, tasks, sizes, *refs):
    refs = bound(tasks, sizes, refs)
    (dh, x, gain, cos, sin, seg_col, seg_row, qkv_in) = refs[:8]
    own, other = refs[8:12], refs[12:16]
    (dx_out, gain_out, da_out, dqkv_out) = refs[16:20]
    (wq, wk, wv, wo, wqkv, qkv, d_o, dqkv, dsmall, total, wsem, tsem) = refs[20:32]
    pair = Pair(*refs[32:35])
    line = Line(n, *refs[35:])
    me = line.me
    group = heads // kv_heads
    weights = Weights(layer, wsem)
    sources = [ref for both in zip(own, other) for ref in both] + [wq, wk, wv]
    attn_weights(weights, wo, sources)
    weights.start()
    take = pltpu.make_async_copy(qkv_in, qkv, tsem)
    take.start()
    line.full[me] = dh[...].astype(BF16)
    clear_pads(wo)
    line.enter(tasks.peers())
    line.gather_step(0)
    tasks.start()
    weights.wait()
    spread_qkv(wq, wk, wv, wqkv)
    take.wait()
    wide = wo.shape[0] * LANES

    def compute(shard):
        d_o[shard] = dot_nt(line.full[shard], wo[...].reshape(wide, -1)).astype(BF16)

    later_shards(line, compute)
    pair.share(line.full, da_out)
    tasks.advance()
    allowed = allowed_pairs(seg_col, seg_row)
    cosine = cos[...].reshape(-1, LANES)
    sine = -sin[...].reshape(-1, LANES)
    scale = HEAD ** (-0.5)

    @pl.loop(0, kv_heads)
    def _(g):
        keys = head_rows(qkv, heads + g)
        values = head_rows(qkv, heads + kv_heads + g)
        d_keys = d_values = None
        turned = []
        for member in range(group):
            h = g * group + member
            queries = head_rows(qkv, h)
            d_out = head_rows(d_o, h)
            probs = probabilities(queries, keys, allowed)
            d_probs = dot_nt(d_out, values)
            inner = jnp.sum(probs * d_probs, axis=-1, keepdims=True)
            d_scores = (probs * (d_probs - inner)).astype(BF16)
            d_queries = dot_nn(d_scores, keys) * scale
            turned.append(rotated(d_queries, cosine, sine).astype(BF16))
            dqkv[:, :, lane_block(h)] = turned[-1].reshape(n, -1, LANES)
            dk = dot_tn(d_scores, queries)
            dv = dot_tn(probs.astype(BF16), d_out)
            d_keys = dk if d_keys is None else d_keys + dk
            d_values = dv if d_values is None else d_values + dv
        turned.append(rotated(d_keys * scale, cosine, sine).astype(BF16))
        dqkv[:, :, lane_block(heads + g)] = turned[-1].reshape(n, -1, LANES)
        low_values = d_values.astype(BF16)
        dqkv[:, :, lane_block(heads + kv_heads + g)] = low_values.reshape(n, -1, LANES)
        small = dot_nt(jnp.concatenate(turned, axis=1), pick_split((group + 1) * HEAD))
        small_values = dot_nt(low_values, pick_plain(HEAD))
        dsmall[g] = (
            jnp.concatenate([small, small_values], axis=1).astype(BF16).reshape(dsmall.shape[1:])
        )

    pair.share_half(dsmall, dqkv_out)

    def partial(shard):
        return dot_nt(dqkv[shard], wqkv[...])

    sums_after(line, partial)
    total[...] = partial(me)
    tasks.advance()
    line.sum_take(total)
    d_resid, gain_part = norm_back(total[...], x[...].astype(F32), gain[...])
    dx_out[...] = (dh[...] + d_resid).astype(BF16)
    gain_out[...] = gain_part
    line.gather_end()
    line.sum_end()
    pair.wait()
    tasks.finish()


def ffn_fwd_kernel(layer, n, *refs):
    (h, gain, wg0, wg1, wu0, wu1, wd0, wd1) = refs[:8]
    (y_out, n_out, gate_out, up_out, hid_out) = refs[8:13]
    (wg, wu, wd, gate, up, hid, part, wsem) = refs[13:21]
    pair = Pair(*refs[21:24])
    line = Line(n, *refs[24:])
    me = line.me
    weights = Weights(layer, wsem)
    weights.want(wg0.at[0], wg1.at[0], wg)
    weights.want(wu0.at[0], wu1.at[0], wu)
    weights.want(wd0.at[0], wd1.at[0], wd)
    weights.start()
    resid = h[...]
    line.full[me] = (resid * rms_scale(resid) * gain[...]).astype(BF16)
    line.enter()
    line.gather_step(0)
    weights.wait()
    middle = hid.shape[3]

    def compute(shard):
        rows = line.full[shard]
        g = dot_nn(rows, wg[...])
        u = dot_nn(rows, wu[...])
        gate[shard] = g
        up[shard] = u
        low = (g * jax.nn.sigmoid(g) * u).astype(BF16)
        hid[0, shard] = low[:, :middle]
        hid[1, shard] = low[:, middle:]
        part[shard] = dot_nn(low, wd[...])

    rows_then_sums(line, compute, lambda shard: part[shard])
    pair.share(line.full, n_out)
    pair.share_half(hid, hid_out)
    pair.keep(gate, gate_out)
    pair.keep(up, up_out)
    part[me] += h[...]
    line.sum_take(part.at[me])
    y_out[...] = part[me].astype(BF16)
    line.gather_end()
    line.sum_end()
    pair.wait()


def ffn_bwd_kernel(layer, n, tasks, sizes, *refs):
    refs = bound(tasks, sizes, refs)
    (dy, h, gain, gate_in, up_in, wg0, wg1, wu0, wu1, wd0, wd1) = refs[:11]
    (dh_out, gain_out, df_out, dmid_out) = refs[11:15]
    (wg, wu, wd, gate, up, dmid, part, wsem, tsem) = refs[15:24]
    pair = Pair(*refs[24:27])
    line = Line(n, *refs[27:])
    me = line.me
    weights = Weights(layer, wsem)
    weights.want(wd0.at[0], wd1.at[0], wd)
    weights.want(wg0.at[0], wg1.at[0], wg)
    weights.want(wu0.at[0], wu1.at[0], wu)
    weights.start()
    takes = [
        pltpu.make_async_copy(gate_in, gate, tsem.at[0]),
        pltpu.make_async_copy(up_in, up, tsem.at[1]),
    ]
    for take in takes:
        take.start()
    line.full[me] = dy[...]
    line.enter(tasks.peers())
    line.gather_step(0)
    tasks.start()
    weights.wait()
    for take in takes:
        take.wait()
    middle = dmid.shape[3] // 2

    def compute(shard):
        d_hidden = dot_nt(line.full[shard], wd[...])
        g = gate[shard]
        sig = jax.nn.sigmoid(g)
        d_g = (d_hidden * up[shard] * sig * (1.0 + g * (1.0 - sig))).astype(BF16)
        d_u = (d_hidden * g * sig).astype(BF16)
        for core in range(2):
            lanes = slice(core * middle, (core + 1) * middle)
            dmid[core, shard, :, :middle] = d_g[:, lanes]
            dmid[core, shard, :, middle:] = d_u[:, lanes]
        part[shard] = dot_nt(d_g, wg[...]) + dot_nt(d_u, wu[...])

    rows_then_sums(line, compute, lambda shard: part[shard], tasks.advance)
    pair.share(line.full, df_out)
    pair.share_half(dmid, dmid_out)
    tasks.advance()
    line.sum_take(part.at[me])
    d_resid, gain_part = norm_back(part[me], h[...], gain[...])
    dh_out[...] = dy[...].astype(F32) + d_resid
    gain_out[...] = gain_part
    line.gather_end()
    line.sum_end()
    pair.wait()
    tasks.finish()


def run_kernel(body, args, in_specs, outs, scratch, cid, flops, nbytes, name, aliases=None):
    return pl.pallas_call(
        body,
        input_output_aliases=aliases or {},
        name=name,
        in_specs=in_specs,
        out_shape=[jax.ShapeDtypeStruct(shape, dtype) for shape, dtype, _ in outs],
        out_specs=[spec for _, _, spec in outs],
        scratch_shapes=scratch,
        cost_estimate=pl.CostEstimate(flops=flops, bytes_accessed=nbytes, transcendentals=0),
        compiler_params=pltpu.CompilerParams(
            collective_id=cid, has_side_effects=True, vmem_limit_bytes=44 << 20
        ),
    )(*args)


def attn_forward(layer, n, x, gain, tables, own, other):
    rows, width = x.shape
    heads = own[0].shape[2] // HEAD
    kv_heads = own[1].shape[2] // HEAD
    wide = (heads + 2 * kv_heads) * LANES
    small = heads // kv_heads * HEAD
    args = [x, gain, *tables, *own]
    specs = [VMEM_SPEC] * 6 + [HBM_SPEC] * len(own)
    outs = [
        ((rows, width), F32, VMEM_SPEC),
        ((2, n, rows, width), BF16, HBM_SPEC),
        ((n, rows, wide), BF16, HBM_SPEC),
        ((2, n, rows, small), BF16, HBM_SPEC),
    ]
    if other is None:
        outs += [(weight.shape, weight.dtype, HBM_SPEC) for weight in own]
    else:
        args += [*other]
        specs += [HBM_SPEC] * len(other)
    scratch = (
        [
            VMEM((width, heads * HEAD), BF16),
            VMEM((width, kv_heads * HEAD), BF16),
            VMEM((width, kv_heads * HEAD), BF16),
            VMEM((heads, LANES, width), BF16),
            VMEM((width, wide), BF16),
            VMEM((n, rows, wide), BF16),
            VMEM((n, rows, heads * LANES), BF16),
            VMEM((kv_heads, n, rows, small), BF16),
            DMA((3 + heads,)),
        ]
        + pair_scratch(3, 2 + (len(own) if other is None else 0))
        + line_scratch(n, rows, width)
    )
    body = functools.partial(attn_fwd_kernel, layer, n, heads, kv_heads, len(own))
    flops = 2 * n * rows * width * wide * 3 // 2
    return run_kernel(body, args, specs, outs, scratch, 1 + layer, flops, 8 << 20, f"attn_fwd{layer}")


def attn_backward(layer, n, dh, x, gain, tables, qkv, own, other, tasks):
    rows, width = x.shape
    heads = own[0].shape[2] // HEAD
    kv_heads = own[1].shape[2] // HEAD
    wide = (heads + 2 * kv_heads) * LANES
    small = (heads // kv_heads + 2) * HEAD
    args = [dh, x, gain, *tables, qkv, *own, *other]
    specs = [VMEM_SPEC] * 7 + [HBM_SPEC] * 9
    outs = [
        ((rows, width), BF16, VMEM_SPEC),
        ((1, width), F32, VMEM_SPEC),
        ((2, n, rows, width), BF16, HBM_SPEC),
        ((2, n, rows, small), BF16, HBM_SPEC),
    ]
    scratch = (
        [
            VMEM((width, heads * HEAD), BF16),
            VMEM((width, kv_heads * HEAD), BF16),
            VMEM((width, kv_heads * HEAD), BF16),
            VMEM((heads, LANES, width), BF16),
            VMEM((width, wide), BF16),
            VMEM((n, rows, wide), BF16),
            VMEM((n, rows, heads * LANES), BF16),
            VMEM((n, rows, wide), BF16),
            VMEM((kv_heads, n, rows, small), BF16),
            VMEM((rows, width), F32),
            DMA((3 + heads,)),
            DMA,
        ]
        + pair_scratch(2, 2)
        + line_scratch(n, rows, width)
    )
    body = functools.partial(attn_bwd_kernel, layer, n, heads, kv_heads)
    flops = 2 * n * rows * width * wide * 2
    return run_with_tasks(
        body, tasks, args, specs, outs, scratch, 3 + layer, flops, 8 << 20, f"attn_bwd{layer}"
    )


def ffn_forward(layer, n, h, gain, own, other):
    rows, width = h.shape
    hidden = own[0].shape[2]
    args = [h, gain]
    for mine, theirs in zip(own, other):
        args += [mine, theirs]
    specs = [VMEM_SPEC] * 2 + [HBM_SPEC] * 6
    outs = [
        ((rows, width), BF16, VMEM_SPEC),
        ((2, n, rows, width), BF16, HBM_SPEC),
        ((n, rows, hidden), F32, HBM_SPEC),
        ((n, rows, hidden), F32, HBM_SPEC),
        ((2, n, rows, hidden // 2), BF16, HBM_SPEC),
    ]
    scratch = (
        [
            VMEM((width, hidden), BF16),
            VMEM((width, hidden), BF16),
            VMEM((hidden, width), BF16),
            VMEM((n, rows, hidden), F32),
            VMEM((n, rows, hidden), F32),
            VMEM((2, n, rows, hidden // 2), BF16),
            VMEM((n, rows, width), F32),
            DMA((3,)),
        ]
        + pair_scratch(4, 2)
        + line_scratch(n, rows, width)
    )
    body = functools.partial(ffn_fwd_kernel, layer, n)
    flops = 6 * n * rows * width * hidden
    return run_kernel(body, args, specs, outs, scratch, 5 + layer, flops, 16 << 20, f"ffn_fwd{layer}")


def ffn_backward(layer, n, dy, h, gain, gate, up, own, other, tasks):
    rows, width = h.shape
    hidden = own[0].shape[2]
    args = [dy, h, gain, gate, up]
    for mine, theirs in zip(own, other):
        args += [mine, theirs]
    specs = [VMEM_SPEC] * 3 + [HBM_SPEC] * 8
    outs = [
        ((rows, width), F32, VMEM_SPEC),
        ((1, width), F32, VMEM_SPEC),
        ((2, n, rows, width), BF16, HBM_SPEC),
        ((2, n, rows, hidden), BF16, HBM_SPEC),
    ]
    scratch = (
        [
            VMEM((width, hidden), BF16),
            VMEM((width, hidden), BF16),
            VMEM((hidden, width), BF16),
            VMEM((n, rows, hidden), F32),
            VMEM((n, rows, hidden), F32),
            VMEM((2, n, rows, hidden), BF16),
            VMEM((n, rows, width), F32),
            DMA((3,)),
            DMA((2,)),
        ]
        + pair_scratch(2, 2)
        + line_scratch(n, rows, width)
    )
    body = functools.partial(ffn_bwd_kernel, layer, n)
    flops = 6 * n * rows * width * hidden
    return run_with_tasks(
        body, tasks, args, specs, outs, scratch, 7 + layer, flops, 16 << 20, f"ffn_bwd{layer}"
    )


def run_with_tasks(body, tasks, args, specs, outs, scratch, cid, flops, nbytes, name):
    more_args, more_outs, more_scratch = tasks.arguments(), tasks.outputs(), tasks.scratch()
    sizes = (
        (len(args), len(more_args)),
        (len(outs), len(more_outs)),
        (len(scratch), len(more_scratch)),
    )
    return run_kernel(
        functools.partial(body, tasks, sizes),
        args + more_args,
        specs + [HBM_SPEC] * len(more_args),
        outs + more_outs,
        scratch + more_scratch,
        cid,
        flops,
        nbytes,
        name,
    )


def tail_kernel(n, count, sizes, *refs):
    ffn_size, attn_size = sizes
    at = 0

    def take(number):
        nonlocal at
        at += number
        return list(refs[at - number : at])

    (gains,) = take(1)
    ffn_blocks, attn_arrays, _aliased = take(ffn_size), take(attn_size), take(ffn_size + attn_size)
    (gains_out,) = take(1)
    ffn_outs, attn_outs = take(ffn_size), take(attn_size)
    by_tensor, by_dp, by_core = take(3)
    small_sems = take(2)
    ffn_vmem, attn_vmem = take(ffn_size), take(attn_size)
    (load_sem,) = take(1)
    ffn_sems, attn_sems = take(3), take(3)
    reduce = Reduce(0, count, attn_arrays, attn_vmem, take(len(refs) - at))
    gather_ffn = Gather(0, count, ffn_vmem, ffn_outs, ffn_sems)
    gather_attn = Gather(0, count, attn_vmem, attn_outs, attn_sems)
    loads = [
        pltpu.make_async_copy(ffn_blocks[a], ffn_vmem[a], load_sem.at[a]) for a in range(ffn_size)
    ]
    for load in loads:
        load.start()
    axes = (("tensor", n, by_tensor), ("dp", count, by_dp), ("section", 2, by_core))
    barrier = pltpu.get_barrier_semaphore()
    peers = 0
    for axis, size, _ in axes:
        place = lax.axis_index(axis)
        for shift in range(1, size):
            pl.semaphore_signal(
                barrier, 1, device_id={axis: (place + shift) % size}, device_id_type=MESH
            )
            peers += 1
    pl.semaphore_wait(barrier, peers)

    def small(stage, shift):
        axis, size, slots = axes[stage]
        place = lax.axis_index(axis)
        ref = slots.at[place]
        return pltpu.make_async_remote_copy(
            ref,
            ref,
            small_sems[0].at[stage, shift],
            small_sems[1].at[stage, shift],
            device_id={axis: (place + shift) % size},
            device_id_type=MESH,
        )

    def small_start(stage, value):
        axis, size, slots = axes[stage]
        slots[lax.axis_index(axis)] = value
        for shift in range(1, size):
            small(stage, shift).start()

    def small_end(stage):
        _, size, slots = axes[stage]
        for shift in range(1, size):
            small(stage, shift).wait()
        value = slots[0]
        for index in range(1, size):
            value = value + slots[index]
        return value

    small_start(0, gains[...])
    reduce.start()
    for load in loads:
        load.wait()
    gather_ffn.start()
    small_start(1, small_end(0))
    reduce.advance()
    small_start(2, small_end(1))
    gather_ffn.advance()
    reduce.finish()
    gather_attn.start()
    gains_out[...] = small_end(2)
    gather_attn.advance()
    gather_ffn.finish()
    gather_attn.finish()


def tail(n, count, gains, ffn_blocks, attn_arrays, ffn_full, attn_full):
    sizes = (len(ffn_blocks), len(attn_arrays))
    args = [gains, *ffn_blocks, *attn_arrays, *ffn_full, *attn_full]
    specs = [VMEM_SPEC] + [HBM_SPEC] * (len(args) - 1)
    outs = [(gains.shape, F32, VMEM_SPEC)]
    outs += [(full.shape, BF16, HBM_SPEC) for full in (*ffn_full, *attn_full)]
    scratch = [VMEM((size,) + gains.shape, F32) for size in (n, count, 2)]
    scratch += [DMA((3, max(n, count, 2)))] * 2
    scratch += [VMEM(block.shape, BF16) for block in ffn_blocks]
    scratch += [VMEM((2, 2) + array.shape[-2:], BF16) for array in attn_arrays]
    scratch += [DMA((sizes[0],))]
    scratch += gather_sems(count, sizes[0]) + gather_sems(count, sizes[1])
    scratch += reduce_scratch(count, [array.shape for array in attn_arrays])
    first = 1 + sizes[0] + sizes[1]
    aliases = {first + index: 1 + index for index in range(sum(sizes))}
    body = functools.partial(tail_kernel, n, count, sizes)
    return run_kernel(body, args, specs, outs, scratch, 9, 1 << 20, 16 << 20, "tail", aliases)


def swap(values):
    return lax.ppermute(values, "section", [(0, 1), (1, 0)])


def segment_tables(lengths_row, n, rows):
    full_rows = n * rows
    slot_count = lengths_row.shape[0]
    seq_ends = jnp.cumsum(lengths_row)
    row_index = jnp.arange(full_rows, dtype=jnp.int32)
    segment = jnp.sum((row_index[:, None] >= seq_ends[None, :]).astype(jnp.int32), axis=1)
    starts = jnp.concatenate([seq_ends - lengths_row, seq_ends[-1:]])
    chosen = segment[:, None] == jnp.arange(slot_count + 1, dtype=jnp.int32)[None, :]
    position = row_index - jnp.sum(jnp.where(chosen, starts[None, :], 0), axis=1)
    segment = jnp.where(segment < slot_count, segment, slot_count + row_index)
    lane = jnp.arange(LANES, dtype=jnp.int32)
    inner = lane % (LANES // 2)
    inverse = rope_base ** (-inner.astype(F32) * 2.0 / HEAD)
    angle = position.astype(F32)[:, None] * inverse[None, :]
    live = (inner < HALF)[None, :]
    sign = jnp.where(lane < LANES // 2, -1.0, 1.0)[None, :]
    cosine = jnp.where(live, jnp.cos(angle), 0.0)
    sine = jnp.where(live, sign * jnp.sin(angle), 0.0)
    shape = (n, rows, LANES)
    return cosine.reshape(shape), sine.reshape(shape), segment[:, None], segment[None, :]


def shards(
    inputs,
    cotangent,
    seq_lengths,
    gain_attn,
    w_query,
    w_key,
    w_value,
    w_out,
    gain_ffn,
    w_gate,
    w_up,
    w_down,
):
    section = lax.axis_index("section")
    first = section == 0
    n = lax.axis_size("tensor")
    rows, width = inputs.shape[1:]

    def mine(stacked):
        return jnp.where(first, stacked[0], stacked[1])

    attn_own = (w_query, w_key, w_value, w_out)
    ffn_own = (w_gate, w_up, w_down)
    gains = jnp.concatenate([gain_attn, gain_ffn], axis=0)
    gains_other = swap(gains)
    gains_by_layer = [
        jnp.where(first, gains, gains_other).astype(F32),
        jnp.where(first, gains_other, gains).astype(F32),
    ]
    tables = segment_tables(mine(seq_lengths[0]), n, rows)

    x = mine(inputs)
    kept = []
    outs = []
    for layer in range(2):
        gain_a, gain_f = gains_by_layer[layer][0:1], gains_by_layer[layer][1:2]
        if layer == 0:
            h, n_all, qkv, o, *swapped = attn_forward(
                layer, n, x, gain_a, tables, attn_own + ffn_own, None
            )
            attn_other, ffn_other = tuple(swapped[:4]), tuple(swapped[4:])
        else:
            h, n_all, qkv, o = attn_forward(layer, n, x, gain_a, tables, attn_own, attn_other)
        y, n2_all, gate, up, hid = ffn_forward(layer, n, h, gain_f, ffn_own, ffn_other)
        kept.append((x, h, n_all, qkv, o, n2_all, gate, up, hid, gain_a, gain_f))
        outs.append(y)
        x = y

    count = lax.axis_size("dp")
    cube = (2,) + (2,) * (count.bit_length() - 1)

    def weight_grad(left, right):
        left = left.reshape(-1, left.shape[-1])
        right = right.reshape(-1, right.shape[-1])
        return dot_tn(left, right).astype(BF16)

    def blocked(array):
        return array.reshape(*cube, -1, array.shape[-1])

    dy = mine(cotangent)
    in_grads = [None, None]
    gain_parts = [None, None]
    sums = {}
    ffn_grad = attn_grad = None
    for layer in (1, 0):
        x, h, n_all, qkv, o, n2_all, gate, up, hid, gain_a, gain_f = kept[layer]
        plan = {}
        if layer == 0:
            plan = {"reduce": (1, attn_grad), "gather": (1, sums["ffn1"])}
        dh, gf_part, df_all, dmid, *more = ffn_backward(
            layer, n, dy, h, gain_f, gate, up, ffn_own, ffn_other, Tasks(count, plan)
        )
        if layer == 0:
            sums["attn1"], ffn_full = more[:2], more[2:]
        ffn_grad = [blocked(weight_grad(n2_all, dmid)), blocked(weight_grad(hid, df_all))]
        plan = {"reduce": (layer, ffn_grad)}
        if layer == 0:
            plan["gather"] = (1, sums["attn1"])
        dx, ga_part, da_all, dqkv, *more = attn_backward(
            layer, n, dh, x, gain_a, tables, qkv, attn_own, attn_other, Tasks(count, plan)
        )
        sums[f"ffn{layer}"] = more[:2]
        if layer == 0:
            attn_full = more[2:]
        attn_grad = [blocked(weight_grad(n_all, dqkv)), blocked(weight_grad(o, da_all))]
        gain_parts[layer] = jnp.concatenate([ga_part, gf_part], axis=0)
        in_grads[layer] = dx
        dy = dx
    gain_sums, g_mid, g_down, g_qkv, g_out = tail(
        n,
        count,
        jnp.concatenate(gain_parts, axis=0),
        sums["ffn0"],
        attn_grad,
        ffn_full,
        attn_full,
    )
    gain_own = jnp.where(first, gain_sums[0:2], gain_sums[2:4])
    g_mid, g_qkv = (array.reshape(2, -1, array.shape[-1]) for array in (g_mid, g_qkv))
    g_down, g_out = (array.reshape(-1, array.shape[-1]).astype(F32)[None] for array in (g_down, g_out))

    def columns(array, start, size):
        parts = [array[core, :, start : start + size].astype(F32) for core in range(2)]
        return jnp.concatenate(parts, axis=1)[None]

    mid = w_gate.shape[2] // 2
    g_gate, g_up = columns(g_mid, 0, mid), columns(g_mid, mid, mid)
    q_half, k_half = w_query.shape[2] // 2, w_key.shape[2] // 2
    g_query = columns(g_qkv, 0, q_half)
    g_key, g_value = (columns(g_qkv, q_half + at, k_half) for at in (0, k_half))

    def by_layer(values):
        keep = jnp.where(first, values[0], values[1])
        got = swap(jnp.where(first, values[1], values[0]))
        return jnp.stack([jnp.where(first, keep, got), jnp.where(first, got, keep)])[None]

    return (
        by_layer(outs),
        by_layer(in_grads),
        gain_own[0:1],
        g_query,
        g_key,
        g_value,
        g_out,
        gain_own[1:2],
        g_gate,
        g_up,
        g_down,
    )


def solution(mesh):
    placed = (
        P(None, ("dp", "tensor"), None),
        P(None, ("dp", "tensor"), None),
        P("dp", None, None),
        P("section", None),
        P("section", None, "tensor"),
        P("section", None, "tensor"),
        P("section", None, "tensor"),
        P("section", "tensor", None),
        P("section", None),
        P("section", None, "tensor"),
        P("section", None, "tensor"),
        P("section", "tensor", None),
    )
    return jax.shard_map(
        shards,
        mesh=mesh,
        in_specs=placed,
        out_specs=(
            P("section", None, ("dp", "tensor"), None),
            P("section", None, ("dp", "tensor"), None),
            P("section", None),
            P("section", None, "tensor"),
            P("section", None, "tensor"),
            P("section", None, "tensor"),
            P("section", "tensor", None),
            P("section", None),
            P("section", None, "tensor"),
            P("section", None, "tensor"),
            P("section", "tensor", None),
        ),
        check_vma=False,
    )
```

time: 1600 us -> 578 us (0.36)
  waiting for transfers between devices: 1200 us -> 0.01 us
  Pallas kernels: 0 us -> 484 us
  matrix products: 173 us -> 18.8 us
  blocking collectives: 77.1 us -> 0 us
  other arithmetic: 56.3 us -> 31.4 us
  local copies, waits for them, and re-layouts: 53.3 us -> 32.8 us
    reduce_scatter x12 -> x0, waiting for transfers between devices: 502 us -> none  [the longest x6 269 us: spread_grads(): lax.psum_scatter(term(jnp.int32(0), share_rows * lax.axis_size('tensor'))...]
    pallas_call x0 -> x9, Pallas kernels: none -> 484 us  [run_kernel(): pl.pallas_call(body, input_output_aliases=aliases or {}, name=name, in_sp...]
    psum x1 -> x0, waiting for transfers between devices: 382 us -> none  [shards(): lax.psum((grad_query, grad_key, grad_value, grad_out, grad_gate, grad_up,...]
    all_gather x12 -> x0, waiting for transfers between devices: 312 us -> none  [the longest x6 166 us: collect_rows(): return lax.all_gather(values, 'tensor', axis=0, tiled=True)]
    dot_general x81 -> x8, matrix products: 173 us -> 18.8 us  [dot_tn(): lax.dot_general(left, right, (((0,), (0,)), ((), ())), preferred_element_...]
    psum x1 -> x0, blocking collectives: 77.1 us -> none  [shards(): lax.psum((grad_gain_attn, grad_gain_ffn), ('dp', 'tensor'))]
    unnamed x422 -> x148, local copies, waits for them, and re-layouts: 50.7 us -> 29.4 us
    reduce_sum x21 -> x2, other arithmetic: 17 us -> 0.17 us  [the longest x1 0.09 us: segment_tables(): jnp.sum(jnp.where(chosen, starts[None, :], 0), axis=1)]
  transfers between devices with their start and end apart: 29 -> 3, of which waited for: 27 -> 0; matrix products, arithmetic and copies ran while one was open for 7% -> 6% of each run, Pallas kernels for 0% -> 0%
where the time goes in v2:
time: 578 us; the launch traced here: 570 us
  Pallas kernels  484 us (84%)
  local copies, waits for them, and re-layouts  32.8 us (6%)
  other arithmetic  31.4 us (5%)
  matrix products  18.8 us (3%)
    pallas_call x9, Pallas kernels, run_kernel(): pl.pallas_call(body, input_output_aliases=aliases or {}, name=name, in_sp...  484 us
    unnamed x148, local copies, waits for them, and re-layouts  29.4 us
    dot_general x8, matrix products, dot_tn(): lax.dot_general(left, right, (((0,), (0,)), ((), ())), preferred_element_...  18.8 us
  transfers between devices with their start and end apart: 3, of which 0 were waited for; matrix products, arithmetic and copies ran while one was open for 6% of the time, Pallas kernels for 0%

profile of v2, /device:TPU:0, one launch (start us, length us, event | category | flops | bytes accessed | tf_op | source)
XLA Modules:
  0.0 570.2 jit_solution(15810459511598788998)
XLA Ops:
  0.7 0.8 pad_maximum_fusion.1
  2.0 0.8 fusion.16
  3.6 0.8 bitcast_subtract_fusion
  4.4 0.8 compare_select_fusion.refs_4_.refs_5_
  5.2 0.7 pad_add_fusion
  6.2 1.9 select_bitcast_fusion.5.refs_0_.refs_1_
  8.1 1.8 select_bitcast_fusion.2.refs_0_
  9.9 1.5 fusion.13
  12.1 0.9 copy-done.6
  13.0 0.9 copy-done.8
  13.9 0.9 copy-done.10
  14.8 1.0 copy-done.19
  15.8 51.0 %attn_fwd0.1 = (f32[96,1536]{1,0:T(8,128)S(1)}, bf16[2,4,96,1536]{3,2,1,0:T(8,128)(2,1)}, bf16[4,96,1024]{2,1,0:T(8,128)(2,1)S(1)}, bf16[2,4,96,192]{3,2,1,0:T(8...) custom-call(bf16[96,1536]{1,0:T(8,128)(2,1)S(1)} %copy-done.19, ...), custom_call_target="tpu_custom_call" | custom-call | flops 1811939328 | bytes 8388608 | tf_op jit(solution)/shard_map/attn_fwd0/pallas_call | solution.py:965
  66.8 1.0 copy-done.5
  67.8 0.9 copy-done.39
  68.7 0.8 copy-done.47
  69.5 42.4 %ffn_fwd0.1 = (bf16[96,1536]{1,0:T(8,128)(2,1)S(1)}, bf16[2,4,96,1536]{3,2,1,0:T(8,128)(2,1)S(1)}, f32[4,96,1024]{2,1,0:T(8,128)S(1)}, f32[4,96,1024]{2,1,0:T(8,128)S(1)}, bf16[2,4,96,512]{3,2,1,0:T(8,128)(2,1)S(1)}) custom-call(f32[96,1536]{1,0:T(8,128)S(1)} %get-tuple-element.67.refs_0_.refs_1_, f32[1,1536]{1,0:T(1,128)S(1)} %get-tuple-element.148.refs_1_.refs_2_, ...), custom_call_target="tpu_custom_call" | custom-call | flops 3623878656 | bytes 16777216 | tf_op jit(solution)/shard_map/ffn_fwd0/pallas_call | solution.py:965
  111.9 1.1 copy-done.25
  113.0 1.1 copy-done.27
  114.1 0.9 copy-done.43
  115.0 48.1 %attn_fwd1.1 = (f32[96,1536]{1,0:T(8,128)S(1)}, bf16[2,4,96,1536]{3,2,1,0:T(8,128)(2,1)}, bf16[4,96,1024]{2,1,0:T(8,128)(2,1)S(1)}, bf16[2,4,96,192]{3,2,1,0:T(8,128)(2,1)S(1)}) custom-call(bf16[96,1536]{1,0:T(8,128)(2,1)S(1)} %get-tuple-element.71.refs_0_.refs_1_, f32[1,1536]{1,0:T(1,128)S(1)} %get-tuple-element.140.refs_1_.refs_2_, ...), custom_call_target="tpu_custom_call" | custom-call | flops 1811939328 | bytes 8388608 | tf_op jit(solution)/shard_map/attn_fwd1/pallas_call | solution.py:965
  163.2 0.9 copy-done.41
  164.1 0.8 copy-done.49
  164.9 40.5 %ffn_fwd1.1 = (bf16[96,1536]{1,0:T(8,128)(2,1)S(1)}, bf16[2,4,96,1536]{3,2,1,0:T(8,128)(2,1)S(1)}, f32[4,96,1024]{2,1,0:T(8,128)S(1)}, f32[4,96,1024]{2,1,0:T(8,128)S(1)}, bf16[2,4,96,512]{3,2,1,0:T(8,128)(2,1)S(1)}) custom-call(f32[96,1536]{1,0:T(8,128)S(1)} %get-tuple-element.76.refs_0_.refs_1_, f32[1,1536]{1,0:T(1,128)S(1)} %get-tuple-element.139.refs_1_.refs_2_, ...), custom_call_target="tpu_custom_call" | custom-call | flops 3623878656 | bytes 16777216 | tf_op jit(solution)/shard_map/ffn_fwd1/pallas_call | solution.py:965
  205.4 1.1 copy-done.30
  206.5 1.1 copy-done.32
  207.7 1.4 copy-done.53
  209.1 1.5 copy-done.24
  210.5 1.4 copy-done.31
  211.9 1.4 copy-done.33
  213.4 46.0 %ffn_bwd1.1 = (f32[96,1536]{1,0:T(8,128)S(1)}, f32[1,1536]{1,0:T(1,128)S(1)}, bf16[2,4,96,1536]{3,2,1,0:T(8,128)(2,1)S(1)}, bf16[2,4,96,1024]{3,2,1,0:T(8,128)(2,1)S(1)}) custom-call(bf16[96,1536]{1,0:T(8,128)(2,1)S(1)} %copy-done.38, f32[96,1536]{1,0:T(8,128)S(1)} %copy-done.24, f32[1,1536]{1,0:T(1,128)S(1)} %get-tuple-element.139.refs_1_.refs_2_, ...), custom_call_target="tpu_custom_call" | custom-call | flops 3623878656 | bytes 16777216 | tf_op jit(solution)/shard_map/ffn_bwd1/pallas_call | solution.py:965
  259.4 1.1 copy-done.55
  260.5 5.5 bitcast_convert_fusion.1
  266.0 2.6 fusion.2
  268.6 61.1 %attn_bwd1.1 = (bf16[96,1536]{1,0:T(8,128)(2,1)S(1)}, f32[1,1536]{1,0:T(1,128)S(1)}, bf16[2,4,96,1536]{3,2,1,0:T(8,128)(2,1)}, bf16[2,4,96,384]{3,2,1,0:T(8,128)...) custom-call(f32[96,1536]{1,0:T(8,128)S(1)} %get-tuple-element.80.refs_0_, ...), custom_call_target="tpu_custom_call" | custom-call | flops 2415919104 | bytes 8388608 | tf_op jit(solution)/shard_map/attn_bwd1/pallas_call | solution.py:965
  329.7 1.4 fusion.4
  331.6 0.7 fusion.6
  333.0 45.1 %ffn_bwd0.1 = (f32[96,1536]{1,0:T(8,128)S(1)}, f32[1,1536]{1,0:T(1,128)S(1)}, bf16[2,4,96,1536]{3,2,1,0:T(8,128)(2,1)}, bf16[2,4,96,1024]{3,2,1,0:T(8,128)(2,1)S...) custom-call(bf16[96,1536]{1,0:T(8,128)(2,1)S(1)} %get-tuple-element., ...), custom_call_target="tpu_custom_call" | custom-call | flops 3623878656 | bytes 16777216 | tf_op jit(solution)/shard_map/ffn_bwd0/pallas_call | solution.py:965
  378.1 4.0 bitcast_convert_fusion
  382.2 2.6 fusion.3
  384.8 77.2 %attn_bwd0.1 = (bf16[96,1536]{1,0:T(8,128)(2,1)S(1)}, f32[1,1536]{1,0:T(1,128)S(1)}, bf16[2,4,96,1536]{3,2,1,0:T(8,128)(2,1)}, bf16[2,4,96,384]{3,2,1,0:T(8,128)...) custom-call(f32[96,1536]{1,0:T(8,128)S(1)} %get-tuple-element.95.ref, ...), custom_call_target="tpu_custom_call" | custom-call | flops 2415919104 | bytes 8388608 | tf_op jit(solution)/shard_map/attn_bwd0/pallas_call | solution.py:965
  462.0 1.4 fusion.5
  463.9 0.7 fusion.7
  464.6 0.8 copy-done.3
  465.3 73.0 %tail.1 = (f32[4,1536]{1,0:T(4,128)S(1)}, bf16[2,2,2,2,192,1024]{5,4,3,2,1,0:T(8,128)(2,1)}, bf16[2,2,2,2,64,1536]{5,4,3,2,1,0:T(8,128)(2,1)}, bf16[2,2,2,2,192,...) custom-call(f32[4,1536]{1,0:T(4,128)S(1)} %pad_maximum_fusion.refs_0, ...), custom_call_target="tpu_custom_call", output_to_operand_aliasing={{1}: (5, {}), {2}: (6, {}), {3}: (7, {}), {4}: (8, {})} | custom-call | flops 1048576 | bytes 16777216 | tf_op jit(solution)/shard_map/tail/pallas_call | solution.py:965
  538.3 1.4 fusion.17
  539.8 0.8 broadcast_select_fusion.2
  540.6 0.6 fusion.18
  541.2 0.8 broadcast_select_fusion
  542.5 1.9 copy.85
  544.4 1.9 copy.84
  546.2 0.9 copy.83
  547.3 1.7 convert.25
  549.0 1.0 copy-done.56
  550.0 3.6 convert.28
  554.6 1.1 fusion.10
  555.7 1.1 fusion.9
  556.9 3.6 fusion.1
  560.5 3.6 fusion
  564.0 1.8 fusion.8
  565.8 1.0 select_bitcast_fusion.4
  566.9 0.9 maximum_bitcast_fusion.3
  567.8 1.0 select_bitcast_fusion.1
  568.8 0.9 maximum_bitcast_fusion.4
  (146 shorter events, 5.7 us)
Async XLA Ops:
  0.6 10.8 %copy-start.63 = (bf16[1,1536,192]{1,2,0:T(8,128)(2,1)S(1)}, bf16[1,1536,192]{1,2,0:T(8,128)(2,1)}, u32[]{:S(2)}) copy-start(bf16[1,1536,192]{1,2,0:T(8,128)(2,1)} %param.17) | copy-start | bytes 1769476
  0.7 11.0 %copy-start.64 = (bf16[1,1536,192]{1,2,0:T(8,128)(2,1)S(1)}, bf16[1,1536,192]{1,2,0:T(8,128)(2,1)}, u32[]{:S(2)}) copy-start(bf16[1,1536,192]{1,2,0:T(8,128)(2,1)} %param.18) | copy-start | bytes 1769476
  1.5 10.5 %collective-permute-start = (bf16[2,1536]{1,0:T(2,128)(2,1)S(1)}, bf16[2,1536]{1,0:T(2,128)(2,1)S(1)}, u32[]{:S(2)}, u32[]{:S(2)}) collective-permute-start(bf16[2,1536]{1,0:T(2,128)(2,1)S(1)} %pad_maximum_fusion.1), channel_id=1, source_target_pairs={{0,16},{16,0},{1,17},{17,1},{2,18},{18,2},{3,19},{19,3},{4,20},{20... | collective-permute-start | bytes 18440 | tf_op jit(solution)/shard_map/ppermute | solution.py:1249
  6.1 5.8 %copy-start.65 = (bf16[1,1536]{1,0:T(2,128)(2,1)S(1)}, bf16[1,1536]{1,0:T(2,128)(2,1)}, u32[]{:S(2)}) copy-start(bf16[1,1536]{1,0:T(2,128)(2,1)} %param.20) | copy-start | bytes 9220
  6.1 5.9 %copy-start.66 = (bf16[1,1536]{1,0:T(2,128)(2,1)S(1)}, bf16[1,1536]{1,0:T(2,128)(2,1)}, u32[]{:S(2)}) copy-start(bf16[1,1536]{1,0:T(2,128)(2,1)} %param.15) | copy-start | bytes 9220
  6.1 5.9 %copy-start.1 = (bf16[1,1536,384]{2,1,0:T(8,128)(2,1)S(1)}, bf16[1,1536,384]{2,1,0:T(8,128)(2,1)}, u32[]{:S(2)}) copy-start(bf16[1,1536,384]{2,1,0:T(8,128)(2,1)} %refs_8_.5) | copy-start | bytes 3538948
  15.8 53.6 %copy-start = (bf16[1,1536,1024]{2,1,0:T(8,128)(2,1)S(1)}, bf16[1,1536,1024]{2,1,0:T(8,128)(2,1)}, u32[]{:S(2)}) copy-start(bf16[1,1536,1024]{2,1,0:T(8,128)(2,1)} %refs_5_.3) | copy-start | bytes 9437188
  66.8 1.0 copy-start.5
  69.4 42.4 %copy-start.21 = (f32[96,1536]{1,0:T(8,128)}, f32[96,1536]{1,0:T(8,128)S(1)}, u32[]{:S(2)}) copy-start(f32[96,1536]{1,0:T(8,128)S(1)} %get-tuple-element.67.refs_0_.refs_1_) | copy-start | bytes 1769476
  69.4 45.6 %copy-start.4 = (bf16[1,1536,384]{2,1,0:T(8,128)(2,1)}, bf16[1,1536,384]{2,1,0:T(8,128)(2,1)S(1)}, u32[]{:S(2)}) copy-start(bf16[1,1536,384]{2,1,0:T(8,128)(2,1)S(1)} %get-tuple-element.72.refs_10_.refs_12_) | copy-start | bytes 3538948
  69.4 45.6 %copy-start.2 = (bf16[1,384,1536]{2,1,0:T(8,128)(2,1)S(1)}, bf16[1,384,1536]{2,1,0:T(8,128)(2,1)}, u32[]{:S(2)}) copy-start(bf16[1,384,1536]{2,1,0:T(8,128)(2,1)} %refs_11_.5) | copy-start | bytes 3538948
  69.5 45.6 %copy-start.9 = (f32[4,96,128]{2,1,0:T(8,128)S(1)}, f32[4,96,128]{2,1,0:T(8,128)}, u32[]{:S(2)}) copy-start(f32[4,96,128]{2,1,0:T(8,128)} %get-tuple-element.145.refs_3_.refs_4_) | copy-start | bytes 589828
  111.9 1.1 copy-start.25
  113.0 1.1 copy-start.27
  115.0 48.2 %copy-start.14 = (bf16[96,1536]{1,0:T(8,128)(2,1)}, bf16[96,1536]{1,0:T(8,128)(2,1)S(1)}, u32[]{:S(2)}) copy-start(bf16[96,1536]{1,0:T(8,128)(2,1)S(1)} %get-tuple-element.71.refs_0_.refs_1_) | copy-start | bytes 884740
  115.0 48.2 %copy-start.51 = (bf16[2,4,96,1536]{3,2,1,0:T(8,128)(2,1)}, bf16[2,4,96,1536]{3,2,1,0:T(8,128)(2,1)S(1)}, u32[]{:S(2)}) copy-start(bf16[2,4,96,1536]{3,2,1,0:T(8,128)(2,1)S(1)} %get-tuple-element.97) | copy-start | bytes 7077892
  164.9 40.5 %copy-start.23 = (f32[96,1536]{1,0:T(8,128)}, f32[96,1536]{1,0:T(8,128)S(1)}, u32[]{:S(2)}) copy-start(f32[96,1536]{1,0:T(8,128)S(1)} %get-tuple-element.76.refs_0_.refs_1_) | copy-start | bytes 1769476
  164.9 44.2 %copy-start.38 = (bf16[96,1536]{1,0:T(8,128)(2,1)S(1)}, bf16[96,1536]{1,0:T(8,128)(2,1)}, u32[]{:S(2)}) copy-start(bf16[96,1536]{1,0:T(8,128)(2,1)} %select_bitcast_fusion.2.refs_0_) | copy-start | bytes 884740
  205.4 1.1 copy-start.30
  206.5 1.1 copy-start.32
  207.7 1.4 copy-start.53
  209.1 50.3 %copy-start.45 = (bf16[2,4,96,512]{3,2,1,0:T(8,128)(2,1)}, bf16[2,4,96,512]{3,2,1,0:T(8,128)(2,1)S(1)}, u32[]{:S(2)}) copy-start(bf16[2,4,96,512]{3,2,1,0:T(8,128)(2,1)S(1)} %get-tuple-element.84) | copy-start | bytes 2359300
  209.1 330.7 %copy-start.34 = (bf16[96,1536]{1,0:T(8,128)(2,1)}, bf16[96,1536]{1,0:T(8,128)(2,1)S(1)}, u32[]{:S(2)}) copy-start(bf16[96,1536]{1,0:T(8,128)(2,1)S(1)} %get-tuple-element.77) | copy-start | bytes 884740
  209.1 1.5 copy-start.24
  210.5 1.4 copy-start.31
  211.9 1.4 copy-start.33
  213.4 47.2 %copy-start.54 = (bf16[2,4,96,1536]{3,2,1,0:T(8,128)(2,1)S(1)}, bf16[2,4,96,1536]{3,2,1,0:T(8,128)(2,1)}, u32[]{:S(2)}) copy-start(bf16[2,4,96,1536]{3,2,1,0:T(8,128)(2,1)} %copy-done.53) | copy-start | bytes 7077892
  259.4 1.1 copy-start.55
  260.5 5.5 copy-start.46
  266.0 2.6 copy-start.7
  266.0 2.6 copy-start.11
  266.0 2.6 copy-start.15
  266.0 2.6 copy-start.42
  268.6 61.1 %copy-start.68 = (bf16[2,4,96,1536]{3,2,1,0:T(8,128)(2,1)S(1)}, bf16[2,4,96,1536]{3,2,1,0:T(8,128)(2,1)}, u32[]{:S(2)}) copy-start(bf16[2,4,96,1536]{3,2,1,0:T(8,128)(2,1)} %get-tuple-element.89) | copy-start | bytes 7077892
  329.7 211.5 %copy-start.17 = (bf16[96,1536]{1,0:T(8,128)(2,1)}, bf16[96,1536]{1,0:T(8,128)(2,1)S(1)}, u32[]{:S(2)}) copy-start(bf16[96,1536]{1,0:T(8,128)(2,1)S(1)} %get-tuple-element.86.refs_0_) | copy-start | bytes 884740
  329.7 1.5 copy-start.50
  329.7 1.9 copy-start.59
  329.7 2.5 copy-start.28
  331.2 1.3 copy-start.22
  331.2 1.8 copy-start.26
  333.0 45.1 %copy-start.52 = (bf16[2,4,96,1536]{3,2,1,0:T(8,128)(2,1)S(1)}, bf16[2,4,96,1536]{3,2,1,0:T(8,128)(2,1)}, u32[]{:S(2)}) copy-start(bf16[2,4,96,1536]{3,2,1,0:T(8,128)(2,1)} %copy-done.51) | copy-start | bytes 7077892
  378.1 4.1 copy-start.44
  378.1 4.1 copy-start.58
  382.2 2.6 copy-start.20
  382.2 2.6 copy-start.40
  384.8 77.2 %copy-start.67 = (bf16[2,4,96,1536]{3,2,1,0:T(8,128)(2,1)S(1)}, bf16[2,4,96,1536]{3,2,1,0:T(8,128)(2,1)}, u32[]{:S(2)}) copy-start(bf16[2,4,96,1536]{3,2,1,0:T(8,128)(2,1)} %get-tuple-element.110) | copy-start | bytes 7077892
  462.0 79.2 %copy-start.36 = (bf16[96,1536]{1,0:T(8,128)(2,1)}, bf16[96,1536]{1,0:T(8,128)(2,1)S(1)}, u32[]{:S(2)}) copy-start(bf16[96,1536]{1,0:T(8,128)(2,1)S(1)} %get-tuple-element.103) | copy-start | bytes 884740
  462.0 1.5 copy-start.48
  462.0 1.9 copy-start.57
  462.0 2.6 copy-start.29
  463.4 1.9 copy-start.3
  538.3 1.5 copy-start.12
  539.8 7.5 %copy-start.13 = (bf16[2,2,2,2,24,1536]{5,4,3,2,1,0:T(8,128)(2,1)S(1)}, bf16[2,2,2,2,24,1536]{5,4,3,2,1,0:T(8,128)(2,1)}, u32[]{:S(2)}) copy-start(bf16[2,2,2,2,24,1536]{5,4,3,2,1,0:T(8,128)(2,1)} %copy-done.12) | copy-start | bytes 3538948
  540.6 25.3 %collective-permute-start.1 = (bf16[96,1536]{1,0:T(8,128)(2,1)}, bf16[96,1536]{1,0:T(8,128)(2,1)}, u32[]{:S(2)}, u32[]{:S(2)}) collective-permute-start(bf16[96,1536]{1,0:T(8,128)(2,1)} %broadcast_select_fusion.2), channel_id=1, source_target_pairs={{0,16},{16,0},{1,17},{17,1},{2,18},{18,2},{3,19},{19,3},{4,20},{20... | collective-permute-start | bytes 884744 | tf_op jit(solution)/shard_map/ppermute | solution.py:1249
  542.0 25.8 %collective-permute-start.2 = (bf16[96,1536]{1,0:T(8,128)(2,1)}, bf16[96,1536]{1,0:T(8,128)(2,1)}, u32[]{:S(2)}, u32[]{:S(2)}) collective-permute-start(bf16[96,1536]{1,0:T(8,128)(2,1)} %broadcast_select_fusion), channel_id=1, source_target_pairs={{0,16},{16,0},{1,17},{17,1},{2,18},{18,2},{3,19},{19,3},{4,20},{20... | collective-permute-start | bytes 884744 | tf_op jit(solution)/shard_map/ppermute | solution.py:1249
  547.3 2.7 copy-start.56
  547.3 6.3 %slice-start = ((s8[6291456]{0:T(1024)(128)(4,1)}), s8[4194304]{0:T(1024)(128)(4,1)S(1)}, s32[]{:S(2)}) async-start(s8[6291456]{0:T(1024)(128)(4,1)} %bitcast.145), calls=%async_computation | async-start | bytes 8388608
  550.0 3.6 slice-start.1
  553.6 2.1 copy-start.60
  553.6 2.1 copy-start.62
  564.0 1.8 copy-start.16
  564.0 1.8 copy-start.35
  564.0 3.7 copy-start.18
  564.0 3.7 copy-start.37
  (10 other events, 8.9 us)

commit v3 on v2

--- a/solution.py
+++ b/solution.py
@@ -10,12 +10,13 @@
 HEAD = 96
 HALF = HEAD // 2
 LANES = 128
-CHUNKS = 2
+CHUNKS = 3
 BF16 = jnp.bfloat16
 F32 = jnp.float32
 MESH = pl.DeviceIdType.MESH
 VMEM = pltpu.VMEM
 VMEM_SPEC = pl.BlockSpec(memory_space=pltpu.VMEM)
+LOAD, LOAD_MINE = "load", "load mine"
 HBM_SPEC = pl.BlockSpec(memory_space=pltpu.HBM)
 DMA = pltpu.SemaphoreType.DMA
 
@@ -198,6 +199,10 @@
         def _():
             line.gather_step(step)
 
+        @pl.when(step == n - 1)
+        def _():
+            halfway()
+
         @pl.when(step < n)
         def _():
             @pl.loop(0, 2)
@@ -211,10 +216,6 @@
         line.sum_step(0, step - me, partial)
         line.sum_step(1, 2 * (n - 1) - step - me, partial)
 
-        @pl.when(step == n - 1)
-        def _():
-            halfway()
-
 
 def later_shards(line, compute):
     me, n = line.me, line.n
@@ -234,13 +235,37 @@
                 compute(shard)
 
 
-def sums_after(line, partial):
+def sums_after(line, partial, each=lambda step: None):
     me, n = line.me, line.n
 
     @pl.loop(0, n - 1)
     def _(step):
         line.sum_step(0, me + n - 1 - step, partial)
         line.sum_step(1, step - (n - 1 - me), partial)
+        each(step)
+
+
+def sums_alone(line, compute, partial, halfway):
+    me, n = line.me, line.n
+
+    @pl.loop(0, n)
+    def _(step):
+        @pl.loop(0, 2)
+        def _(side):
+            shard = jnp.where(side == 0, me + n - 1 - step, step - (n - 1 - me))
+            first = jnp.where(side == 0, me, 0)
+            last = jnp.where(side == 0, n, me)
+
+            @pl.when((shard >= first) & (shard < last))
+            def _():
+                compute(shard)
+
+        line.sum_step(0, me + n - 1 - step, partial)
+        line.sum_step(1, step - (n - 1 - me), partial)
+
+        @pl.when(step == n - 2)
+        def _():
+            halfway()
 
 
 class Weights:
@@ -279,18 +304,19 @@
         self.core = lax.axis_index("section")
         self.sems = local_sems, send_sems, recv_sems
         self.kept, self.sent = [], []
+        self.streams = []
 
     def keep(self, source, target):
-        copy = pltpu.make_async_copy(source, target, self.sems[0].at[len(self.kept)])
+        copy = pltpu.make_async_copy(source, target, self.sems[0].at[len(self.kept), 0])
         copy.start()
         self.kept.append(copy)
 
-    def copy(self, source, target, index):
+    def copy(self, source, target, index, part=0):
         return pltpu.make_async_remote_copy(
             source,
             target,
-            self.sems[1].at[index],
-            self.sems[2].at[index],
+            self.sems[1].at[index, part],
+            self.sems[2].at[index, part],
             device_id={"section": 1 - self.core},
             device_id_type=MESH,
         )
@@ -300,23 +326,52 @@
         copy.start()
         self.sent.append(copy)
 
-    def share(self, source, pair):
-        self.keep(source, pair.at[0])
-        self.send(source, pair.at[1])
-
     def share_half(self, halves, pair):
         self.keep(halves.at[self.core], pair.at[0])
         self.send(halves.at[1 - self.core], pair.at[1])
 
-    def wait(self):
-        for copy in self.kept:
-            copy.wait()
-        for copy in self.sent:
-            copy.wait()
-
-
-def pair_scratch(kept, sent):
-    return [DMA((max(kept, 1),)), DMA((max(sent, 1),)), DMA((max(sent, 1),))]
+    def stream_keep(self, source, target):
+        self.streams.append((source, target, len(self.kept), None))
+        self.kept.append(None)
+
+    def stream_share(self, source, pair):
+        self.stream_keep(source, pair.at[0])
+        self.streams.append((source, pair.at[1], None, len(self.sent)))
+        self.sent.append(None)
+
+    def stream_share_half(self, halves, pair):
+        self.stream_keep(halves.at[self.core], pair.at[0])
+        self.streams.append((halves.at[1 - self.core], pair.at[1], None, len(self.sent)))
+        self.sent.append(None)
+
+    def streamed(self, shard):
+        copies = []
+        for source, target, kept, sent in self.streams:
+            pieces = source.at[shard], target.at[shard]
+            if sent is None:
+                copies.append(pltpu.make_async_copy(*pieces, self.sems[0].at[kept, shard]))
+            else:
+                copies.append(self.copy(*pieces, sent, shard))
+        return copies
+
+    def stream(self, shard):
+        for copy in self.streamed(shard):
+            copy.start()
+
+    def wait(self, count=0):
+        for copy in self.kept + self.sent:
+            if copy is not None:
+                copy.wait()
+        if self.streams:
+
+            @pl.loop(0, count)
+            def _(shard):
+                for copy in self.streamed(shard):
+                    copy.wait()
+
+
+def pair_scratch(count, kept, sent):
+    return [DMA((max(kept, 1), count)), DMA((max(sent, 1), count)), DMA((max(sent, 1), count))]
 
 
 class Cube:
@@ -346,7 +401,7 @@
         size = len(sources)
         self.accs = scratch[:size]
         self.recvs = [scratch[size * (t + 1) : size * (t + 2)] for t in range(self.bits)]
-        self.local, self.ss, self.sr, self.fs, self.fr = scratch[size * (self.bits + 1) :]
+        self.local, self.ss, self.sr, self.fs = scratch[size * (self.bits + 1) :]
         self.t = 0
         self.place = [
             {b: slice(None) for b in self.down if b != self.order(c)[0]} for c in range(2)
@@ -404,117 +459,122 @@
                 self.place[c][b] = self.bit[b]
         self.t = t + 1
 
-    def hand_over(self, a, c):
-        return pltpu.make_async_remote_copy(
-            self.accs[a].at[self.spot(c)],
-            self.outs[a].at[self.core, c],
-            self.fs.at[a, c],
-            self.fr.at[a, c],
-            device_id={"section": 1 - self.core},
-            device_id_type=MESH,
-        )
-
     def put_away(self, a, c):
         return pltpu.make_async_copy(
-            self.accs[a].at[self.spot(c)], self.outs[a].at[self.core, c], self.fs.at[a, c]
+            self.accs[a].at[self.spot(c)], self.outs[a].at[c], self.fs.at[a, c]
         )
 
     def finish(self):
         while self.t < self.bits:
             self.advance()
-
-        @pl.when(self.active)
-        def _():
-            for a, c in self.items():
-                self.put_away(a, c).start()
-
-        @pl.when(jnp.logical_not(self.active))
-        def _():
-            for a, c in self.items():
-                self.hand_over(a, c).start()
-
+        for a, c in self.items():
+            self.put_away(a, c).start()
         for a, c in self.items():
             for t in range(self.bits):
                 self.copy(a, c, t, self.recvs[t][a].at[c]).wait_send()
-
-        @pl.when(self.active)
-        def _():
-            for a, c in self.items():
-                self.put_away(a, c).wait()
-                self.hand_over(a, c).wait_recv()
-
-        @pl.when(jnp.logical_not(self.active))
-        def _():
-            for a, c in self.items():
-                self.hand_over(a, c).wait_send()
+        for a, c in self.items():
+            self.put_away(a, c).wait()
 
 
 class Gather(Cube):
     def __init__(self, layer, count, blocks, outs, sems):
         super().__init__(layer, count)
         self.blocks, self.outs = blocks, outs
-        self.keep, self.ss, self.sr = sems
+        self.keep, self.ss, self.sr, self.hs, self.hr = sems
         self.t = 0
+        off_layer = 1 - self.core if layer == 1 else self.core
+        self.slot = self.core * (1 - off_layer) + 2 * off_layer
 
     def items(self):
-        return [(a, h, c) for a in range(len(self.blocks)) for h in range(2) for c in range(2)]
+        return [(a, c) for a in range(len(self.blocks)) for c in range(2)]
 
     def order(self, colour):
         return super().order(colour)[::-1]
 
-    def region(self, a, h, c, t):
-        free = self.order(c)[:t]
-        index = (slice(None) if b in free else self.bit[b] for b in self.down)
-        return self.outs[a].at[(h, c, *index)]
-
-    def copy(self, a, h, c, t):
-        target = self.region(a, h, c, t)
+    def region(self, a, c, t, half, flipped=None):
+        order = self.order(c)
+        index = []
+        for b in self.down:
+            if b in order[:t]:
+                index.append(slice(None))
+            else:
+                index.append(1 - self.bit[b] if flipped == order.index(b) else self.bit[b])
+        return self.outs[a].at[(half, c, *index)]
+
+    def copy(self, a, c, t):
+        target = self.region(a, c, t, self.slot)
         return pltpu.make_async_remote_copy(
-            self.blocks[a].at[h, c] if t == 0 else target,
+            self.blocks[a].at[c] if t == 0 else target,
             target,
-            self.ss.at[a, h, c, t],
-            self.sr.at[a, h, c, t],
+            self.ss.at[a, c, t],
+            self.sr.at[a, c, t],
             device_id=self.peer(self.order(c)[t]),
             device_id_type=MESH,
         )
 
-    def kept(self, a, h, c):
+    def kept(self, a, c):
         return pltpu.make_async_copy(
-            self.blocks[a].at[h, c], self.region(a, h, c, 0), self.keep.at[a, h, c]
+            self.blocks[a].at[c], self.region(a, c, 0, self.slot), self.keep.at[a, c]
         )
 
+    def hand_over(self, a, c, t):
+        if t == 0:
+            source, target = self.blocks[a].at[c], self.region(a, c, 0, self.core)
+        else:
+            source = self.region(a, c, t - 1, self.slot, t - 1)
+            target = self.region(a, c, t - 1, self.core, t - 1)
+        return pltpu.make_async_remote_copy(
+            source,
+            target,
+            self.hs.at[a, c, t],
+            self.hr.at[a, c, t],
+            device_id={"section": 1 - self.core},
+            device_id_type=MESH,
+        )
+
+    def pass_on(self, t):
+        @pl.when(jnp.logical_not(self.active))
+        def _():
+            for a, c in self.items():
+                self.hand_over(a, c, t).start()
+
     def start(self):
-        @pl.when(self.active)
-        def _():
-            for a, h, c in self.items():
-                self.copy(a, h, c, 0).start()
-                self.kept(a, h, c).start()
+        for a, c in self.items():
+            self.copy(a, c, 0).start()
+            self.kept(a, c).start()
+        self.pass_on(0)
 
     def advance(self):
         t = self.t
         if t >= self.bits:
             return
-
-        @pl.when(self.active)
-        def _():
-            for a, h, c in self.items():
-                if t == 0:
-                    self.kept(a, h, c).wait()
-                self.copy(a, h, c, t).wait_recv()
-                if t + 1 < self.bits:
-                    self.copy(a, h, c, t + 1).start()
-
+        for a, c in self.items():
+            if t == 0:
+                self.kept(a, c).wait()
+            self.copy(a, c, t).wait_recv()
+            if t + 1 < self.bits:
+                self.copy(a, c, t + 1).start()
+        self.pass_on(t + 1)
         self.t = t + 1
 
     def finish(self):
         while self.t < self.bits:
             self.advance()
+        for a, c in self.items():
+            for t in range(self.bits):
+                self.copy(a, c, t).wait_send()
 
         @pl.when(self.active)
         def _():
-            for a, h, c in self.items():
-                for t in range(self.bits):
-                    self.copy(a, h, c, t).wait_send()
+            for a, c in self.items():
+                for t in range(self.bits + 1):
+                    self.hand_over(a, c, t).wait_recv()
+
+        @pl.when(jnp.logical_not(self.active))
+        def _():
+            for a, c in self.items():
+                for t in range(self.bits + 1):
+                    self.hand_over(a, c, t).wait_send()
 
 
 def reduce_scratch(count, arrays):
@@ -528,13 +588,18 @@
         DMA((size, 2, bits)),
         DMA((size, 2, bits)),
         DMA((size, 2)),
-        DMA((size, 2)),
     ]
 
 
 def gather_sems(count, size):
     bits = count.bit_length() - 1
-    return [DMA((size, 2, 2)), DMA((size, 2, 2, bits)), DMA((size, 2, 2, bits))]
+    return [
+        DMA((size, 2)),
+        DMA((size, 2, bits)),
+        DMA((size, 2, bits)),
+        DMA((size, 2, bits + 1)),
+        DMA((size, 2, bits + 1)),
+    ]
 
 
 class Tasks:
@@ -550,11 +615,11 @@
     def outputs(self):
         outs = []
         if self.reduce:
-            outs += [((2, 2) + ref.shape[-2:], BF16, HBM_SPEC) for ref in self.reduce[1]]
+            outs += [((2,) + ref.shape[-2:], BF16, HBM_SPEC) for ref in self.reduce[1]]
         if self.gather:
             middle = (2,) * (self.count.bit_length() - 1)
             outs += [
-                ((2, 2) + middle + ref.shape[-2:], BF16, HBM_SPEC) for ref in self.gather[1]
+                ((3, 2) + middle + ref.shape[-2:], BF16, HBM_SPEC) for ref in self.gather[1]
             ]
         return outs
 
@@ -586,7 +651,7 @@
                 pltpu.make_async_copy(args[a], blocks[a], scratch[size].at[a]) for a in range(size)
             ]
             self.running.append(
-                Gather(self.gather[0], count, blocks, outs, scratch[size + 1 : size + 4])
+                Gather(self.gather[0], count, blocks, outs, scratch[size + 1 : size + 6])
             )
         for load in self.loads:
             load.start()
@@ -675,30 +740,46 @@
     return exp_scores / jnp.sum(exp_scores, axis=-1, keepdims=True)
 
 
-def attn_fwd_kernel(layer, n, heads, kv_heads, others, *refs):
+def attn_fwd_kernel(layer, n, heads, kv_heads, others, loads_done, *refs):
+    ahead = layer == 1
     x, gain, cos, sin, seg_col, seg_row = refs[:6]
-    own = refs[6 : 6 + others]
-    at = 6 + others
+    at = 6
+    if ahead:
+        rows_ahead = refs[at]
+        at += 1
+    own = refs[at : at + others]
+    at += others
     if layer == 0:
-        h_out, n_out, qkv_out, o_out = refs[at : at + 4]
-        other = refs[at + 4 : at + 4 + others]
+        h_out, h_save, n_out, qkv_out, o_out = refs[at : at + 5]
+        other = refs[at + 5 : at + 5 + others]
     else:
         other = refs[at : at + others]
-        h_out, n_out, qkv_out, o_out = refs[at + others : at + others + 4]
-    at += 4 + others
+        h_out, h_save, n_out, qkv_out, o_out, ahead_out = refs[at + others : at + others + 6]
+        at += 1
+    at += 5 + others
     (wq, wk, wv, wo, wqkv, qkv, o, osmall, wsem) = refs[at : at + 9]
     pair = Pair(*refs[at + 9 : at + 12])
-    line = Line(n, *refs[at + 12 :])
+    at += 12
+    if ahead:
+        second = Line(n, refs[at], None, None, *refs[at + 1 : at + 3], None, None)
+        at += 3
+    line = Line(n, *refs[at:])
     me = line.me
     group = heads // kv_heads
     weights = Weights(layer, wsem)
     sources = [ref for both in zip(own[:4], other[:4]) for ref in both] + [wq, wk, wv]
     attn_weights(weights, wo, sources)
+    if layer == 0:
+        weights.start_own()
+    else:
+        weights.start()
+    loads_done()
     resid = x[...].astype(F32)
     line.full[me] = (resid * rms_scale(resid) * gain[...]).astype(BF16)
     clear_pads(wo)
+    if ahead:
+        second.full[me] = rows_ahead[...]
     if layer == 0:
-        weights.start_own()
         line.enter()
         line.gather_step(0)
         for mine, theirs in zip(own, other):
@@ -710,7 +791,6 @@
 
         weights.start_other(arrived)
     else:
-        weights.start()
         line.enter()
         line.gather_step(0)
     weights.wait()
@@ -723,10 +803,13 @@
             qkv[shard, :, lanes] = rotated(products[:, lanes], cos[shard], sin[shard]).astype(BF16)
         lanes = slice((heads + kv_heads) * LANES, None)
         qkv[shard, :, lanes] = products[:, lanes].astype(BF16)
-
+        pair.stream(shard)
+
+    pair.stream_share(line.full, n_out)
+    pair.stream_keep(qkv, qkv_out)
     later_shards(line, compute)
-    pair.share(line.full, n_out)
-    pair.keep(qkv, qkv_out)
+    if ahead:
+        second.gather_step(0)
     allowed = allowed_pairs(seg_col, seg_row)
 
     @pl.loop(0, kv_heads)
@@ -749,9 +832,17 @@
     def partial(shard):
         return dot_nn(o[shard], wo[...].reshape(wide, -1))
 
-    sums_after(line, partial)
+    if ahead:
+        sums_after(line, partial, lambda step: second.gather_step(step + 1))
+        pair.keep(second.full, ahead_out.at[0])
+        pair.send(second.full, ahead_out.at[1])
+    else:
+        sums_after(line, partial)
     h_out[...] = resid + partial(me)
     line.sum_take(h_out)
+    pair.keep(h_out, h_save)
+    if ahead:
+        second.gather_end()
     line.gather_end()
     line.sum_end()
     if layer == 0:
@@ -765,8 +856,8 @@
             for index in range(4):
                 pair.copy(own[index], other[index], index).wait_recv()
 
-        pair.sent = pair.sent[others:]
-    pair.wait()
+        pair.sent[:others] = [None] * others
+    pair.wait(n)
 
 
 def bound(tasks, sizes, refs):
@@ -778,14 +869,14 @@
     return [ref for own, _ in groups for ref in own]
 
 
-def attn_bwd_kernel(layer, n, heads, kv_heads, tasks, sizes, *refs):
+def attn_bwd_kernel(layer, n, heads, kv_heads, tasks, sizes, loads_done, *refs):
     refs = bound(tasks, sizes, refs)
     (dh, x, gain, cos, sin, seg_col, seg_row, qkv_in) = refs[:8]
     own, other = refs[8:12], refs[12:16]
-    (dx_out, gain_out, da_out, dqkv_out) = refs[16:20]
-    (wq, wk, wv, wo, wqkv, qkv, d_o, dqkv, dsmall, total, wsem, tsem) = refs[20:32]
-    pair = Pair(*refs[32:35])
-    line = Line(n, *refs[35:])
+    (dx_out, dx_save, gain_out, da_out, dqkv_out) = refs[16:21]
+    (wq, wk, wv, wo, wqkv, qkv, d_o, dqkv, dsmall, total, wsem, tsem) = refs[21:33]
+    pair = Pair(*refs[33:36])
+    line = Line(n, *refs[36:])
     me = line.me
     group = heads // kv_heads
     weights = Weights(layer, wsem)
@@ -799,6 +890,7 @@
     line.enter(tasks.peers())
     line.gather_step(0)
     tasks.start()
+    loads_done()
     weights.wait()
     spread_qkv(wq, wk, wv, wqkv)
     take.wait()
@@ -806,10 +898,10 @@
 
     def compute(shard):
         d_o[shard] = dot_nt(line.full[shard], wo[...].reshape(wide, -1)).astype(BF16)
-
+        pair.stream(shard)
+
+    pair.stream_share(line.full, da_out)
     later_shards(line, compute)
-    pair.share(line.full, da_out)
-    tasks.advance()
     allowed = allowed_pairs(seg_col, seg_row)
     cosine = cos[...].reshape(-1, LANES)
     sine = -sin[...].reshape(-1, LANES)
@@ -851,31 +943,32 @@
     def partial(shard):
         return dot_nt(dqkv[shard], wqkv[...])
 
-    sums_after(line, partial)
+    sums_after(line, partial, lambda step: pl.when(step == 0)(tasks.advance))
     total[...] = partial(me)
-    tasks.advance()
     line.sum_take(total)
     d_resid, gain_part = norm_back(total[...], x[...].astype(F32), gain[...])
     dx_out[...] = (dh[...] + d_resid).astype(BF16)
     gain_out[...] = gain_part
+    pair.keep(dx_out, dx_save)
     line.gather_end()
     line.sum_end()
-    pair.wait()
+    pair.wait(n)
     tasks.finish()
 
 
-def ffn_fwd_kernel(layer, n, *refs):
+def ffn_fwd_kernel(layer, n, loads_done, *refs):
     (h, gain, wg0, wg1, wu0, wu1, wd0, wd1) = refs[:8]
-    (y_out, n_out, gate_out, up_out, hid_out) = refs[8:13]
-    (wg, wu, wd, gate, up, hid, part, wsem) = refs[13:21]
-    pair = Pair(*refs[21:24])
-    line = Line(n, *refs[24:])
+    (y_out, y_save, n_out, gate_out, up_out, hid_out) = refs[8:14]
+    (wg, wu, wd, gate, up, hid, part, wsem) = refs[14:22]
+    pair = Pair(*refs[22:25])
+    line = Line(n, *refs[25:])
     me = line.me
     weights = Weights(layer, wsem)
     weights.want(wg0.at[0], wg1.at[0], wg)
     weights.want(wu0.at[0], wu1.at[0], wu)
     weights.want(wd0.at[0], wd1.at[0], wd)
     weights.start()
+    loads_done()
     resid = h[...]
     line.full[me] = (resid * rms_scale(resid) * gain[...]).astype(BF16)
     line.enter()
@@ -892,25 +985,31 @@
         low = (g * jax.nn.sigmoid(g) * u).astype(BF16)
         hid[0, shard] = low[:, :middle]
         hid[1, shard] = low[:, middle:]
+        pair.stream(shard)
         part[shard] = dot_nn(low, wd[...])
 
+    pair.stream_share(line.full, n_out)
+    pair.stream_share_half(hid, hid_out)
+    pair.stream_keep(gate, gate_out)
+    pair.stream_keep(up, up_out)
     rows_then_sums(line, compute, lambda shard: part[shard])
-    pair.share(line.full, n_out)
-    pair.share_half(hid, hid_out)
-    pair.keep(gate, gate_out)
-    pair.keep(up, up_out)
     part[me] += h[...]
     line.sum_take(part.at[me])
     y_out[...] = part[me].astype(BF16)
+    pair.keep(y_out, y_save)
     line.gather_end()
     line.sum_end()
-    pair.wait()
-
-
-def ffn_bwd_kernel(layer, n, tasks, sizes, *refs):
+    pair.wait(n)
+
+
+def ffn_bwd_kernel(layer, n, tasks, sizes, loads_done, *refs):
     refs = bound(tasks, sizes, refs)
+    gathered = layer == 1
     (dy, h, gain, gate_in, up_in, wg0, wg1, wu0, wu1, wd0, wd1) = refs[:11]
-    (dh_out, gain_out, df_out, dmid_out) = refs[11:15]
+    if gathered:
+        (df_all, dh_out, gain_out, dmid_out) = refs[11:15]
+    else:
+        (dh_out, gain_out, df_all, dmid_out) = refs[11:15]
     (wg, wu, wd, gate, up, dmid, part, wsem, tsem) = refs[15:24]
     pair = Pair(*refs[24:27])
     line = Line(n, *refs[27:])
@@ -924,11 +1023,17 @@
         pltpu.make_async_copy(gate_in, gate, tsem.at[0]),
         pltpu.make_async_copy(up_in, up, tsem.at[1]),
     ]
+    if gathered:
+        takes.append(pltpu.make_async_copy(df_all.at[0], line.full, tsem.at[2]))
     for take in takes:
         take.start()
-    line.full[me] = dy[...]
-    line.enter(tasks.peers())
-    line.gather_step(0)
+    loads_done()
+    if gathered:
+        line.enter(tasks.peers())
+    else:
+        line.full[me] = dy[...]
+        line.enter(tasks.peers())
+        line.gather_step(0)
     tasks.start()
     weights.wait()
     for take in takes:
@@ -945,31 +1050,61 @@
             lanes = slice(core * middle, (core + 1) * middle)
             dmid[core, shard, :, :middle] = d_g[:, lanes]
             dmid[core, shard, :, middle:] = d_u[:, lanes]
+        pair.stream(shard)
         part[shard] = dot_nt(d_g, wg[...]) + dot_nt(d_u, wu[...])
 
-    rows_then_sums(line, compute, lambda shard: part[shard], tasks.advance)
-    pair.share(line.full, df_out)
-    pair.share_half(dmid, dmid_out)
-    tasks.advance()
+    pair.stream_share_half(dmid, dmid_out)
+    if gathered:
+        sums_alone(line, compute, lambda shard: part[shard], tasks.advance)
+    else:
+        pair.stream_share(line.full, df_all)
+        rows_then_sums(line, compute, lambda shard: part[shard], tasks.advance)
     line.sum_take(part.at[me])
     d_resid, gain_part = norm_back(part[me], h[...], gain[...])
     dh_out[...] = dy[...].astype(F32) + d_resid
     gain_out[...] = gain_part
-    line.gather_end()
+    if not gathered:
+        line.gather_end()
     line.sum_end()
-    pair.wait()
+    pair.wait(n)
     tasks.finish()
 
 
 def run_kernel(body, args, in_specs, outs, scratch, cid, flops, nbytes, name, aliases=None):
+    loaded = [index for index, spec in enumerate(in_specs) if spec in (LOAD, LOAD_MINE)]
+    buffers = [
+        VMEM(args[index].shape[1:] if in_specs[index] == LOAD_MINE else args[index].shape, args[index].dtype)
+        for index in loaded
+    ]
+    inputs, results, own = len(args), len(outs), len(scratch)
+
+    def kernel(*refs):
+        places = list(refs[: inputs + results + own])
+        extra = refs[inputs + results + own :]
+        copies = []
+        for number, index in enumerate(loaded):
+            source = refs[index]
+            if in_specs[index] == LOAD_MINE:
+                source = source.at[lax.axis_index("section")]
+            copies.append(pltpu.make_async_copy(source, extra[number], extra[-1].at[number]))
+            places[index] = extra[number]
+        for copy in copies:
+            copy.start()
+
+        def loads_done():
+            for copy in copies:
+                copy.wait()
+
+        body(loads_done, *places)
+
     return pl.pallas_call(
-        body,
-        input_output_aliases=aliases or {},
+        kernel,
         name=name,
-        in_specs=in_specs,
+        in_specs=[HBM_SPEC if spec in (LOAD, LOAD_MINE) else spec for spec in in_specs],
         out_shape=[jax.ShapeDtypeStruct(shape, dtype) for shape, dtype, _ in outs],
         out_specs=[spec for _, _, spec in outs],
-        scratch_shapes=scratch,
+        scratch_shapes=[*scratch, *buffers, DMA((max(len(loaded), 1),))],
+        input_output_aliases=aliases or {},
         cost_estimate=pl.CostEstimate(flops=flops, bytes_accessed=nbytes, transcendentals=0),
         compiler_params=pltpu.CompilerParams(
             collective_id=cid, has_side_effects=True, vmem_limit_bytes=44 << 20
@@ -977,16 +1112,22 @@
     )(*args)
 
 
-def attn_forward(layer, n, x, gain, tables, own, other):
-    rows, width = x.shape
+def attn_forward(layer, n, x, gain, tables, own, other, rows_ahead):
+    rows, width = x.shape[-2:]
     heads = own[0].shape[2] // HEAD
     kv_heads = own[1].shape[2] // HEAD
     wide = (heads + 2 * kv_heads) * LANES
     small = heads // kv_heads * HEAD
-    args = [x, gain, *tables, *own]
-    specs = [VMEM_SPEC] * 6 + [HBM_SPEC] * len(own)
+    args = [x, gain, *tables]
+    specs = [LOAD_MINE if x.ndim == 3 else VMEM_SPEC] + [LOAD] * 5
+    if layer == 1:
+        args.append(rows_ahead)
+        specs.append(LOAD_MINE)
+    args += own
+    specs += [HBM_SPEC] * len(own)
     outs = [
         ((rows, width), F32, VMEM_SPEC),
+        ((rows, width), F32, HBM_SPEC),
         ((2, n, rows, width), BF16, HBM_SPEC),
         ((n, rows, wide), BF16, HBM_SPEC),
         ((2, n, rows, small), BF16, HBM_SPEC),
@@ -996,6 +1137,7 @@
     else:
         args += [*other]
         specs += [HBM_SPEC] * len(other)
+        outs.append(((2, n, rows, width), BF16, HBM_SPEC))
     scratch = (
         [
             VMEM((width, heads * HEAD), BF16),
@@ -1008,7 +1150,8 @@
             VMEM((kv_heads, n, rows, small), BF16),
             DMA((3 + heads,)),
         ]
-        + pair_scratch(3, 2 + (len(own) if other is None else 0))
+        + pair_scratch(n, 5, 3 + (len(own) if other is None else 0))
+        + ([VMEM((n, rows, width), BF16)] + [DMA((2, n, CHUNKS))] * 2 if layer == 1 else [])
         + line_scratch(n, rows, width)
     )
     body = functools.partial(attn_fwd_kernel, layer, n, heads, kv_heads, len(own))
@@ -1017,15 +1160,16 @@
 
 
 def attn_backward(layer, n, dh, x, gain, tables, qkv, own, other, tasks):
-    rows, width = x.shape
+    rows, width = dh.shape
     heads = own[0].shape[2] // HEAD
     kv_heads = own[1].shape[2] // HEAD
     wide = (heads + 2 * kv_heads) * LANES
     small = (heads // kv_heads + 2) * HEAD
     args = [dh, x, gain, *tables, qkv, *own, *other]
-    specs = [VMEM_SPEC] * 7 + [HBM_SPEC] * 9
+    specs = [VMEM_SPEC, LOAD_MINE if x.ndim == 3 else LOAD] + [LOAD] * 5 + [HBM_SPEC] * 9
     outs = [
         ((rows, width), BF16, VMEM_SPEC),
+        ((rows, width), BF16, HBM_SPEC),
         ((1, width), F32, VMEM_SPEC),
         ((2, n, rows, width), BF16, HBM_SPEC),
         ((2, n, rows, small), BF16, HBM_SPEC),
@@ -1045,7 +1189,7 @@
             DMA((3 + heads,)),
             DMA,
         ]
-        + pair_scratch(2, 2)
+        + pair_scratch(n, 3, 2)
         + line_scratch(n, rows, width)
     )
     body = functools.partial(attn_bwd_kernel, layer, n, heads, kv_heads)
@@ -1061,9 +1205,10 @@
     args = [h, gain]
     for mine, theirs in zip(own, other):
         args += [mine, theirs]
-    specs = [VMEM_SPEC] * 2 + [HBM_SPEC] * 6
+    specs = [VMEM_SPEC, LOAD] + [HBM_SPEC] * 6
     outs = [
         ((rows, width), BF16, VMEM_SPEC),
+        ((rows, width), BF16, HBM_SPEC),
         ((2, n, rows, width), BF16, HBM_SPEC),
         ((n, rows, hidden), F32, HBM_SPEC),
         ((n, rows, hidden), F32, HBM_SPEC),
@@ -1080,7 +1225,7 @@
             VMEM((n, rows, width), F32),
             DMA((3,)),
         ]
-        + pair_scratch(4, 2)
+        + pair_scratch(n, 5, 2)
         + line_scratch(n, rows, width)
     )
     body = functools.partial(ffn_fwd_kernel, layer, n)
@@ -1088,19 +1233,23 @@
     return run_kernel(body, args, specs, outs, scratch, 5 + layer, flops, 16 << 20, f"ffn_fwd{layer}")
 
 
-def ffn_backward(layer, n, dy, h, gain, gate, up, own, other, tasks):
+def ffn_backward(layer, n, dy, h, gain, gate, up, own, other, tasks, df_all):
     rows, width = h.shape
     hidden = own[0].shape[2]
     args = [dy, h, gain, gate, up]
     for mine, theirs in zip(own, other):
         args += [mine, theirs]
-    specs = [VMEM_SPEC] * 3 + [HBM_SPEC] * 8
+    specs = [LOAD_MINE if dy.ndim == 3 else VMEM_SPEC, LOAD, LOAD] + [HBM_SPEC] * 8
     outs = [
         ((rows, width), F32, VMEM_SPEC),
         ((1, width), F32, VMEM_SPEC),
-        ((2, n, rows, width), BF16, HBM_SPEC),
         ((2, n, rows, hidden), BF16, HBM_SPEC),
     ]
+    if layer == 1:
+        args.append(df_all)
+        specs.append(HBM_SPEC)
+    else:
+        outs.insert(2, ((2, n, rows, width), BF16, HBM_SPEC))
     scratch = (
         [
             VMEM((width, hidden), BF16),
@@ -1111,9 +1260,9 @@
             VMEM((2, n, rows, hidden), BF16),
             VMEM((n, rows, width), F32),
             DMA((3,)),
-            DMA((2,)),
+            DMA((3,)),
         ]
-        + pair_scratch(2, 2)
+        + pair_scratch(n, 2, 2)
         + line_scratch(n, rows, width)
     )
     body = functools.partial(ffn_bwd_kernel, layer, n)
@@ -1143,7 +1292,7 @@
     )
 
 
-def tail_kernel(n, count, sizes, *refs):
+def tail_kernel(n, count, sizes, loads_done, *refs):
     ffn_size, attn_size = sizes
     at = 0
 
@@ -1152,15 +1301,16 @@
         at += number
         return list(refs[at - number : at])
 
-    (gains,) = take(1)
+    gains = take(4)
+    rows = take(4)
     ffn_blocks, attn_arrays, _aliased = take(ffn_size), take(attn_size), take(ffn_size + attn_size)
-    (gains_out,) = take(1)
+    (gains_out, section_out, in_grad) = take(3)
     ffn_outs, attn_outs = take(ffn_size), take(attn_size)
     by_tensor, by_dp, by_core = take(3)
     small_sems = take(2)
     ffn_vmem, attn_vmem = take(ffn_size), take(attn_size)
     (load_sem,) = take(1)
-    ffn_sems, attn_sems = take(3), take(3)
+    ffn_sems, attn_sems, row_sems = take(5), take(5), take(3)
     reduce = Reduce(0, count, attn_arrays, attn_vmem, take(len(refs) - at))
     gather_ffn = Gather(0, count, ffn_vmem, ffn_outs, ffn_sems)
     gather_attn = Gather(0, count, attn_vmem, attn_outs, attn_sems)
@@ -1209,11 +1359,40 @@
             value = value + slots[index]
         return value
 
-    small_start(0, gains[...])
-    reduce.start()
+    loads_done()
+    small_start(0, jnp.concatenate([gain[...] for gain in gains], axis=0))
     for load in loads:
         load.wait()
     gather_ffn.start()
+    reduce.start()
+    core = lax.axis_index("section")
+
+    def row_target(index):
+        return (section_out, in_grad)[index // 2].at[core]
+
+    def row_keep(index):
+        return pltpu.make_async_copy(rows[index], row_target(index), row_sems[0].at[index])
+
+    def row_send(index):
+        return pltpu.make_async_remote_copy(
+            rows[index],
+            row_target(index),
+            row_sems[1].at[index],
+            row_sems[2].at[index],
+            device_id={"section": 1 - core},
+            device_id_type=MESH,
+        )
+
+    for index in range(4):
+
+        @pl.when(core == index % 2)
+        def _():
+            row_keep(index).start()
+
+        @pl.when(core != index % 2)
+        def _():
+            row_send(index).start()
+
     small_start(1, small_end(0))
     reduce.advance()
     small_start(2, small_end(1))
@@ -1224,23 +1403,35 @@
     gather_attn.advance()
     gather_ffn.finish()
     gather_attn.finish()
-
-
-def tail(n, count, gains, ffn_blocks, attn_arrays, ffn_full, attn_full):
+    for index in range(4):
+
+        @pl.when(core == index % 2)
+        def _():
+            row_keep(index).wait()
+            row_send(index).wait_recv()
+
+        @pl.when(core != index % 2)
+        def _():
+            row_send(index).wait_send()
+
+
+def tail(n, count, gains, rows, ffn_blocks, attn_arrays, ffn_full, attn_full):
     sizes = (len(ffn_blocks), len(attn_arrays))
-    args = [gains, *ffn_blocks, *attn_arrays, *ffn_full, *attn_full]
-    specs = [VMEM_SPEC] + [HBM_SPEC] * (len(args) - 1)
-    outs = [(gains.shape, F32, VMEM_SPEC)]
+    args = [*gains, *rows, *ffn_blocks, *attn_arrays, *ffn_full, *attn_full]
+    specs = [LOAD] * 8 + [HBM_SPEC] * (len(args) - 8)
+    together = (4, gains[0].shape[1])
+    outs = [(together, F32, VMEM_SPEC)]
+    outs += [((2,) + rows[0].shape, BF16, HBM_SPEC)] * 2
     outs += [(full.shape, BF16, HBM_SPEC) for full in (*ffn_full, *attn_full)]
-    scratch = [VMEM((size,) + gains.shape, F32) for size in (n, count, 2)]
+    scratch = [VMEM((size,) + together, F32) for size in (n, count, 2)]
     scratch += [DMA((3, max(n, count, 2)))] * 2
     scratch += [VMEM(block.shape, BF16) for block in ffn_blocks]
-    scratch += [VMEM((2, 2) + array.shape[-2:], BF16) for array in attn_arrays]
+    scratch += [VMEM((2,) + array.shape[-2:], BF16) for array in attn_arrays]
     scratch += [DMA((sizes[0],))]
-    scratch += gather_sems(count, sizes[0]) + gather_sems(count, sizes[1])
+    scratch += gather_sems(count, sizes[0]) + gather_sems(count, sizes[1]) + [DMA((4,))] * 3
     scratch += reduce_scratch(count, [array.shape for array in attn_arrays])
-    first = 1 + sizes[0] + sizes[1]
-    aliases = {first + index: 1 + index for index in range(sum(sizes))}
+    first = 8 + sizes[0] + sizes[1]
+    aliases = {first + index: 3 + index for index in range(sum(sizes))}
     body = functools.partial(tail_kernel, n, count, sizes)
     return run_kernel(body, args, specs, outs, scratch, 9, 1 << 20, 16 << 20, "tail", aliases)
 
@@ -1288,11 +1479,7 @@
     section = lax.axis_index("section")
     first = section == 0
     n = lax.axis_size("tensor")
-    rows, width = inputs.shape[1:]
-
-    def mine(stacked):
-        return jnp.where(first, stacked[0], stacked[1])
-
+    rows = inputs.shape[1]
     attn_own = (w_query, w_key, w_value, w_out)
     ffn_own = (w_gate, w_up, w_down)
     gains = jnp.concatenate([gain_attn, gain_ffn], axis=0)
@@ -1301,24 +1488,26 @@
         jnp.where(first, gains, gains_other).astype(F32),
         jnp.where(first, gains_other, gains).astype(F32),
     ]
-    tables = segment_tables(mine(seq_lengths[0]), n, rows)
-
-    x = mine(inputs)
+    tables = segment_tables(jnp.where(first, seq_lengths[0, 0], seq_lengths[0, 1]), n, rows)
+
+    x = x_saved = inputs
     kept = []
     outs = []
     for layer in range(2):
         gain_a, gain_f = gains_by_layer[layer][0:1], gains_by_layer[layer][1:2]
         if layer == 0:
-            h, n_all, qkv, o, *swapped = attn_forward(
-                layer, n, x, gain_a, tables, attn_own + ffn_own, None
+            h, h_saved, n_all, qkv, o, *swapped = attn_forward(
+                layer, n, x, gain_a, tables, attn_own + ffn_own, None, None
             )
             attn_other, ffn_other = tuple(swapped[:4]), tuple(swapped[4:])
         else:
-            h, n_all, qkv, o = attn_forward(layer, n, x, gain_a, tables, attn_own, attn_other)
-        y, n2_all, gate, up, hid = ffn_forward(layer, n, h, gain_f, ffn_own, ffn_other)
-        kept.append((x, h, n_all, qkv, o, n2_all, gate, up, hid, gain_a, gain_f))
-        outs.append(y)
-        x = y
+            h, h_saved, n_all, qkv, o, df_ahead = attn_forward(
+                layer, n, x, gain_a, tables, attn_own, attn_other, cotangent
+            )
+        y, y_saved, n2_all, gate, up, hid = ffn_forward(layer, n, h, gain_f, ffn_own, ffn_other)
+        kept.append((x_saved, h_saved, n_all, qkv, o, n2_all, gate, up, hid, gain_a, gain_f))
+        outs.append(y_saved)
+        x, x_saved = y, y_saved
 
     count = lax.axis_size("dp")
     cube = (2,) + (2,) * (count.bit_length() - 1)
@@ -1331,66 +1520,69 @@
     def blocked(array):
         return array.reshape(*cube, -1, array.shape[-1])
 
-    dy = mine(cotangent)
+    dy = cotangent
     in_grads = [None, None]
     gain_parts = [None, None]
-    sums = {}
-    ffn_grad = attn_grad = None
     for layer in (1, 0):
         x, h, n_all, qkv, o, n2_all, gate, up, hid, gain_a, gain_f = kept[layer]
-        plan = {}
-        if layer == 0:
-            plan = {"reduce": (1, attn_grad), "gather": (1, sums["ffn1"])}
-        dh, gf_part, df_all, dmid, *more = ffn_backward(
-            layer, n, dy, h, gain_f, gate, up, ffn_own, ffn_other, Tasks(count, plan)
-        )
-        if layer == 0:
-            sums["attn1"], ffn_full = more[:2], more[2:]
-        ffn_grad = [blocked(weight_grad(n2_all, dmid)), blocked(weight_grad(hid, df_all))]
-        plan = {"reduce": (layer, ffn_grad)}
-        if layer == 0:
-            plan["gather"] = (1, sums["attn1"])
-        dx, ga_part, da_all, dqkv, *more = attn_backward(
+        if layer == 1:
+            g_down = blocked(weight_grad(hid, df_ahead))
+            plan = {"reduce": (1, [g_down])}
+            dh, gf_part, dmid, sum_down = ffn_backward(
+                layer, n, dy, h, gain_f, gate, up, ffn_own, ffn_other, Tasks(count, plan), df_ahead
+            )
+            g_mid = blocked(weight_grad(n2_all, dmid))
+            plan = {"reduce": (1, [g_mid]), "gather": (1, [sum_down])}
+        else:
+            plan = {"reduce": (1, attn_grad), "gather": (1, [sum_mid])}
+            dh, gf_part, df_all, dmid, *sum_attn, mid_full = ffn_backward(
+                layer, n, dy, h, gain_f, gate, up, ffn_own, ffn_other, Tasks(count, plan), None
+            )
+            g_mid, g_down = blocked(weight_grad(n2_all, dmid)), blocked(weight_grad(hid, df_all))
+            plan = {"reduce": (0, [g_mid, g_down]), "gather": (1, sum_attn)}
+        dx, dx_saved, ga_part, da_all, dqkv, *more = attn_backward(
             layer, n, dh, x, gain_a, tables, qkv, attn_own, attn_other, Tasks(count, plan)
         )
-        sums[f"ffn{layer}"] = more[:2]
-        if layer == 0:
-            attn_full = more[2:]
-        attn_grad = [blocked(weight_grad(n_all, dqkv)), blocked(weight_grad(o, da_all))]
-        gain_parts[layer] = jnp.concatenate([ga_part, gf_part], axis=0)
-        in_grads[layer] = dx
+        if layer == 1:
+            sum_mid, down_full = more
+        else:
+            sum_ffn, attn_full = more[:2], more[2:]
+        attn_grad = [blocked(weight_grad(dqkv, n_all)), blocked(weight_grad(o, da_all))]
+        gain_parts[layer] = [ga_part, gf_part]
+        in_grads[layer] = dx_saved
         dy = dx
-    gain_sums, g_mid, g_down, g_qkv, g_out = tail(
+    gain_sums, section_out, in_grad, g_mid, g_down, g_qkv, g_out = tail(
         n,
         count,
-        jnp.concatenate(gain_parts, axis=0),
-        sums["ffn0"],
+        gain_parts[0] + gain_parts[1],
+        outs + in_grads,
+        sum_ffn,
         attn_grad,
-        ffn_full,
+        [mid_full, down_full],
         attn_full,
     )
     gain_own = jnp.where(first, gain_sums[0:2], gain_sums[2:4])
-    g_mid, g_qkv = (array.reshape(2, -1, array.shape[-1]) for array in (g_mid, g_qkv))
-    g_down, g_out = (array.reshape(-1, array.shape[-1]).astype(F32)[None] for array in (g_down, g_out))
-
-    def columns(array, start, size):
-        parts = [array[core, :, start : start + size].astype(F32) for core in range(2)]
+    g_mid, g_qkv = (array.reshape(3, -1, array.shape[-1]) for array in (g_mid, g_qkv))
+    g_down, g_out = (
+        array[:2].astype(F32).reshape(1, -1, array.shape[-1]) for array in (g_down, g_out)
+    )
+
+    def columns(start, size):
+        parts = [g_mid[core, :, start : start + size].astype(F32) for core in range(2)]
         return jnp.concatenate(parts, axis=1)[None]
 
+    def turned(start, size):
+        parts = [g_qkv[core, start : start + size].astype(F32) for core in range(2)]
+        return jnp.concatenate(parts, axis=0).T[None]
+
     mid = w_gate.shape[2] // 2
-    g_gate, g_up = columns(g_mid, 0, mid), columns(g_mid, mid, mid)
+    g_gate, g_up = columns(0, mid), columns(mid, mid)
     q_half, k_half = w_query.shape[2] // 2, w_key.shape[2] // 2
-    g_query = columns(g_qkv, 0, q_half)
-    g_key, g_value = (columns(g_qkv, q_half + at, k_half) for at in (0, k_half))
-
-    def by_layer(values):
-        keep = jnp.where(first, values[0], values[1])
-        got = swap(jnp.where(first, values[1], values[0]))
-        return jnp.stack([jnp.where(first, keep, got), jnp.where(first, got, keep)])[None]
-
+    g_query = turned(0, q_half)
+    g_key, g_value = turned(q_half, k_half), turned(q_half + k_half, k_half)
     return (
-        by_layer(outs),
-        by_layer(in_grads),
+        section_out[None],
+        in_grad[None],
         gain_own[0:1],
         g_query,
         g_key,

time: 578 us -> 543 us (0.939)
  Pallas kernels: 484 us -> 467 us
  other arithmetic: 31.4 us -> 20.9 us
  local copies, waits for them, and re-layouts: 32.8 us -> 26 us
    pallas_call x9, Pallas kernels: 484 us -> 467 us  [run_kernel(): pl.pallas_call(kernel, name=name, in_specs=[HBM_SPEC if spec in (LOAD, LO...]
    unnamed x148 -> x92, local copies, waits for them, and re-layouts: 29.4 us -> 17.5 us
  transfers between devices with their start and end apart: 3 -> 1, of which waited for: 0 -> 0; matrix products, arithmetic and copies ran while one was open for 6% -> 1% of each run, Pallas kernels for 0% -> 0%
where the time goes in v3:
time: 543 us; the launch traced here: 535 us
  Pallas kernels  467 us (86%)
  local copies, waits for them, and re-layouts  26 us (5%)
  other arithmetic  20.9 us (4%)
  matrix products  19.1 us (4%)
    pallas_call x9, Pallas kernels, run_kernel(): pl.pallas_call(kernel, name=name, in_specs=[HBM_SPEC if spec in (LOAD, LO...  467 us
    dot_general x8, matrix products, dot_tn(): lax.dot_general(left, right, (((0,), (0,)), ((), ())), preferred_element_...  19.1 us
    unnamed x92, local copies, waits for them, and re-layouts  17.5 us
  transfers between devices with their start and end apart: 1, of which 0 were waited for; matrix products, arithmetic and copies ran while one was open for 1% of the time, Pallas kernels for 0%

profile of v3, /device:TPU:0, one launch (start us, length us, event | category | flops | bytes accessed | tf_op | source)
XLA Modules:
  0.0 534.9 jit_solution(10978047204660873869)
XLA Ops:
  0.7 0.8 pad_maximum_fusion
  1.5 0.6 collective-permute-start
  2.1 0.8 fusion.13
  2.8 0.2 reduce-window.4
  3.0 0.6 slice.75
  3.6 0.8 bitcast_subtract_fusion
  4.4 0.1 convert_reduce_fusion
  4.4 0.1 compare_select_fusion.refs_4_.refs_5_
  4.6 0.7 pad_add_fusion
  5.3 0.1 select_reduce_fusion
  5.4 0.1 reduce_sum.26
  5.5 0.8 fusion.10
  6.3 1.3 copy.53.refs_7_.refs_8_.refs_9_
  7.6 1.3 copy.54.refs_8_.refs_9_.refs_10_
  9.1 1.1 copy-done.6
  10.1 51.3 %attn_fwd0.1 = (f32[96,1536]{1,0:T(8,128)S(1)}, f32[96,1536]{1,0:T(8,128)S(1)}, bf16[2,4,96,1536]{3,2,1,0:T(8,128)(2,1)}, bf16[4,96,1024]{2,1,0:T(8,128)(2,1)S(1...) custom-call(bf16[2,96,1536]{2,1,0:T(8,128)(2,1)S(1)} %copy-done.6, ...), custom_call_target="tpu_custom_call" | custom-call | flops 1811939328 | bytes 8388608 | tf_op jit(solution)/shard_map/attn_fwd0/pallas_call | solution.py:1100
  61.5 1.0 copy-done.2
  62.5 1.0 copy-done.3
  63.5 0.8 copy-done.16
  64.3 42.5 %ffn_fwd0.1 = (bf16[96,1536]{1,0:T(8,128)(2,1)S(1)}, bf16[96,1536]{1,0:T(8,128)(2,1)S(1)}, bf16[2,4,96,1536]{3,2,1,0:T(8,128)(2,1)S(1)}, f32[4,96,1024]{2,1,0:T(...) custom-call(f32[96,1536]{1,0:T(8,128)S(1)} %get-tuple-element.73.refs_0_, ...), custom_call_target="tpu_custom_call" | custom-call | flops 3623878656 | bytes 16777216 | tf_op jit(solution)/shard_map/ffn_fwd0/pallas_call | solution.py:1100
  106.9 54.6 %attn_fwd1.1 = (f32[96,1536]{1,0:T(8,128)S(1)}, f32[96,1536]{1,0:T(8,128)S(1)}, bf16[2,4,96,1536]{3,2,1,0:T(8,128)(2,1)}, bf16[4,96,1024]{2,1,0:T(8,128)(2,1)S(1...) custom-call(bf16[96,1536]{1,0:T(8,128)(2,1)S(1)} %get-tuple-element.77.refs_0_, ...), custom_call_target="tpu_custom_call" | custom-call | flops 1811939328 | bytes 8388608 | tf_op jit(solution)/shard_map/attn_fwd1/pallas_call | solution.py:1100
  161.5 0.8 copy-done.18
  162.4 40.9 %ffn_fwd1.1 = (bf16[96,1536]{1,0:T(8,128)(2,1)}, bf16[96,1536]{1,0:T(8,128)(2,1)S(1)}, bf16[2,4,96,1536]{3,2,1,0:T(8,128)(2,1)S(1)}, f32[4,96,1024]{2,1,0:T(8,12...) custom-call(f32[96,1536]{1,0:T(8,128)S(1)} %get-tuple-element.83.refs_0_, ...), custom_call_target="tpu_custom_call" | custom-call | flops 3623878656 | bytes 16777216 | tf_op jit(solution)/shard_map/ffn_fwd1/pallas_call | solution.py:1100
  203.3 0.0 copy-start.8
  203.3 1.1 copy-done.8
  204.4 1.1 copy-done.10
  205.6 1.4 copy-done.28
  207.0 3.2 fusion.2
  210.3 32.1 %ffn_bwd1.1 = (f32[96,1536]{1,0:T(8,128)S(1)}, f32[1,1536]{1,0:T(1,128)S(1)}, bf16[2,4,96,1024]{3,2,1,0:T(8,128)(2,1)S(1)}, bf16[2,64,1536]{2,1,0:T(8,128)(2,1)S(1)}) custom-call(bf16[2,96,1536]{2,1,0:T(8,128)(2,1)S(1)} %copy-done.5, f32[96,1536]{1,0:T(8,128)S(1)} %copy-done.19, f32[1,1536]{1,0:T(1,128)S(1)} %get-tuple-element.147.refs_1_.refs_2_, ...), custom_call_target="tpu_custom_call" | custom-call | flops 3623878656 | bytes 16777216 | tf_op jit(solution)/shard_map/ffn_bwd1/pallas_call | solution.py:1100
  242.4 5.8 %bitcast_convert_fusion.1 = bf16[1536,1024]{1,0:T(8,128)(2,1)} fusion(bf16[2,4,96,1536]{3,2,1,0:T(8,128)(2,1)} %copy-done.28, bf16[2,4,96,1024]{3,2,1,0:T(8,128)(2,1)S(1)} %get-tuple-element.92), kind=kOutput, calls=%fused_computation.1 | convolution fusion | flops 2417491968 | bytes 7077888 | tf_op jit(solution)/shard_map/dot_general | solution.py:37
  248.1 56.5 %attn_bwd1.1 = (bf16[96,1536]{1,0:T(8,128)(2,1)S(1)}, bf16[96,1536]{1,0:T(8,128)(2,1)S(1)}, f32[1,1536]{1,0:T(1,128)S(1)}, bf16[2,4,96,1536]{3,2,1,0:T(8,128)(2,...) custom-call(f32[96,1536]{1,0:T(8,128)S(1)} %get-tuple-element.88.ref, ...), custom_call_target="tpu_custom_call" | custom-call | flops 2415919104 | bytes 8388608 | tf_op jit(solution)/shard_map/attn_bwd1/pallas_call | solution.py:1100
  304.7 1.1 fusion.4
  305.8 0.0 copy-start.17
  305.8 0.6 copy-done.32
  306.5 0.7 fusion.6
  307.1 53.5 %ffn_bwd0.1 = (f32[96,1536]{1,0:T(8,128)S(1)}, f32[1,1536]{1,0:T(1,128)S(1)}, bf16[2,4,96,1536]{3,2,1,0:T(8,128)(2,1)}, bf16[2,4,96,1024]{3,2,1,0:T(8,128)(2,1)S...) custom-call(bf16[96,1536]{1,0:T(8,128)(2,1)S(1)} %get-tuple-element., ...), custom_call_target="tpu_custom_call" | custom-call | flops 3623878656 | bytes 16777216 | tf_op jit(solution)/shard_map/ffn_bwd0/pallas_call | solution.py:1100
  360.7 4.0 bitcast_convert_fusion
  364.7 2.6 fusion.3
  367.3 61.9 %attn_bwd0.1 = (bf16[96,1536]{1,0:T(8,128)(2,1)}, bf16[96,1536]{1,0:T(8,128)(2,1)S(1)}, f32[1,1536]{1,0:T(1,128)S(1)}, bf16[2,4,96,1536]{3,2,1,0:T(8,128)(2,1)},...) custom-call(f32[96,1536]{1,0:T(8,128)S(1)} %get-tuple-element.103.re, ...), custom_call_target="tpu_custom_call" | custom-call | flops 2415919104 | bytes 8388608 | tf_op jit(solution)/shard_map/attn_bwd0/pallas_call | solution.py:1100
  429.2 1.1 fusion.5
  430.3 0.6 copy-done.30
  431.0 0.7 fusion.7
  431.6 0.3 copy-done.4
  431.9 0.0 copy-done.25
  432.0 73.6 %tail.1 = (f32[4,1536]{1,0:T(4,128)S(1)}, bf16[2,96,1536]{2,1,0:T(8,128)(2,1)S(1)}, bf16[2,96,1536]{2,1,0:T(8,128)(2,1)S(1)}, bf16[3,2,2,2,192,1024]{5,4,3,2,1,0...) custom-call(f32[1,1536]{1,0:T(1,128)S(1)} %get-tuple-element.111.ref, ...), custom_call_target="tpu_custom_call", output_to_operand_aliasing={{3}: (12, {}), {4}: (13, {}), {5}: (14, {}), {6}: (15, {})} | custom-call | flops 1048576 | bytes 16777216 | tf_op jit(solution)/shard_map/tail/pallas_call | solution.py:1100
  505.6 2.2 slice_bitcast_fusion.5
  507.7 2.1 fusion.14
  509.9 0.6 fusion.15
  510.5 0.1 slice.89
  510.6 1.7 convert.25
  512.3 0.3 copy.75
  512.6 2.3 copy.76
  514.9 2.3 slice.95
  517.2 3.6 convert.28
  520.8 0.5 slice_bitcast_fusion.1
  521.3 0.4 copy-done.36
  521.7 0.1 copy-done.37
  521.8 1.1 convert_bitcast_fusion.1
  523.0 1.8 convert_bitcast_fusion
  524.8 1.1 convert_bitcast_fusion.2
  525.9 3.6 fusion.1
  529.5 3.6 fusion
  533.1 0.8 copy.83
  533.9 0.8 copy.84
  (79 shorter events, 0.2 us)
Async XLA Ops:
  0.6 8.3 %copy-start.38 = (bf16[1,1536]{1,0:T(2,128)(2,1)S(1)}, bf16[1,1536]{1,0:T(2,128)(2,1)}, u32[]{:S(2)}) copy-start(bf16[1,1536]{1,0:T(2,128)(2,1)} %param.20) | copy-start | bytes 9220
  0.7 8.3 %copy-start.39 = (bf16[1,1536]{1,0:T(2,128)(2,1)S(1)}, bf16[1,1536]{1,0:T(2,128)(2,1)}, u32[]{:S(2)}) copy-start(bf16[1,1536]{1,0:T(2,128)(2,1)} %param.15) | copy-start | bytes 9220
  0.7 8.4 %copy-start = (bf16[1,1536,384]{2,1,0:T(8,128)(2,1)S(1)}, bf16[1,1536,384]{2,1,0:T(8,128)(2,1)}, u32[]{:S(2)}) copy-start(bf16[1,1536,384]{2,1,0:T(8,128)(2,1)} %refs_8_.5) | copy-start | bytes 3538948
  1.5 7.5 %collective-permute-start = (bf16[2,1536]{1,0:T(2,128)(2,1)S(1)}, bf16[2,1536]{1,0:T(2,128)(2,1)S(1)}, u32[]{:S(2)}, u32[]{:S(2)}) collective-permute-start(bf16[2,1536]{1,0:T(2,128)(2,1)S(1)} %pad_maximum_fusion), channel_id=1, source_target_pairs={{0,16},{16,0},{1,17},{17,1},{2,18},{18,2},{3,19},{19,3},{4,20},{20... | collective-permute-start | bytes 18440 | tf_op jit(solution)/shard_map/ppermute | solution.py:1440
  9.1 1.1 copy-start.6
  61.5 1.0 copy-start.2
  62.5 1.0 copy-start.3
  63.5 0.8 copy-start.16
  64.3 42.5 %copy-start.20 = (bf16[2,4,96,192]{3,2,1,0:T(8,128)(2,1)}, bf16[2,4,96,192]{3,2,1,0:T(8,128)(2,1)S(1)}, u32[]{:S(2)}) copy-start(bf16[2,4,96,192]{3,2,1,0:T(8,128)(2,1)S(1)} %get-tuple-element.122) | copy-start | bytes 884740
  64.3 42.6 %copy-start.1 = (bf16[1,384,1536]{2,1,0:T(8,128)(2,1)S(1)}, bf16[1,384,1536]{2,1,0:T(8,128)(2,1)}, u32[]{:S(2)}) copy-start(bf16[1,384,1536]{2,1,0:T(8,128)(2,1)} %refs_11_.5) | copy-start | bytes 3538948
  64.3 42.6 %copy-start.5 = (bf16[2,96,1536]{2,1,0:T(8,128)(2,1)S(1)}, bf16[2,96,1536]{2,1,0:T(8,128)(2,1)}, u32[]{:S(2)}) copy-start(bf16[2,96,1536]{2,1,0:T(8,128)(2,1)} %refs_0_.3) | copy-start | bytes 1769476
  106.8 54.7 %copy-start.12 = (bf16[2,4,96,512]{3,2,1,0:T(8,128)(2,1)}, bf16[2,4,96,512]{3,2,1,0:T(8,128)(2,1)S(1)}, u32[]{:S(2)}) copy-start(bf16[2,4,96,512]{3,2,1,0:T(8,128)(2,1)S(1)} %get-tuple-element.107) | copy-start | bytes 2359300
  106.9 54.7 %copy-start.26 = (bf16[2,4,96,1536]{3,2,1,0:T(8,128)(2,1)}, bf16[2,4,96,1536]{3,2,1,0:T(8,128)(2,1)S(1)}, u32[]{:S(2)}) copy-start(bf16[2,4,96,1536]{3,2,1,0:T(8,128)(2,1)S(1)} %get-tuple-element.105) | copy-start | bytes 7077892
  161.5 0.8 copy-start.18
  162.4 40.9 %copy-start.14 = (bf16[4,96,1024]{2,1,0:T(8,128)(2,1)}, bf16[4,96,1024]{2,1,0:T(8,128)(2,1)S(1)}, u32[]{:S(2)}) copy-start(bf16[4,96,1024]{2,1,0:T(8,128)(2,1)S(1)} %get-tuple-element.90.refs_7_) | copy-start | bytes 2359300
  162.4 40.9 %copy-start.22 = (bf16[2,4,96,192]{3,2,1,0:T(8,128)(2,1)}, bf16[2,4,96,192]{3,2,1,0:T(8,128)(2,1)S(1)}, u32[]{:S(2)}) copy-start(bf16[2,4,96,192]{3,2,1,0:T(8,128)(2,1)S(1)} %get-tuple-element.100) | copy-start | bytes 884740
  203.3 1.1 copy-start.8
  204.4 1.1 copy-start.10
  205.6 1.4 copy-start.28
  207.0 3.2 copy-start.24
  207.0 3.3 copy-start.9
  207.0 3.3 copy-start.11
  207.0 3.3 copy-start.19
  242.3 5.8 %copy-start.15 = (bf16[4,96,1024]{2,1,0:T(8,128)(2,1)S(1)}, bf16[4,96,1024]{2,1,0:T(8,128)(2,1)}, u32[]{:S(2)}) copy-start(bf16[4,96,1024]{2,1,0:T(8,128)(2,1)} %copy-done.14) | copy-start | bytes 2359300
  248.1 56.6 %copy-start.34 = (bf16[2,4,96,1536]{3,2,1,0:T(8,128)(2,1)S(1)}, bf16[2,4,96,1536]{3,2,1,0:T(8,128)(2,1)}, u32[]{:S(2)}) copy-start(bf16[2,4,96,1536]{3,2,1,0:T(8,128)(2,1)} %get-tuple-element.99) | copy-start | bytes 7077892
  304.6 1.2 copy-start.23
  304.7 1.8 copy-start.32
  305.8 1.3 copy-start.17
  307.1 53.5 %copy-start.27 = (bf16[2,4,96,1536]{3,2,1,0:T(8,128)(2,1)S(1)}, bf16[2,4,96,1536]{3,2,1,0:T(8,128)(2,1)}, u32[]{:S(2)}) copy-start(bf16[2,4,96,1536]{3,2,1,0:T(8,128)(2,1)} %copy-done.26) | copy-start | bytes 7077892
  360.6 4.1 copy-start.13
  360.7 4.1 copy-start.31
  364.7 2.6 copy-start.7
  367.3 61.9 %copy-start.33 = (bf16[2,4,96,1536]{3,2,1,0:T(8,128)(2,1)S(1)}, bf16[2,4,96,1536]{3,2,1,0:T(8,128)(2,1)}, u32[]{:S(2)}) copy-start(bf16[2,4,96,1536]{3,2,1,0:T(8,128)(2,1)} %get-tuple-element.121) | copy-start | bytes 7077892
  429.2 1.2 copy-start.21
  429.2 1.8 copy-start.30
  430.3 1.6 copy-start.4
  430.3 1.6 copy-start.25
  512.5 8.2 %slice-start = ((s8[9437184]{0:T(1024)(128)(4,1)}), s8[1048576]{0:T(1024)(128)(4,1)S(1)}, s32[]{:S(2)}) async-start(s8[9437184]{0:T(1024)(128)(4,1)} %bitcast.130), calls=%async_computation | async-start | bytes 2097152
  514.9 5.9 %slice-start.1 = ((s8[9437184]{0:T(1024)(128)(4,1)}), s8[4194304]{0:T(1024)(128)(4,1)S(1)}, s32[]{:S(2)}) async-start(s8[9437184]{0:T(1024)(128)(4,1)} %bitcast.130), calls=%async_computation.1 | async-start | bytes 8388608
  517.2 3.6 slice-start.2
  520.8 1.0 copy-start.36
  520.8 1.0 copy-start.37
  520.8 2.2 copy-start.29
  523.0 1.8 copy-start.35

commit v4 on v3

--- a/solution.py
+++ b/solution.py
@@ -17,6 +17,7 @@
 VMEM = pltpu.VMEM
 VMEM_SPEC = pl.BlockSpec(memory_space=pltpu.VMEM)
 LOAD, LOAD_MINE = "load", "load mine"
+VMEM_LIMITS = {"attn_fwd0": 61, "tail": 61}
 HBM_SPEC = pl.BlockSpec(memory_space=pltpu.HBM)
 DMA = pltpu.SemaphoreType.DMA
 
@@ -137,22 +138,21 @@
         goes = (shard > me) & (shard < n) if d == 0 else (shard >= 0) & (shard < me)
         first = (me == 0) if d == 0 else (me == n - 1)
 
-        @pl.when(goes & first)
+        @pl.when(goes)
         def _():
-            mine = partial(shard)
             for c in range(CHUNKS):
-                rows = slice(c * self.rows, (c + 1) * self.rows)
-                self.sbuf[shard, self.span(c)] = mine[rows].astype(BF16)
-                self.sum_copy(d, shard, c).start()
-
-        @pl.when(goes & jnp.logical_not(first))
-        def _():
-            mine = partial(shard)
-            for c in range(CHUNKS):
-                rows = slice(c * self.rows, (c + 1) * self.rows)
-                self.sum_copy(d, shard, c).wait_recv()
-                arrived = self.rbuf[d, shard, self.span(c)].astype(F32)
-                self.sbuf[shard, self.span(c)] = (mine[rows] + arrived).astype(BF16)
+                mine = partial[shard, self.span(c)]
+
+                @pl.when(first)
+                def _():
+                    self.sbuf[shard, self.span(c)] = mine.astype(BF16)
+
+                @pl.when(jnp.logical_not(first))
+                def _():
+                    self.sum_copy(d, shard, c).wait_recv()
+                    arrived = self.rbuf[d, shard, self.span(c)].astype(F32)
+                    self.sbuf[shard, self.span(c)] = (mine + arrived).astype(BF16)
+
                 self.sum_copy(d, shard, c).start()
 
     def sum_take(self, total):
@@ -235,17 +235,7 @@
                 compute(shard)
 
 
-def sums_after(line, partial, each=lambda step: None):
-    me, n = line.me, line.n
-
-    @pl.loop(0, n - 1)
-    def _(step):
-        line.sum_step(0, me + n - 1 - step, partial)
-        line.sum_step(1, step - (n - 1 - me), partial)
-        each(step)
-
-
-def sums_alone(line, compute, partial, halfway):
+def sums_alone(line, compute, partial, each):
     me, n = line.me, line.n
 
     @pl.loop(0, n)
@@ -262,10 +252,7 @@
 
         line.sum_step(0, me + n - 1 - step, partial)
         line.sum_step(1, step - (n - 1 - me), partial)
-
-        @pl.when(step == n - 2)
-        def _():
-            halfway()
+        each(step)
 
 
 class Weights:
@@ -696,11 +683,18 @@
 
 
 def spread_qkv(wq, wk, wv, wqkv):
+    small = wk.shape[0]
     q_wide = wq.shape[1] // HEAD * LANES
-    k_wide = wk.shape[1] // HEAD * LANES
-    wqkv[:, :q_wide] = dot_nn(wq[...], pick_split(wq.shape[1])).astype(BF16)
-    wqkv[:, q_wide : q_wide + k_wide] = dot_nn(wk[...], pick_split(wk.shape[1])).astype(BF16)
-    wqkv[:, q_wide + k_wide :] = dot_nn(wv[...], pick_plain(wv.shape[1])).astype(BF16)
+    k_wide = small // HEAD * LANES
+    pick_q, pick_k, pick_v = pick_split(wq.shape[1]), pick_split(small), pick_plain(small)
+    size = 2 * LANES
+
+    @pl.loop(0, wq.shape[0] // size)
+    def _(block):
+        rows = pl.ds(pl.multiple_of(block * size, size), size)
+        wqkv[rows, :q_wide] = dot_nn(wq[rows], pick_q).astype(BF16)
+        wqkv[rows, q_wide : q_wide + k_wide] = dot_tn(wk[:, rows], pick_k).astype(BF16)
+        wqkv[rows, q_wide + k_wide :] = dot_tn(wv[:, rows], pick_v).astype(BF16)
 
 
 def allowed_pairs(seg_col, seg_row):
@@ -757,9 +751,9 @@
         h_out, h_save, n_out, qkv_out, o_out, ahead_out = refs[at + others : at + others + 6]
         at += 1
     at += 5 + others
-    (wq, wk, wv, wo, wqkv, qkv, o, osmall, wsem) = refs[at : at + 9]
-    pair = Pair(*refs[at + 9 : at + 12])
-    at += 12
+    (wq, wk, wv, wo, wqkv, qkv, o, osmall, part, wsem) = refs[at : at + 10]
+    pair = Pair(*refs[at + 10 : at + 13])
+    at += 13
     if ahead:
         second = Line(n, refs[at], None, None, *refs[at + 1 : at + 3], None, None)
         at += 3
@@ -829,16 +823,22 @@
     pair.share_half(osmall, o_out)
     wide = wo.shape[0] * LANES
 
-    def partial(shard):
-        return dot_nn(o[shard], wo[...].reshape(wide, -1))
+    def project(shard):
+        part[shard] = dot_nn(o[shard], wo[...].reshape(wide, -1))
 
     if ahead:
-        sums_after(line, partial, lambda step: second.gather_step(step + 1))
+
+        def each(step):
+            @pl.when(step < n - 1)
+            def _():
+                second.gather_step(step + 1)
+
+        sums_alone(line, project, part, each)
         pair.keep(second.full, ahead_out.at[0])
         pair.send(second.full, ahead_out.at[1])
     else:
-        sums_after(line, partial)
-    h_out[...] = resid + partial(me)
+        sums_alone(line, project, part, lambda step: None)
+    h_out[...] = x[...].astype(F32) + part[me]
     line.sum_take(h_out)
     pair.keep(h_out, h_save)
     if ahead:
@@ -874,7 +874,7 @@
     (dh, x, gain, cos, sin, seg_col, seg_row, qkv_in) = refs[:8]
     own, other = refs[8:12], refs[12:16]
     (dx_out, dx_save, gain_out, da_out, dqkv_out) = refs[16:21]
-    (wq, wk, wv, wo, wqkv, qkv, d_o, dqkv, dsmall, total, wsem, tsem) = refs[21:33]
+    (wq, wk, wv, wo, wqkv, qkv, d_o, dqkv, dsmall, part, wsem, tsem) = refs[21:33]
     pair = Pair(*refs[33:36])
     line = Line(n, *refs[36:])
     me = line.me
@@ -940,13 +940,12 @@
 
     pair.share_half(dsmall, dqkv_out)
 
-    def partial(shard):
-        return dot_nt(dqkv[shard], wqkv[...])
-
-    sums_after(line, partial, lambda step: pl.when(step == 0)(tasks.advance))
-    total[...] = partial(me)
-    line.sum_take(total)
-    d_resid, gain_part = norm_back(total[...], x[...].astype(F32), gain[...])
+    def project(shard):
+        part[shard] = dot_nt(dqkv[shard], wqkv[...])
+
+    sums_alone(line, project, part, lambda step: pl.when(step == 0)(tasks.advance))
+    line.sum_take(part.at[me])
+    d_resid, gain_part = norm_back(part[me], x[...].astype(F32), gain[...])
     dx_out[...] = (dh[...] + d_resid).astype(BF16)
     gain_out[...] = gain_part
     pair.keep(dx_out, dx_save)
@@ -992,7 +991,7 @@
     pair.stream_share_half(hid, hid_out)
     pair.stream_keep(gate, gate_out)
     pair.stream_keep(up, up_out)
-    rows_then_sums(line, compute, lambda shard: part[shard])
+    rows_then_sums(line, compute, part)
     part[me] += h[...]
     line.sum_take(part.at[me])
     y_out[...] = part[me].astype(BF16)
@@ -1055,10 +1054,10 @@
 
     pair.stream_share_half(dmid, dmid_out)
     if gathered:
-        sums_alone(line, compute, lambda shard: part[shard], tasks.advance)
+        sums_alone(line, compute, part, lambda step: pl.when(step == n - 2)(tasks.advance))
     else:
         pair.stream_share(line.full, df_all)
-        rows_then_sums(line, compute, lambda shard: part[shard], tasks.advance)
+        rows_then_sums(line, compute, part, tasks.advance)
     line.sum_take(part.at[me])
     d_resid, gain_part = norm_back(part[me], h[...], gain[...])
     dh_out[...] = dy[...].astype(F32) + d_resid
@@ -1107,7 +1106,7 @@
         input_output_aliases=aliases or {},
         cost_estimate=pl.CostEstimate(flops=flops, bytes_accessed=nbytes, transcendentals=0),
         compiler_params=pltpu.CompilerParams(
-            collective_id=cid, has_side_effects=True, vmem_limit_bytes=44 << 20
+            collective_id=cid, has_side_effects=True, vmem_limit_bytes=VMEM_LIMITS.get(name, 44) << 20
         ),
     )(*args)
 
@@ -1115,11 +1114,11 @@
 def attn_forward(layer, n, x, gain, tables, own, other, rows_ahead):
     rows, width = x.shape[-2:]
     heads = own[0].shape[2] // HEAD
-    kv_heads = own[1].shape[2] // HEAD
+    kv_heads = own[1].shape[1] // HEAD
     wide = (heads + 2 * kv_heads) * LANES
     small = heads // kv_heads * HEAD
     args = [x, gain, *tables]
-    specs = [LOAD_MINE if x.ndim == 3 else VMEM_SPEC] + [LOAD] * 5
+    specs = [LOAD_MINE] + [VMEM_SPEC] * 5 if layer == 0 else [VMEM_SPEC] + [LOAD] * 5
     if layer == 1:
         args.append(rows_ahead)
         specs.append(LOAD_MINE)
@@ -1141,13 +1140,14 @@
     scratch = (
         [
             VMEM((width, heads * HEAD), BF16),
-            VMEM((width, kv_heads * HEAD), BF16),
-            VMEM((width, kv_heads * HEAD), BF16),
+            VMEM((kv_heads * HEAD, width), BF16),
+            VMEM((kv_heads * HEAD, width), BF16),
             VMEM((heads, LANES, width), BF16),
             VMEM((width, wide), BF16),
             VMEM((n, rows, wide), BF16),
             VMEM((n, rows, heads * LANES), BF16),
             VMEM((kv_heads, n, rows, small), BF16),
+            VMEM((n, rows, width), F32),
             DMA((3 + heads,)),
         ]
         + pair_scratch(n, 5, 3 + (len(own) if other is None else 0))
@@ -1162,7 +1162,7 @@
 def attn_backward(layer, n, dh, x, gain, tables, qkv, own, other, tasks):
     rows, width = dh.shape
     heads = own[0].shape[2] // HEAD
-    kv_heads = own[1].shape[2] // HEAD
+    kv_heads = own[1].shape[1] // HEAD
     wide = (heads + 2 * kv_heads) * LANES
     small = (heads // kv_heads + 2) * HEAD
     args = [dh, x, gain, *tables, qkv, *own, *other]
@@ -1177,15 +1177,15 @@
     scratch = (
         [
             VMEM((width, heads * HEAD), BF16),
-            VMEM((width, kv_heads * HEAD), BF16),
-            VMEM((width, kv_heads * HEAD), BF16),
+            VMEM((kv_heads * HEAD, width), BF16),
+            VMEM((kv_heads * HEAD, width), BF16),
             VMEM((heads, LANES, width), BF16),
             VMEM((width, wide), BF16),
             VMEM((n, rows, wide), BF16),
             VMEM((n, rows, heads * LANES), BF16),
             VMEM((n, rows, wide), BF16),
             VMEM((kv_heads, n, rows, small), BF16),
-            VMEM((rows, width), F32),
+            VMEM((n, rows, width), F32),
             DMA((3 + heads,)),
             DMA,
         ]
@@ -1436,6 +1436,108 @@
     return run_kernel(body, args, specs, outs, scratch, 9, 1 << 20, 16 << 20, "tail", aliases)
 
 
+BLOCK = 256
+
+
+def widen_kernel(mid_in, down_in, qkv_in, out_in, *refs):
+    outs, (mid, down, qkv, o), wide, (in_sem, out_sem) = refs[:7], refs[7:11], refs[11:18], refs[18:]
+    gate_w, up_w, down_w, q_w, k_w, v_w, out_w = wide
+    blocks = mid.shape[1] // BLOCK
+    half = mid.shape[2] // 2
+    down_rows, out_rows = down.shape[1], o.shape[1]
+    q_half, k_half = q_w.shape[1] // 2, k_w.shape[0] // 2
+
+    def part(block):
+        return pl.ds(pl.multiple_of(block * BLOCK, BLOCK), BLOCK)
+
+    def mid_load(core, block):
+        return pltpu.make_async_copy(
+            mid_in.at[core, part(block)], mid.at[core, part(block)], in_sem.at[core, block]
+        )
+
+    def whole_load(index):
+        source, target = ((down_in, down), (qkv_in, qkv), (out_in, o))[index]
+        return pltpu.make_async_copy(
+            source.at[pl.ds(0, 2)], target, in_sem.at[2, index]
+        )
+
+    def store(index, block=None):
+        if block is None:
+            return pltpu.make_async_copy(wide[index], outs[index], out_sem.at[index, 0])
+        return pltpu.make_async_copy(
+            wide[index].at[part(block)], outs[index].at[part(block)], out_sem.at[index, block]
+        )
+
+    @pl.loop(0, blocks)
+    def _(block):
+        for core in range(2):
+            mid_load(core, block).start()
+
+    for index in range(3):
+        whole_load(index).start()
+
+    @pl.loop(0, blocks)
+    def _(block):
+        for core in range(2):
+            mid_load(core, block).wait()
+            lanes = slice(core * half, (core + 1) * half)
+            gate_w[part(block), lanes] = mid[core, part(block), :half].astype(F32)
+            up_w[part(block), lanes] = mid[core, part(block), half:].astype(F32)
+        store(0, block).start()
+        store(1, block).start()
+
+    whole_load(0).wait()
+    for core in range(2):
+        down_w[core * down_rows : (core + 1) * down_rows] = down[core].astype(F32)
+    store(2).start()
+    whole_load(1).wait()
+
+    @pl.loop(0, qkv.shape[2] // BLOCK)
+    def _(block):
+        rows = jnp.concatenate(
+            [qkv[core, :q_half, part(block)].astype(F32) for core in range(2)], axis=0
+        )
+        q_w[part(block)] = rows.T
+
+    store(3).start()
+    for core in range(2):
+        rows = slice(core * k_half, (core + 1) * k_half)
+        k_w[rows] = qkv[core, q_half : q_half + k_half].astype(F32)
+        v_w[rows] = qkv[core, q_half + k_half :].astype(F32)
+    store(4).start()
+    store(5).start()
+    whole_load(2).wait()
+    for core in range(2):
+        out_w[core * out_rows : (core + 1) * out_rows] = o[core].astype(F32)
+    store(6).start()
+
+    @pl.loop(0, blocks)
+    def _(block):
+        store(0, block).wait()
+        store(1, block).wait()
+
+    for index in range(2, 7):
+        store(index).wait()
+
+
+def widened(g_mid, g_down, g_qkv, g_out, q_size, k_size):
+    width, hidden = g_mid.shape[1:]
+    shapes = [(width, hidden)] * 2 + [(2 * g_down.shape[1], width), (width, q_size)]
+    shapes += [(k_size, width)] * 2 + [(2 * g_out.shape[1], width)]
+    blocks = width // BLOCK
+    return pl.pallas_call(
+        widen_kernel,
+        name="widen",
+        in_specs=[HBM_SPEC] * 4,
+        out_shape=[jax.ShapeDtypeStruct(shape, F32) for shape in shapes],
+        out_specs=[HBM_SPEC] * 7,
+        scratch_shapes=[VMEM((2,) + array.shape[1:], BF16) for array in (g_mid, g_down, g_qkv, g_out)]
+        + [VMEM(shape, F32) for shape in shapes]
+        + [DMA((3, max(blocks, 3))), DMA((7, blocks))],
+        compiler_params=pltpu.CompilerParams(vmem_limit_bytes=61 << 20),
+    )(g_mid, g_down, g_qkv, g_out)
+
+
 def swap(values):
     return lax.ppermute(values, "section", [(0, 1), (1, 0)])
 
@@ -1480,7 +1582,7 @@
     first = section == 0
     n = lax.axis_size("tensor")
     rows = inputs.shape[1]
-    attn_own = (w_query, w_key, w_value, w_out)
+    attn_own = (w_query, jnp.swapaxes(w_key, 1, 2), jnp.swapaxes(w_value, 1, 2), w_out)
     ffn_own = (w_gate, w_up, w_down)
     gains = jnp.concatenate([gain_attn, gain_ffn], axis=0)
     gains_other = swap(gains)
@@ -1562,24 +1664,14 @@
         attn_full,
     )
     gain_own = jnp.where(first, gain_sums[0:2], gain_sums[2:4])
-    g_mid, g_qkv = (array.reshape(3, -1, array.shape[-1]) for array in (g_mid, g_qkv))
-    g_down, g_out = (
-        array[:2].astype(F32).reshape(1, -1, array.shape[-1]) for array in (g_down, g_out)
+    g_mid, g_down, g_qkv, g_out = (
+        array.reshape(array.shape[0], -1, array.shape[-1])
+        for array in (g_mid, g_down, g_qkv, g_out)
     )
-
-    def columns(start, size):
-        parts = [g_mid[core, :, start : start + size].astype(F32) for core in range(2)]
-        return jnp.concatenate(parts, axis=1)[None]
-
-    def turned(start, size):
-        parts = [g_qkv[core, start : start + size].astype(F32) for core in range(2)]
-        return jnp.concatenate(parts, axis=0).T[None]
-
-    mid = w_gate.shape[2] // 2
-    g_gate, g_up = columns(0, mid), columns(mid, mid)
-    q_half, k_half = w_query.shape[2] // 2, w_key.shape[2] // 2
-    g_query = turned(0, q_half)
-    g_key, g_value = turned(q_half, k_half), turned(q_half + k_half, k_half)
+    g_gate, g_up, g_down, g_query, g_key, g_value, g_out = (
+        grad[None] for grad in widened(g_mid, g_down, g_qkv, g_out, w_query.shape[2], w_key.shape[2])
+    )
+    g_key, g_value = jnp.swapaxes(g_key, 1, 2), jnp.swapaxes(g_value, 1, 2)
     return (
         section_out[None],
         in_grad[None],

time: 543 us -> 525 us (0.967)
  local copies, waits for them, and re-layouts: 26 us -> 9.76 us
  other arithmetic: 20.9 us -> 7.8 us
  Pallas kernels: 467 us -> 479 us
    pallas_call x0 -> x1, Pallas kernels: none -> 13.4 us  [widened(): pl.pallas_call(widen_kernel, name='widen', in_specs=[HBM_SPEC] * 4, out_s...]
    broadcast_in_dim x5 -> x0, other arithmetic: 11.2 us -> none  [the longest x2 7.16 us: columns(): return jnp.concatenate(parts, axis=1)[None]]
    unnamed x92 -> x98, local copies, waits for them, and re-layouts: 17.5 us -> 7.87 us
where the time goes in v4:
time: 525 us; the launch traced here: 517 us
  Pallas kernels  479 us (91%)
  matrix products  17.4 us (3%)
  local copies, waits for them, and re-layouts  9.76 us (2%)
  other arithmetic  7.8 us (1%)
    pallas_call x9, Pallas kernels, run_kernel(): pl.pallas_call(kernel, name=name, in_specs=[HBM_SPEC if spec in (LOAD, LO...  466 us
    dot_general x8, matrix products, dot_tn(): lax.dot_general(left, right, (((0,), (0,)), ((), ())), preferred_element_...  17.4 us
    pallas_call x1, Pallas kernels, widened(): pl.pallas_call(widen_kernel, name='widen', in_specs=[HBM_SPEC] * 4, out_s...  13.4 us
  transfers between devices with their start and end apart: 1, of which 0 were waited for; matrix products, arithmetic and copies ran while one was open for 1% of the time, Pallas kernels for 0%

profile of v4, /device:TPU:0, one launch (start us, length us, event | category | flops | bytes accessed | tf_op | source)
XLA Modules:
  0.0 516.5 jit_solution(3022398426895908330)
XLA Ops:
  0.6 0.7 pad_maximum_fusion
  1.4 0.6 collective-permute-start
  1.9 0.8 fusion.11
  2.7 0.2 reduce-window.4
  2.9 0.6 slice.39
  3.5 0.8 bitcast_subtract_fusion
  4.2 0.1 convert_reduce_fusion
  4.3 0.8 compare_select_fusion.refs_4_.refs_5_
  5.1 0.7 pad_add_fusion
  5.8 0.1 select_reduce_fusion
  5.9 0.1 reduce_sum.26
  6.0 1.5 fusion.8
  7.6 0.6 compare_select_fusion.1.refs_5_.refs_6_
  8.1 0.7 fusion.10
  8.9 0.6 fusion.13
  9.5 47.3 %attn_fwd0.1 = (f32[96,1536]{1,0:T(8,128)}, f32[96,1536]{1,0:T(8,128)}, bf16[2,4,96,1536]{3,2,1,0:T(8,128)(2,1)}, bf16[4,96,1024]{2,1,0:T(8,128)(2,1)}, bf16[2,4...) custom-call(bf16[2,96,1536]{2,1,0:T(8,128)(2,1)} %refs_1_.1, ...), custom_call_target="tpu_custom_call" | custom-call | flops 1811939328 | bytes 8388608 | tf_op jit(solution)/shard_map/attn_fwd0/pallas_call | solution.py:1099
  56.8 1.1 copy-done.24
  57.8 0.0 copy-start.4
  57.9 0.0 copy-start.7
  57.9 0.0 copy-start.8
  57.9 0.0 copy-start.9
  57.9 0.0 copy-start.10
  57.9 0.0 copy-start.32
  57.9 46.1 %ffn_fwd0.1 = (bf16[96,1536]{1,0:T(8,128)(2,1)S(1)}, bf16[96,1536]{1,0:T(8,128)(2,1)S(1)}, bf16[2,4,96,1536]{3,2,1,0:T(8,128)(2,1)S(1)}, f32[4,96,1024]{2,1,0:T(...) custom-call(f32[96,1536]{1,0:T(8,128)S(1)} %copy-done.24, ...), custom_call_target="tpu_custom_call" | custom-call | flops 3623878656 | bytes 16777216 | tf_op jit(solution)/shard_map/ffn_fwd0/pallas_call | solution.py:1099
  104.0 0.0 copy-start.17
  104.0 0.0 copy-start.37
  104.0 0.0 copy-start.14
  104.2 54.5 %attn_fwd1.1 = (f32[96,1536]{1,0:T(8,128)S(1)}, f32[96,1536]{1,0:T(8,128)S(1)}, bf16[2,4,96,1536]{3,2,1,0:T(8,128)(2,1)}, bf16[4,96,1024]{2,1,0:T(8,128)(2,1)S(1...) custom-call(bf16[96,1536]{1,0:T(8,128)(2,1)S(1)} %get-tuple-element.84.refs_0_, ...), custom_call_target="tpu_custom_call" | custom-call | flops 1811939328 | bytes 8388608 | tf_op jit(solution)/shard_map/attn_fwd1/pallas_call | solution.py:1099
  158.7 0.0 copy-start.19
  158.7 0.9 copy-done.19
  159.6 0.8 copy-done.22
  160.4 0.7 copy-done.25
  161.2 40.4 %ffn_fwd1.1 = (bf16[96,1536]{1,0:T(8,128)(2,1)}, bf16[96,1536]{1,0:T(8,128)(2,1)S(1)}, bf16[2,4,96,1536]{3,2,1,0:T(8,128)(2,1)S(1)}, f32[4,96,1024]{2,1,0:T(8,12...) custom-call(f32[96,1536]{1,0:T(8,128)S(1)} %get-tuple-element.90.refs_0_, ...), custom_call_target="tpu_custom_call" | custom-call | flops 3623878656 | bytes 16777216 | tf_op jit(solution)/shard_map/ffn_fwd1/pallas_call | solution.py:1099
  201.5 0.0 copy-start.12
  201.6 1.1 copy-done.12
  202.7 1.4 fusion
  204.1 0.1 copy-done.13
  204.2 0.1 copy-done.23
  204.3 31.8 %ffn_bwd1.1 = (f32[96,1536]{1,0:T(8,128)S(1)}, f32[1,1536]{1,0:T(1,128)S(1)}, bf16[2,4,96,1024]{3,2,1,0:T(8,128)(2,1)S(1)}, bf16[2,64,1536]{2,1,0:T(8,128)(2,1)S(1)}) custom-call(bf16[2,96,1536]{2,1,0:T(8,128)(2,1)S(1)} %copy-done.10, f32[96,1536]{1,0:T(8,128)S(1)} %copy-done.23, f32[1,1536]{1,0:T(1,128)S(1)} %get-tuple-element.151.refs_1_.refs_2_, ...), custom_call_target="tpu_custom_call" | custom-call | flops 3623878656 | bytes 16777216 | tf_op jit(solution)/shard_map/ffn_bwd1/pallas_call | solution.py:1099
  236.1 0.0 copy-start.20
  236.2 4.0 bitcast_convert_fusion.1
  240.2 56.0 %attn_bwd1.1 = (bf16[96,1536]{1,0:T(8,128)(2,1)S(1)}, bf16[96,1536]{1,0:T(8,128)(2,1)S(1)}, f32[1,1536]{1,0:T(1,128)S(1)}, bf16[2,4,96,1536]{3,2,1,0:T(8,128)(2,...) custom-call(f32[96,1536]{1,0:T(8,128)S(1)} %get-tuple-element.95.ref, ...), custom_call_target="tpu_custom_call" | custom-call | flops 2415919104 | bytes 8388608 | tf_op jit(solution)/shard_map/attn_bwd1/pallas_call | solution.py:1099
  296.3 0.0 copy-start.26
  296.3 1.1 fusion.2
  297.4 0.7 copy-done.42
  298.2 0.6 fusion.4
  298.9 52.7 %ffn_bwd0.1 = (f32[96,1536]{1,0:T(8,128)S(1)}, f32[1,1536]{1,0:T(1,128)S(1)}, bf16[2,4,96,1536]{3,2,1,0:T(8,128)(2,1)}, bf16[2,4,96,1024]{3,2,1,0:T(8,128)(2,1)S...) custom-call(bf16[96,1536]{1,0:T(8,128)(2,1)S(1)} %get-tuple-element., ...), custom_call_target="tpu_custom_call" | custom-call | flops 3623878656 | bytes 16777216 | tf_op jit(solution)/shard_map/ffn_bwd0/pallas_call | solution.py:1099
  351.6 0.0 copy-start.35
  351.6 0.0 copy-start.18
  351.6 4.0 bitcast_convert_fusion
  355.7 2.6 fusion.1
  358.3 62.1 %attn_bwd0.1 = (bf16[96,1536]{1,0:T(8,128)(2,1)}, bf16[96,1536]{1,0:T(8,128)(2,1)S(1)}, f32[1,1536]{1,0:T(1,128)S(1)}, bf16[2,4,96,1536]{3,2,1,0:T(8,128)(2,1)},...) custom-call(f32[96,1536]{1,0:T(8,128)S(1)} %get-tuple-element.110.re, ...), custom_call_target="tpu_custom_call" | custom-call | flops 2415919104 | bytes 8388608 | tf_op jit(solution)/shard_map/attn_bwd0/pallas_call | solution.py:1099
  420.4 0.0 copy-start.27
  420.4 0.0 copy-start.30
  420.4 2.1 fusion.3
  422.6 0.2 copy-done.40
  422.7 0.3 copy-done.47
  423.0 1.5 fusion.5
  424.5 75.0 %tail.1 = (f32[4,1536]{1,0:T(4,128)}, bf16[2,96,1536]{2,1,0:T(8,128)(2,1)}, bf16[2,96,1536]{2,1,0:T(8,128)(2,1)}, bf16[3,2,2,2,192,1024]{5,4,3,2,1,0:T(8,128)(2,...) custom-call(f32[1,1536]{1,0:T(1,128)} %copy-done.36, ...), custom_call_target="tpu_custom_call", output_to_operand_aliasing={{3}: (12, {}), {4}: (13, {}), {5}: (14, {}), {6}: (15, {})} | custom-call | flops 1048576 | bytes 16777216 | tf_op jit(solution)/shard_map/tail/pallas_call | solution.py:1099
  499.6 0.8 slice_select_fusion
  500.4 0.6 fusion.12
  501.0 13.4 %widen.1 = (f32[1536,1024]{1,0:T(8,128)}, f32[1536,1024]{1,0:T(8,128)}, f32[1024,1536]{1,0:T(8,128)}, f32[1536,384]{1,0:T(8,128)}, f32[192,1536]{1,0:T(8,128)}, ...) custom-call(bf16[3,1536,1024]{2,1,0:T(8,128)(2,1)} %bitcast.105, bf16[3,512,1536]{2,1,0:T(8,128)(2,1)} %bitcast.106, ...), custom_call_target="tpu_custom_call" | custom-call | tf_op jit(solution)/shard_map/widen/pallas_call | solution.py:1528
  514.4 0.8 copy.53
  515.2 0.8 copy.54
  (73 shorter events, 0.2 us)
Async XLA Ops:
  1.4 6.7 %collective-permute-start = (bf16[2,1536]{1,0:T(2,128)(2,1)S(1)}, bf16[2,1536]{1,0:T(2,128)(2,1)S(1)}, u32[]{:S(2)}, u32[]{:S(2)}) collective-permute-start(bf16[2,1536]{1,0:T(2,128)(2,1)S(1)} %pad_maximum_fusion), channel_id=1, source_target_pairs={{0,16},{16,0},{1,17},{17,1},{2,18},{18,2},{3,19},{19,3},{4,20},{20... | collective-permute-start | bytes 18440 | tf_op jit(solution)/shard_map/ppermute | solution.py:1542
  56.7 1.1 copy-start.24
  57.8 46.2 %copy-start = (bf16[1,1536,384]{2,1,0:T(8,128)(2,1)S(1)}, bf16[1,1536,384]{2,1,0:T(8,128)(2,1)}, u32[]{:S(2)}) copy-start(bf16[1,1536,384]{2,1,0:T(8,128)(2,1)} %refs_8_.3) | copy-start | bytes 3538948
  57.8 46.2 %copy-start.1 = (bf16[1,384,1536]{2,1,0:T(8,128)(2,1)S(1)}, bf16[1,384,1536]{2,1,0:T(8,128)(2,1)}, u32[]{:S(2)}) copy-start(bf16[1,384,1536]{2,1,0:T(8,128)(2,1)} %refs_11_.5) | copy-start | bytes 3538948
  57.8 46.2 %copy-start.2 = (bf16[1,1536,384]{2,1,0:T(8,128)(2,1)S(1)}, bf16[1,1536,384]{2,1,0:T(8,128)(2,1)}, u32[]{:S(2)}) copy-start(bf16[1,1536,384]{2,1,0:T(8,128)(2,1)} %get-tuple-element.85.refs_11_.refs_12_) | copy-start | bytes 3538948
  57.8 46.3 %copy-start.3 = (bf16[1,1536,192]{1,2,0:T(8,128)(2,1)S(1)}, bf16[1,1536,192]{1,2,0:T(8,128)(2,1)}, u32[]{:S(2)}) copy-start(bf16[1,1536,192]{1,2,0:T(8,128)(2,1)} %param.17) | copy-start | bytes 1769476
  57.8 46.3 %copy-start.4 = (bf16[1,1536,192]{1,2,0:T(8,128)(2,1)S(1)}, bf16[1,1536,192]{1,2,0:T(8,128)(2,1)}, u32[]{:S(2)}) copy-start(bf16[1,1536,192]{1,2,0:T(8,128)(2,1)} %param.18) | copy-start | bytes 1769476
  57.8 46.3 %copy-start.5 = (bf16[1,192,1536]{2,1,0:T(8,128)(2,1)S(1)}, bf16[1,192,1536]{2,1,0:T(8,128)(2,1)}, u32[]{:S(2)}) copy-start(bf16[1,192,1536]{2,1,0:T(8,128)(2,1)} %get-tuple-element.86.refs_12_.refs_13_) | copy-start | bytes 1769476
  57.8 46.3 %copy-start.6 = (bf16[1,192,1536]{2,1,0:T(8,128)(2,1)S(1)}, bf16[1,192,1536]{2,1,0:T(8,128)(2,1)}, u32[]{:S(2)}) copy-start(bf16[1,192,1536]{2,1,0:T(8,128)(2,1)} %get-tuple-element.87.refs_13_.refs_14_) | copy-start | bytes 1769476
  57.9 46.3 %copy-start.7 = (s32[384,1]{1,0:T(8,128)S(1)}, s32[384,1]{1,0:T(8,128)}, u32[]{:S(2)}) copy-start(s32[384,1]{1,0:T(8,128)} %compare_select_fusion.refs_4_.refs_5_) | copy-start | bytes 4612
  57.9 46.3 %copy-start.8 = (f32[4,96,128]{2,1,0:T(8,128)S(1)}, f32[4,96,128]{2,1,0:T(8,128)}, u32[]{:S(2)}) copy-start(f32[4,96,128]{2,1,0:T(8,128)} %get-tuple-element.157.refs_3_.refs_4_) | copy-start | bytes 589828
  57.9 46.3 %copy-start.9 = (f32[4,96,128]{2,1,0:T(8,128)S(1)}, f32[4,96,128]{2,1,0:T(8,128)}, u32[]{:S(2)}) copy-start(f32[4,96,128]{2,1,0:T(8,128)} %get-tuple-element.158.refs_2_.refs_3_) | copy-start | bytes 589828
  57.9 46.3 %copy-start.10 = (bf16[2,96,1536]{2,1,0:T(8,128)(2,1)S(1)}, bf16[2,96,1536]{2,1,0:T(8,128)(2,1)}, u32[]{:S(2)}) copy-start(bf16[2,96,1536]{2,1,0:T(8,128)(2,1)} %refs_0_.3) | copy-start | bytes 1769476
  57.9 46.2 %copy-start.32 = (s32[1,384]{1,0:T(1,128)S(1)}, s32[1,384]{1,0:T(1,128)}, u32[]{:S(2)}) copy-start(s32[1,384]{1,0:T(1,128)} %compare_select_fusion.1.refs_5_.refs_6_) | copy-start | bytes 4612
  104.0 54.7 %copy-start.17 = (bf16[2,4,96,512]{3,2,1,0:T(8,128)(2,1)}, bf16[2,4,96,512]{3,2,1,0:T(8,128)(2,1)S(1)}, u32[]{:S(2)}) copy-start(bf16[2,4,96,512]{3,2,1,0:T(8,128)(2,1)S(1)} %get-tuple-element.114) | copy-start | bytes 2359300
  104.0 54.7 %copy-start.37 = (bf16[2,4,96,1536]{3,2,1,0:T(8,128)(2,1)}, bf16[2,4,96,1536]{3,2,1,0:T(8,128)(2,1)S(1)}, u32[]{:S(2)}) copy-start(bf16[2,4,96,1536]{3,2,1,0:T(8,128)(2,1)S(1)} %get-tuple-element.112) | copy-start | bytes 7077892
  104.0 136.2 %copy-start.14 = (bf16[96,1536]{1,0:T(8,128)(2,1)}, bf16[96,1536]{1,0:T(8,128)(2,1)S(1)}, u32[]{:S(2)}) copy-start(bf16[96,1536]{1,0:T(8,128)(2,1)S(1)} %get-tuple-element.96.refs_1_.refs_4_) | copy-start | bytes 884740
  158.7 0.9 copy-start.19
  159.6 0.8 copy-start.22
  160.4 0.7 copy-start.25
  161.2 41.5 %copy-start.39 = (bf16[2,4,96,1536]{3,2,1,0:T(8,128)(2,1)S(1)}, bf16[2,4,96,1536]{3,2,1,0:T(8,128)(2,1)}, u32[]{:S(2)}) copy-start(bf16[2,4,96,1536]{3,2,1,0:T(8,128)(2,1)} %get-tuple-element.93.refs_11_) | copy-start | bytes 7077892
  201.5 1.1 copy-start.12
  202.7 1.4 copy-start.28
  202.7 1.5 copy-start.13
  202.7 1.6 copy-start.23
  236.1 4.1 copy-start.33
  236.1 4.1 copy-start.20
  240.2 56.1 %copy-start.44 = (bf16[2,4,96,1536]{3,2,1,0:T(8,128)(2,1)S(1)}, bf16[2,4,96,1536]{3,2,1,0:T(8,128)(2,1)}, u32[]{:S(2)}) copy-start(bf16[2,4,96,1536]{3,2,1,0:T(8,128)(2,1)} %get-tuple-element.106) | copy-start | bytes 7077892
  296.3 2.6 copy-start.29
  296.3 2.6 copy-start.34
  296.3 1.2 copy-start.26
  296.3 1.9 copy-start.42
  297.4 1.4 copy-start.21
  298.9 52.7 %copy-start.38 = (bf16[2,4,96,1536]{3,2,1,0:T(8,128)(2,1)S(1)}, bf16[2,4,96,1536]{3,2,1,0:T(8,128)(2,1)}, u32[]{:S(2)}) copy-start(bf16[2,4,96,1536]{3,2,1,0:T(8,128)(2,1)} %copy-done.37) | copy-start | bytes 7077892
  351.6 4.1 copy-start.35
  351.6 4.1 copy-start.18
  351.6 4.1 copy-start.41
  355.7 2.6 copy-start.11
  355.7 2.6 copy-start.15
  355.7 2.6 copy-start.31
  358.3 62.2 %copy-start.43 = (bf16[2,4,96,1536]{3,2,1,0:T(8,128)(2,1)S(1)}, bf16[2,4,96,1536]{3,2,1,0:T(8,128)(2,1)}, u32[]{:S(2)}) copy-start(bf16[2,4,96,1536]{3,2,1,0:T(8,128)(2,1)} %get-tuple-element.128) | copy-start | bytes 7077892
  420.4 4.2 copy-start.16
  420.4 4.2 copy-start.27
  420.4 4.2 copy-start.30
  420.4 4.1 copy-start.36
  420.4 2.3 copy-start.40
  420.4 2.6 copy-start.47
  501.0 13.4 %copy-start.46 = (bf16[2,96,1536]{2,1,0:T(8,128)(2,1)S(1)}, bf16[2,96,1536]{2,1,0:T(8,128)(2,1)}, u32[]{:S(2)}) copy-start(bf16[2,96,1536]{2,1,0:T(8,128)(2,1)} %get-tuple-element.135) | copy-start | bytes 1769476
  501.0 14.2 %copy-start.45 = (bf16[2,96,1536]{2,1,0:T(8,128)(2,1)S(1)}, bf16[2,96,1536]{2,1,0:T(8,128)(2,1)}, u32[]{:S(2)}) copy-start(bf16[2,96,1536]{2,1,0:T(8,128)(2,1)} %get-tuple-element.136) | copy-start | bytes 1769476

commit v5 on v4

--- a/solution.py
+++ b/solution.py
@@ -61,7 +61,7 @@
         self.rows = full.shape[1] // CHUNKS
 
     def span(self, c):
-        return pl.ds(c * self.rows, self.rows)
+        return pl.ds(pl.multiple_of(c * self.rows, self.rows), self.rows)
 
     def neighbour(self, d):
         return self.me + 1 if d == 0 else self.me - 1
@@ -140,7 +140,8 @@
 
         @pl.when(goes)
         def _():
-            for c in range(CHUNKS):
+            @pl.loop(0, CHUNKS)
+            def _(c):
                 mine = partial[shard, self.span(c)]
 
                 @pl.when(first)
@@ -161,7 +162,8 @@
 
             @pl.when(there)
             def _():
-                for c in range(CHUNKS):
+                @pl.loop(0, CHUNKS)
+                def _(c):
                     self.sum_copy(d, me, c).wait_recv()
                     total[self.span(c)] += self.rbuf[d, me, self.span(c)].astype(F32)
 
@@ -436,7 +438,7 @@
                 self.kept(a, c).wait()
             self.copy(a, c, t, self.recvs[t][a].at[c]).wait_recv()
             acc, spot = self.accs[a], self.spot(c)
-            acc[spot] = (acc[spot].astype(F32) + self.recvs[t][a][c].astype(F32)).astype(BF16)
+            self.add(acc, spot, self.recvs[t][a], c)
             if t + 1 < self.bits:
                 b = self.order(c)[t + 1]
                 self.copy(a, c, t + 1, acc.at[self.spot(c, [(b, 1 - self.bit[b])])]).start()
@@ -445,6 +447,17 @@
                 b = self.order(c)[t + 1]
                 self.place[c][b] = self.bit[b]
         self.t = t + 1
+
+    def add(self, acc, spot, arrived, c):
+        rows = acc.shape[-2]
+        step = 32 if rows % 32 == 0 else rows
+
+        @pl.loop(0, rows // step)
+        def _(block):
+            part = pl.ds(pl.multiple_of(block * step, step), step)
+            free = (slice(None),) * (len(arrived.shape) - 3)
+            total = acc[(*spot, part)].astype(F32) + arrived[(c, *free, part)].astype(F32)
+            acc[(*spot, part)] = total.astype(BF16)
 
     def put_away(self, a, c):
         return pltpu.make_async_copy(
@@ -810,14 +823,16 @@
     def _(g):
         keys = head_rows(qkv, heads + g)
         values = head_rows(qkv, heads + kv_heads + g)
-        rows = []
-        for member in range(group):
+
+        @pl.loop(0, group)
+        def _(member):
             h = g * group + member
             probs = probabilities(head_rows(qkv, h), keys, allowed)
             attended = dot_nn(probs.astype(BF16), values).astype(BF16)
             o[:, :, lane_block(h)] = attended.reshape(n, -1, LANES)
-            rows.append(attended)
-        small = dot_nt(jnp.concatenate(rows, axis=1), pick_plain(group * HEAD))
+
+        wide_heads = [head_rows(o, g * group + member) for member in range(group)]
+        small = dot_nt(jnp.concatenate(wide_heads, axis=1), pick_plain(group * HEAD))
         osmall[g] = small.astype(BF16).reshape(osmall.shape[1:])
 
     pair.share_half(osmall, o_out)
@@ -874,9 +889,9 @@
     (dh, x, gain, cos, sin, seg_col, seg_row, qkv_in) = refs[:8]
     own, other = refs[8:12], refs[12:16]
     (dx_out, dx_save, gain_out, da_out, dqkv_out) = refs[16:21]
-    (wq, wk, wv, wo, wqkv, qkv, d_o, dqkv, dsmall, part, wsem, tsem) = refs[21:33]
-    pair = Pair(*refs[33:36])
-    line = Line(n, *refs[36:])
+    (wq, wk, wv, wo, wqkv, qkv, d_o, dqkv, dsmall, part, dkv, wsem, tsem) = refs[21:34]
+    pair = Pair(*refs[34:37])
+    line = Line(n, *refs[37:])
     me = line.me
     group = heads // kv_heads
     weights = Weights(layer, wsem)
@@ -911,9 +926,10 @@
     def _(g):
         keys = head_rows(qkv, heads + g)
         values = head_rows(qkv, heads + kv_heads + g)
-        d_keys = d_values = None
-        turned = []
-        for member in range(group):
+        dkv[...] = jnp.zeros_like(dkv)
+
+        @pl.loop(0, group)
+        def _(member):
             h = g * group + member
             queries = head_rows(qkv, h)
             d_out = head_rows(d_o, h)
@@ -922,17 +938,17 @@
             inner = jnp.sum(probs * d_probs, axis=-1, keepdims=True)
             d_scores = (probs * (d_probs - inner)).astype(BF16)
             d_queries = dot_nn(d_scores, keys) * scale
-            turned.append(rotated(d_queries, cosine, sine).astype(BF16))
-            dqkv[:, :, lane_block(h)] = turned[-1].reshape(n, -1, LANES)
-            dk = dot_tn(d_scores, queries)
-            dv = dot_tn(probs.astype(BF16), d_out)
-            d_keys = dk if d_keys is None else d_keys + dk
-            d_values = dv if d_values is None else d_values + dv
-        turned.append(rotated(d_keys * scale, cosine, sine).astype(BF16))
-        dqkv[:, :, lane_block(heads + g)] = turned[-1].reshape(n, -1, LANES)
-        low_values = d_values.astype(BF16)
+            turned = rotated(d_queries, cosine, sine).astype(BF16)
+            dqkv[:, :, lane_block(h)] = turned.reshape(n, -1, LANES)
+            dkv[0] += dot_tn(d_scores, queries)
+            dkv[1] += dot_tn(probs.astype(BF16), d_out)
+
+        low_keys = rotated(dkv[0] * scale, cosine, sine).astype(BF16)
+        low_values = dkv[1].astype(BF16)
+        dqkv[:, :, lane_block(heads + g)] = low_keys.reshape(n, -1, LANES)
         dqkv[:, :, lane_block(heads + kv_heads + g)] = low_values.reshape(n, -1, LANES)
-        small = dot_nt(jnp.concatenate(turned, axis=1), pick_split((group + 1) * HEAD))
+        wide_heads = [head_rows(dqkv, g * group + member) for member in range(group)] + [low_keys]
+        small = dot_nt(jnp.concatenate(wide_heads, axis=1), pick_split((group + 1) * HEAD))
         small_values = dot_nt(low_values, pick_plain(HEAD))
         dsmall[g] = (
             jnp.concatenate([small, small_values], axis=1).astype(BF16).reshape(dsmall.shape[1:])
@@ -976,16 +992,21 @@
     middle = hid.shape[3]
 
     def compute(shard):
-        rows = line.full[shard]
-        g = dot_nn(rows, wg[...])
-        u = dot_nn(rows, wu[...])
-        gate[shard] = g
-        up[shard] = u
-        low = (g * jax.nn.sigmoid(g) * u).astype(BF16)
-        hid[0, shard] = low[:, :middle]
-        hid[1, shard] = low[:, middle:]
+        part[shard] = jnp.zeros(part.shape[1:], F32)
+
+        @pl.loop(0, 2)
+        def _(core):
+            lanes = pl.ds(pl.multiple_of(core * middle, middle), middle)
+            rows = line.full[shard]
+            g = dot_nn(rows, wg[:, lanes])
+            u = dot_nn(rows, wu[:, lanes])
+            gate[shard, :, lanes] = g
+            up[shard, :, lanes] = u
+            low = (g * jax.nn.sigmoid(g) * u).astype(BF16)
+            hid[core, shard] = low
+            part[shard] += dot_nn(low, wd[lanes])
+
         pair.stream(shard)
-        part[shard] = dot_nn(low, wd[...])
 
     pair.stream_share(line.full, n_out)
     pair.stream_share_half(hid, hid_out)
@@ -1040,17 +1061,21 @@
     middle = dmid.shape[3] // 2
 
     def compute(shard):
-        d_hidden = dot_nt(line.full[shard], wd[...])
-        g = gate[shard]
-        sig = jax.nn.sigmoid(g)
-        d_g = (d_hidden * up[shard] * sig * (1.0 + g * (1.0 - sig))).astype(BF16)
-        d_u = (d_hidden * g * sig).astype(BF16)
-        for core in range(2):
-            lanes = slice(core * middle, (core + 1) * middle)
-            dmid[core, shard, :, :middle] = d_g[:, lanes]
-            dmid[core, shard, :, middle:] = d_u[:, lanes]
+        part[shard] = jnp.zeros(part.shape[1:], F32)
+
+        @pl.loop(0, 2)
+        def _(core):
+            lanes = pl.ds(pl.multiple_of(core * middle, middle), middle)
+            d_hidden = dot_nt(line.full[shard], wd[lanes])
+            g = gate[shard, :, lanes]
+            sig = jax.nn.sigmoid(g)
+            d_g = (d_hidden * up[shard, :, lanes] * sig * (1.0 + g * (1.0 - sig))).astype(BF16)
+            d_u = (d_hidden * g * sig).astype(BF16)
+            dmid[core, shard, :, :middle] = d_g
+            dmid[core, shard, :, middle:] = d_u
+            part[shard] += dot_nt(d_g, wg[:, lanes]) + dot_nt(d_u, wu[:, lanes])
+
         pair.stream(shard)
-        part[shard] = dot_nt(d_g, wg[...]) + dot_nt(d_u, wu[...])
 
     pair.stream_share_half(dmid, dmid_out)
     if gathered:
@@ -1186,6 +1211,7 @@
             VMEM((n, rows, wide), BF16),
             VMEM((kv_heads, n, rows, small), BF16),
             VMEM((n, rows, width), F32),
+            VMEM((2, n * rows, LANES), F32),
             DMA((3 + heads,)),
             DMA,
         ]

time: 525 us -> 520 us (level); the launches traced: 517 us -> 519 us
  no operation moved by 1% of the time
where the time goes in v5:
time: 520 us; the launch traced here: 519 us
  Pallas kernels  482 us (93%)
  matrix products  17.5 us (3%)
  local copies, waits for them, and re-layouts  9.76 us (2%)
  other arithmetic  7.8 us (2%)
    pallas_call x9, Pallas kernels, run_kernel(): pl.pallas_call(kernel, name=name, in_specs=[HBM_SPEC if spec in (LOAD, LO...  469 us
    dot_general x8, matrix products, dot_tn(): lax.dot_general(left, right, (((0,), (0,)), ((), ())), preferred_element_...  17.5 us
    pallas_call x1, Pallas kernels, widened(): pl.pallas_call(widen_kernel, name='widen', in_specs=[HBM_SPEC] * 4, out_s...  13.4 us
  transfers between devices with their start and end apart: 1, of which 0 were waited for; matrix products, arithmetic and copies ran while one was open for 1% of the time, Pallas kernels for 0%

profile of v5, /device:TPU:0, one launch (start us, length us, event | category | flops | bytes accessed | tf_op | source)
XLA Modules:
  0.0 519.2 jit_solution(15122575878815422575)
XLA Ops:
  0.6 0.7 pad_maximum_fusion
  1.4 0.6 collective-permute-start
  1.9 0.8 fusion.11
  2.7 0.2 reduce-window.4
  2.9 0.6 slice.39
  3.5 0.8 bitcast_subtract_fusion
  4.2 0.1 convert_reduce_fusion
  4.3 0.8 compare_select_fusion.refs_4_.refs_5_
  5.1 0.7 pad_add_fusion
  5.8 0.1 select_reduce_fusion
  5.9 0.1 reduce_sum.26
  6.0 1.5 fusion.8
  7.6 0.6 compare_select_fusion.1.refs_5_.refs_6_
  8.1 0.7 fusion.10
  8.9 0.6 fusion.13
  9.5 47.9 %attn_fwd0.1 = (f32[96,1536]{1,0:T(8,128)}, f32[96,1536]{1,0:T(8,128)}, bf16[2,4,96,1536]{3,2,1,0:T(8,128)(2,1)}, bf16[4,96,1024]{2,1,0:T(8,128)(2,1)}, bf16[2,4...) custom-call(bf16[2,96,1536]{2,1,0:T(8,128)(2,1)} %refs_1_.1, ...), custom_call_target="tpu_custom_call" | custom-call | flops 1811939328 | bytes 8388608 | tf_op jit(solution)/shard_map/attn_fwd0/pallas_call | solution.py:1124
  57.4 1.1 copy-done.24
  58.5 0.0 copy-start.4
  58.5 0.0 copy-start.7
  58.5 0.0 copy-start.8
  58.6 0.0 copy-start.9
  58.6 0.0 copy-start.10
  58.6 0.0 copy-start.32
  58.6 46.1 %ffn_fwd0.1 = (bf16[96,1536]{1,0:T(8,128)(2,1)S(1)}, bf16[96,1536]{1,0:T(8,128)(2,1)S(1)}, bf16[2,4,96,1536]{3,2,1,0:T(8,128)(2,1)S(1)}, f32[4,96,1024]{2,1,0:T(...) custom-call(f32[96,1536]{1,0:T(8,128)S(1)} %copy-done.24, ...), custom_call_target="tpu_custom_call" | custom-call | flops 3623878656 | bytes 16777216 | tf_op jit(solution)/shard_map/ffn_fwd0/pallas_call | solution.py:1124
  104.7 0.0 copy-start.17
  104.8 0.0 copy-start.37
  104.8 0.0 copy-start.14
  104.9 54.4 %attn_fwd1.1 = (f32[96,1536]{1,0:T(8,128)S(1)}, f32[96,1536]{1,0:T(8,128)S(1)}, bf16[2,4,96,1536]{3,2,1,0:T(8,128)(2,1)}, bf16[4,96,1024]{2,1,0:T(8,128)(2,1)S(1...) custom-call(bf16[96,1536]{1,0:T(8,128)(2,1)S(1)} %get-tuple-element.84.refs_0_, ...), custom_call_target="tpu_custom_call" | custom-call | flops 1811939328 | bytes 8388608 | tf_op jit(solution)/shard_map/attn_fwd1/pallas_call | solution.py:1124
  159.3 0.0 copy-start.19
  159.3 0.9 copy-done.19
  160.2 0.8 copy-done.22
  161.0 0.7 copy-done.25
  161.8 41.7 %ffn_fwd1.1 = (bf16[96,1536]{1,0:T(8,128)(2,1)}, bf16[96,1536]{1,0:T(8,128)(2,1)S(1)}, bf16[2,4,96,1536]{3,2,1,0:T(8,128)(2,1)S(1)}, f32[4,96,1024]{2,1,0:T(8,12...) custom-call(f32[96,1536]{1,0:T(8,128)S(1)} %get-tuple-element.90.refs_0_, ...), custom_call_target="tpu_custom_call" | custom-call | flops 3623878656 | bytes 16777216 | tf_op jit(solution)/shard_map/ffn_fwd1/pallas_call | solution.py:1124
  203.5 0.0 copy-start.12
  203.5 1.1 copy-done.12
  204.6 1.4 fusion
  206.1 0.1 copy-done.13
  206.2 0.1 copy-done.23
  206.3 32.1 %ffn_bwd1.1 = (f32[96,1536]{1,0:T(8,128)S(1)}, f32[1,1536]{1,0:T(1,128)S(1)}, bf16[2,4,96,1024]{3,2,1,0:T(8,128)(2,1)S(1)}, bf16[2,64,1536]{2,1,0:T(8,128)(2,1)S(1)}) custom-call(bf16[2,96,1536]{2,1,0:T(8,128)(2,1)S(1)} %copy-done.10, f32[96,1536]{1,0:T(8,128)S(1)} %copy-done.23, f32[1,1536]{1,0:T(1,128)S(1)} %get-tuple-element.151.refs_1_.refs_2_, ...), custom_call_target="tpu_custom_call" | custom-call | flops 3623878656 | bytes 16777216 | tf_op jit(solution)/shard_map/ffn_bwd1/pallas_call | solution.py:1124
  238.4 0.0 copy-start.20
  238.4 4.0 bitcast_convert_fusion.1
  242.5 56.6 %attn_bwd1.1 = (bf16[96,1536]{1,0:T(8,128)(2,1)S(1)}, bf16[96,1536]{1,0:T(8,128)(2,1)S(1)}, f32[1,1536]{1,0:T(1,128)S(1)}, bf16[2,4,96,1536]{3,2,1,0:T(8,128)(2,...) custom-call(f32[96,1536]{1,0:T(8,128)S(1)} %get-tuple-element.95.ref, ...), custom_call_target="tpu_custom_call" | custom-call | flops 2415919104 | bytes 8388608 | tf_op jit(solution)/shard_map/attn_bwd1/pallas_call | solution.py:1124
  299.2 0.0 copy-start.26
  299.2 1.1 fusion.2
  300.3 0.7 copy-done.42
  301.1 0.7 fusion.4
  301.8 53.1 %ffn_bwd0.1 = (f32[96,1536]{1,0:T(8,128)S(1)}, f32[1,1536]{1,0:T(1,128)S(1)}, bf16[2,4,96,1536]{3,2,1,0:T(8,128)(2,1)}, bf16[2,4,96,1024]{3,2,1,0:T(8,128)(2,1)S...) custom-call(bf16[96,1536]{1,0:T(8,128)(2,1)S(1)} %get-tuple-element., ...), custom_call_target="tpu_custom_call" | custom-call | flops 3623878656 | bytes 16777216 | tf_op jit(solution)/shard_map/ffn_bwd0/pallas_call | solution.py:1124
  354.9 4.0 bitcast_convert_fusion
  359.0 0.0 copy-start.31
  359.0 2.6 fusion.1
  361.6 62.1 %attn_bwd0.1 = (bf16[96,1536]{1,0:T(8,128)(2,1)}, bf16[96,1536]{1,0:T(8,128)(2,1)S(1)}, f32[1,1536]{1,0:T(1,128)S(1)}, bf16[2,4,96,1536]{3,2,1,0:T(8,128)(2,1)},...) custom-call(f32[96,1536]{1,0:T(8,128)S(1)} %get-tuple-element.110.re, ...), custom_call_target="tpu_custom_call" | custom-call | flops 2415919104 | bytes 8388608 | tf_op jit(solution)/shard_map/attn_bwd0/pallas_call | solution.py:1124
  423.7 0.0 copy-start.16
  423.7 0.0 copy-start.27
  423.7 0.0 copy-start.36
  423.8 2.1 fusion.3
  425.9 0.2 copy-done.40
  426.1 0.3 copy-done.47
  426.4 1.5 fusion.5
  427.9 74.9 %tail.1 = (f32[4,1536]{1,0:T(4,128)}, bf16[2,96,1536]{2,1,0:T(8,128)(2,1)}, bf16[2,96,1536]{2,1,0:T(8,128)(2,1)}, bf16[3,2,2,2,192,1024]{5,4,3,2,1,0:T(8,128)(2,...) custom-call(f32[1,1536]{1,0:T(1,128)} %copy-done.36, ...), custom_call_target="tpu_custom_call", output_to_operand_aliasing={{3}: (12, {}), {4}: (13, {}), {5}: (14, {}), {6}: (15, {})} | custom-call | flops 1048576 | bytes 16777216 | tf_op jit(solution)/shard_map/tail/pallas_call | solution.py:1124
  502.8 0.8 slice_select_fusion
  503.6 0.6 fusion.12
  504.2 13.4 %widen.1 = (f32[1536,1024]{1,0:T(8,128)}, f32[1536,1024]{1,0:T(8,128)}, f32[1024,1536]{1,0:T(8,128)}, f32[1536,384]{1,0:T(8,128)}, f32[192,1536]{1,0:T(8,128)}, ...) custom-call(bf16[3,1536,1024]{2,1,0:T(8,128)(2,1)} %bitcast.105, bf16[3,512,1536]{2,1,0:T(8,128)(2,1)} %bitcast.106, ...), custom_call_target="tpu_custom_call" | custom-call | tf_op jit(solution)/shard_map/widen/pallas_call | solution.py:1554
  517.6 0.8 copy.53
  518.4 0.8 copy.54
  (73 shorter events, 0.2 us)
Async XLA Ops:
  1.4 6.7 %collective-permute-start = (bf16[2,1536]{1,0:T(2,128)(2,1)S(1)}, bf16[2,1536]{1,0:T(2,128)(2,1)S(1)}, u32[]{:S(2)}, u32[]{:S(2)}) collective-permute-start(bf16[2,1536]{1,0:T(2,128)(2,1)S(1)} %pad_maximum_fusion), channel_id=1, source_target_pairs={{0,16},{16,0},{1,17},{17,1},{2,18},{18,2},{3,19},{19,3},{4,20},{20... | collective-permute-start | bytes 18440 | tf_op jit(solution)/shard_map/ppermute | solution.py:1568
  57.4 1.1 copy-start.24
  58.5 46.3 %copy-start = (bf16[1,1536,384]{2,1,0:T(8,128)(2,1)S(1)}, bf16[1,1536,384]{2,1,0:T(8,128)(2,1)}, u32[]{:S(2)}) copy-start(bf16[1,1536,384]{2,1,0:T(8,128)(2,1)} %refs_8_.3) | copy-start | bytes 3538948
  58.5 46.3 %copy-start.1 = (bf16[1,384,1536]{2,1,0:T(8,128)(2,1)S(1)}, bf16[1,384,1536]{2,1,0:T(8,128)(2,1)}, u32[]{:S(2)}) copy-start(bf16[1,384,1536]{2,1,0:T(8,128)(2,1)} %refs_11_.5) | copy-start | bytes 3538948
  58.5 46.3 %copy-start.2 = (bf16[1,1536,384]{2,1,0:T(8,128)(2,1)S(1)}, bf16[1,1536,384]{2,1,0:T(8,128)(2,1)}, u32[]{:S(2)}) copy-start(bf16[1,1536,384]{2,1,0:T(8,128)(2,1)} %get-tuple-element.85.refs_11_.refs_12_) | copy-start | bytes 3538948
  58.5 46.3 %copy-start.3 = (bf16[1,1536,192]{1,2,0:T(8,128)(2,1)S(1)}, bf16[1,1536,192]{1,2,0:T(8,128)(2,1)}, u32[]{:S(2)}) copy-start(bf16[1,1536,192]{1,2,0:T(8,128)(2,1)} %param.17) | copy-start | bytes 1769476
  58.5 46.3 %copy-start.4 = (bf16[1,1536,192]{1,2,0:T(8,128)(2,1)S(1)}, bf16[1,1536,192]{1,2,0:T(8,128)(2,1)}, u32[]{:S(2)}) copy-start(bf16[1,1536,192]{1,2,0:T(8,128)(2,1)} %param.18) | copy-start | bytes 1769476
  58.5 46.3 %copy-start.5 = (bf16[1,192,1536]{2,1,0:T(8,128)(2,1)S(1)}, bf16[1,192,1536]{2,1,0:T(8,128)(2,1)}, u32[]{:S(2)}) copy-start(bf16[1,192,1536]{2,1,0:T(8,128)(2,1)} %get-tuple-element.86.refs_12_.refs_13_) | copy-start | bytes 1769476
  58.5 46.3 %copy-start.6 = (bf16[1,192,1536]{2,1,0:T(8,128)(2,1)S(1)}, bf16[1,192,1536]{2,1,0:T(8,128)(2,1)}, u32[]{:S(2)}) copy-start(bf16[1,192,1536]{2,1,0:T(8,128)(2,1)} %get-tuple-element.87.refs_13_.refs_14_) | copy-start | bytes 1769476
  58.5 46.3 %copy-start.7 = (s32[384,1]{1,0:T(8,128)S(1)}, s32[384,1]{1,0:T(8,128)}, u32[]{:S(2)}) copy-start(s32[384,1]{1,0:T(8,128)} %compare_select_fusion.refs_4_.refs_5_) | copy-start | bytes 4612
  58.5 46.3 %copy-start.8 = (f32[4,96,128]{2,1,0:T(8,128)S(1)}, f32[4,96,128]{2,1,0:T(8,128)}, u32[]{:S(2)}) copy-start(f32[4,96,128]{2,1,0:T(8,128)} %get-tuple-element.157.refs_3_.refs_4_) | copy-start | bytes 589828
  58.6 46.3 %copy-start.9 = (f32[4,96,128]{2,1,0:T(8,128)S(1)}, f32[4,96,128]{2,1,0:T(8,128)}, u32[]{:S(2)}) copy-start(f32[4,96,128]{2,1,0:T(8,128)} %get-tuple-element.158.refs_2_.refs_3_) | copy-start | bytes 589828
  58.6 46.3 %copy-start.10 = (bf16[2,96,1536]{2,1,0:T(8,128)(2,1)S(1)}, bf16[2,96,1536]{2,1,0:T(8,128)(2,1)}, u32[]{:S(2)}) copy-start(bf16[2,96,1536]{2,1,0:T(8,128)(2,1)} %refs_0_.3) | copy-start | bytes 1769476
  58.6 46.3 %copy-start.32 = (s32[1,384]{1,0:T(1,128)S(1)}, s32[1,384]{1,0:T(1,128)}, u32[]{:S(2)}) copy-start(s32[1,384]{1,0:T(1,128)} %compare_select_fusion.1.refs_5_.refs_6_) | copy-start | bytes 4612
  104.7 54.5 %copy-start.17 = (bf16[2,4,96,512]{3,2,1,0:T(8,128)(2,1)}, bf16[2,4,96,512]{3,2,1,0:T(8,128)(2,1)S(1)}, u32[]{:S(2)}) copy-start(bf16[2,4,96,512]{3,2,1,0:T(8,128)(2,1)S(1)} %get-tuple-element.114) | copy-start | bytes 2359300
  104.8 54.5 %copy-start.37 = (bf16[2,4,96,1536]{3,2,1,0:T(8,128)(2,1)}, bf16[2,4,96,1536]{3,2,1,0:T(8,128)(2,1)S(1)}, u32[]{:S(2)}) copy-start(bf16[2,4,96,1536]{3,2,1,0:T(8,128)(2,1)S(1)} %get-tuple-element.112) | copy-start | bytes 7077892
  104.8 137.7 %copy-start.14 = (bf16[96,1536]{1,0:T(8,128)(2,1)}, bf16[96,1536]{1,0:T(8,128)(2,1)S(1)}, u32[]{:S(2)}) copy-start(bf16[96,1536]{1,0:T(8,128)(2,1)S(1)} %get-tuple-element.96.refs_1_.refs_4_) | copy-start | bytes 884740
  159.3 0.9 copy-start.19
  160.2 0.8 copy-start.22
  161.0 0.7 copy-start.25
  161.8 42.9 %copy-start.39 = (bf16[2,4,96,1536]{3,2,1,0:T(8,128)(2,1)S(1)}, bf16[2,4,96,1536]{3,2,1,0:T(8,128)(2,1)}, u32[]{:S(2)}) copy-start(bf16[2,4,96,1536]{3,2,1,0:T(8,128)(2,1)} %get-tuple-element.93.refs_11_) | copy-start | bytes 7077892
  203.5 1.1 copy-start.12
  204.6 1.4 copy-start.28
  204.6 1.5 copy-start.13
  204.6 1.6 copy-start.23
  238.4 4.1 copy-start.33
  238.4 4.1 copy-start.20
  242.5 56.7 %copy-start.44 = (bf16[2,4,96,1536]{3,2,1,0:T(8,128)(2,1)S(1)}, bf16[2,4,96,1536]{3,2,1,0:T(8,128)(2,1)}, u32[]{:S(2)}) copy-start(bf16[2,4,96,1536]{3,2,1,0:T(8,128)(2,1)} %get-tuple-element.106) | copy-start | bytes 7077892
  299.1 2.6 copy-start.29
  299.1 2.6 copy-start.34
  299.2 1.2 copy-start.26
  299.2 1.9 copy-start.42
  300.3 1.4 copy-start.21
  301.7 53.2 %copy-start.38 = (bf16[2,4,96,1536]{3,2,1,0:T(8,128)(2,1)S(1)}, bf16[2,4,96,1536]{3,2,1,0:T(8,128)(2,1)}, u32[]{:S(2)}) copy-start(bf16[2,4,96,1536]{3,2,1,0:T(8,128)(2,1)} %copy-done.37) | copy-start | bytes 7077892
  354.9 4.1 copy-start.35
  354.9 4.1 copy-start.18
  354.9 4.1 copy-start.41
  359.0 2.6 copy-start.11
  359.0 2.6 copy-start.15
  359.0 2.6 copy-start.31
  361.6 62.2 %copy-start.43 = (bf16[2,4,96,1536]{3,2,1,0:T(8,128)(2,1)S(1)}, bf16[2,4,96,1536]{3,2,1,0:T(8,128)(2,1)}, u32[]{:S(2)}) copy-start(bf16[2,4,96,1536]{3,2,1,0:T(8,128)(2,1)} %get-tuple-element.128) | copy-start | bytes 7077892
  423.7 4.2 copy-start.16
  423.7 4.2 copy-start.27
  423.7 4.1 copy-start.30
  423.7 4.1 copy-start.36
  423.7 2.3 copy-start.40
  423.7 2.6 copy-start.47
  504.2 13.4 %copy-start.46 = (bf16[2,96,1536]{2,1,0:T(8,128)(2,1)S(1)}, bf16[2,96,1536]{2,1,0:T(8,128)(2,1)}, u32[]{:S(2)}) copy-start(bf16[2,96,1536]{2,1,0:T(8,128)(2,1)} %get-tuple-element.135) | copy-start | bytes 1769476
  504.2 14.2 %copy-start.45 = (bf16[2,96,1536]{2,1,0:T(8,128)(2,1)S(1)}, bf16[2,96,1536]{2,1,0:T(8,128)(2,1)}, u32[]{:S(2)}) copy-start(bf16[2,96,1536]{2,1,0:T(8,128)(2,1)} %get-tuple-element.136) | copy-start | bytes 1769476

commit v6 on v5

--- a/solution.py
+++ b/solution.py
@@ -769,7 +769,9 @@
     at += 13
     if ahead:
         second = Line(n, refs[at], None, None, *refs[at + 1 : at + 3], None, None)
-        at += 3
+        passed = Pair(*refs[at + 3 : at + 6])
+        passed.stream_share(second.full, ahead_out)
+        at += 6
     line = Line(n, *refs[at:])
     me = line.me
     group = heads // kv_heads
@@ -817,6 +819,7 @@
     later_shards(line, compute)
     if ahead:
         second.gather_step(0)
+        passed.stream(me)
     allowed = allowed_pairs(seg_col, seg_row)
 
     @pl.loop(0, kv_heads)
@@ -848,9 +851,15 @@
             def _():
                 second.gather_step(step + 1)
 
+                @pl.loop(0, 2)
+                def _(side):
+                    shard = jnp.where(side == 0, me - step - 1, me + step + 1)
+
+                    @pl.when((shard >= 0) & (shard < n))
+                    def _():
+                        passed.stream(shard)
+
         sums_alone(line, project, part, each)
-        pair.keep(second.full, ahead_out.at[0])
-        pair.send(second.full, ahead_out.at[1])
     else:
         sums_alone(line, project, part, lambda step: None)
     h_out[...] = x[...].astype(F32) + part[me]
@@ -858,6 +867,7 @@
     pair.keep(h_out, h_save)
     if ahead:
         second.gather_end()
+        passed.wait(n)
     line.gather_end()
     line.sum_end()
     if layer == 0:
@@ -1176,7 +1186,11 @@
             DMA((3 + heads,)),
         ]
         + pair_scratch(n, 5, 3 + (len(own) if other is None else 0))
-        + ([VMEM((n, rows, width), BF16)] + [DMA((2, n, CHUNKS))] * 2 if layer == 1 else [])
+        + (
+            [VMEM((n, rows, width), BF16)] + [DMA((2, n, CHUNKS))] * 2 + pair_scratch(n, 1, 1)
+            if layer == 1
+            else []
+        )
         + line_scratch(n, rows, width)
     )
     body = functools.partial(attn_fwd_kernel, layer, n, heads, kv_heads, len(own))

time: 520 us -> 521 us (level)
  no operation moved by 1% of the time
where the time goes in v6:
time: 521 us; the launch traced here: 520 us
  Pallas kernels  483 us (93%)
  matrix products  17.4 us (3%)
  local copies, waits for them, and re-layouts  9.76 us (2%)
  other arithmetic  7.8 us (1%)
    pallas_call x9, Pallas kernels, run_kernel(): pl.pallas_call(kernel, name=name, in_specs=[HBM_SPEC if spec in (LOAD, LO...  470 us
    dot_general x8, matrix products, dot_tn(): lax.dot_general(left, right, (((0,), (0,)), ((), ())), preferred_element_...  17.4 us
    pallas_call x1, Pallas kernels, widened(): pl.pallas_call(widen_kernel, name='widen', in_specs=[HBM_SPEC] * 4, out_s...  13.4 us
  transfers between devices with their start and end apart: 1, of which 0 were waited for; matrix products, arithmetic and copies ran while one was open for 1% of the time, Pallas kernels for 0%

profile of v6, /device:TPU:0, one launch (start us, length us, event | category | flops | bytes accessed | tf_op | source)
XLA Modules:
  0.0 519.9 jit_solution(11323260665495643272)
XLA Ops:
  0.6 0.7 pad_maximum_fusion
  1.4 0.6 collective-permute-start
  1.9 0.8 fusion.11
  2.7 0.2 reduce-window.4
  2.9 0.6 slice.39
  3.5 0.8 bitcast_subtract_fusion
  4.2 0.1 convert_reduce_fusion
  4.3 0.8 compare_select_fusion.refs_4_.refs_5_
  5.1 0.7 pad_add_fusion
  5.8 0.1 select_reduce_fusion
  5.9 0.1 reduce_sum.26
  6.0 1.5 fusion.8
  7.6 0.6 compare_select_fusion.1.refs_5_.refs_6_
  8.1 0.7 fusion.10
  8.9 0.6 fusion.13
  9.5 47.9 %attn_fwd0.1 = (f32[96,1536]{1,0:T(8,128)}, f32[96,1536]{1,0:T(8,128)}, bf16[2,4,96,1536]{3,2,1,0:T(8,128)(2,1)}, bf16[4,96,1024]{2,1,0:T(8,128)(2,1)}, bf16[2,4...) custom-call(bf16[2,96,1536]{2,1,0:T(8,128)(2,1)} %refs_1_.1, ...), custom_call_target="tpu_custom_call" | custom-call | flops 1811939328 | bytes 8388608 | tf_op jit(solution)/shard_map/attn_fwd0/pallas_call | solution.py:1134
  57.4 1.1 copy-done.24
  58.5 0.0 copy-start.4
  58.5 0.0 copy-start.7
  58.5 0.0 copy-start.8
  58.6 0.0 copy-start.9
  58.6 0.0 copy-start.10
  58.6 0.0 copy-start.32
  58.6 46.1 %ffn_fwd0.1 = (bf16[96,1536]{1,0:T(8,128)(2,1)S(1)}, bf16[96,1536]{1,0:T(8,128)(2,1)S(1)}, bf16[2,4,96,1536]{3,2,1,0:T(8,128)(2,1)S(1)}, f32[4,96,1024]{2,1,0:T(...) custom-call(f32[96,1536]{1,0:T(8,128)S(1)} %copy-done.24, ...), custom_call_target="tpu_custom_call" | custom-call | flops 3623878656 | bytes 16777216 | tf_op jit(solution)/shard_map/ffn_fwd0/pallas_call | solution.py:1134
  104.7 0.0 copy-start.17
  104.8 0.0 copy-start.37
  104.8 0.0 copy-start.14
  104.9 54.5 %attn_fwd1.1 = (f32[96,1536]{1,0:T(8,128)S(1)}, f32[96,1536]{1,0:T(8,128)S(1)}, bf16[2,4,96,1536]{3,2,1,0:T(8,128)(2,1)}, bf16[4,96,1024]{2,1,0:T(8,128)(2,1)S(1...) custom-call(bf16[96,1536]{1,0:T(8,128)(2,1)S(1)} %get-tuple-element.84.refs_0_, ...), custom_call_target="tpu_custom_call" | custom-call | flops 1811939328 | bytes 8388608 | tf_op jit(solution)/shard_map/attn_fwd1/pallas_call | solution.py:1134
  159.4 0.0 copy-start.19
  159.4 0.9 copy-done.19
  160.3 0.8 copy-done.22
  161.1 0.7 copy-done.25
  161.9 41.7 %ffn_fwd1.1 = (bf16[96,1536]{1,0:T(8,128)(2,1)}, bf16[96,1536]{1,0:T(8,128)(2,1)S(1)}, bf16[2,4,96,1536]{3,2,1,0:T(8,128)(2,1)S(1)}, f32[4,96,1024]{2,1,0:T(8,12...) custom-call(f32[96,1536]{1,0:T(8,128)S(1)} %get-tuple-element.90.refs_0_, ...), custom_call_target="tpu_custom_call" | custom-call | flops 3623878656 | bytes 16777216 | tf_op jit(solution)/shard_map/ffn_fwd1/pallas_call | solution.py:1134
  203.6 1.1 copy-done.12
  204.7 1.4 fusion
  206.2 0.1 copy-done.13
  206.3 0.1 copy-done.23
  206.4 32.1 %ffn_bwd1.1 = (f32[96,1536]{1,0:T(8,128)S(1)}, f32[1,1536]{1,0:T(1,128)S(1)}, bf16[2,4,96,1024]{3,2,1,0:T(8,128)(2,1)S(1)}, bf16[2,64,1536]{2,1,0:T(8,128)(2,1)S(1)}) custom-call(bf16[2,96,1536]{2,1,0:T(8,128)(2,1)S(1)} %copy-done.10, f32[96,1536]{1,0:T(8,128)S(1)} %copy-done.23, f32[1,1536]{1,0:T(1,128)S(1)} %get-tuple-element.151.refs_1_.refs_2_, ...), custom_call_target="tpu_custom_call" | custom-call | flops 3623878656 | bytes 16777216 | tf_op jit(solution)/shard_map/ffn_bwd1/pallas_call | solution.py:1134
  238.5 0.0 copy-start.20
  238.6 4.0 bitcast_convert_fusion.1
  242.6 56.6 %attn_bwd1.1 = (bf16[96,1536]{1,0:T(8,128)(2,1)S(1)}, bf16[96,1536]{1,0:T(8,128)(2,1)S(1)}, f32[1,1536]{1,0:T(1,128)S(1)}, bf16[2,4,96,1536]{3,2,1,0:T(8,128)(2,...) custom-call(f32[96,1536]{1,0:T(8,128)S(1)} %get-tuple-element.95.ref, ...), custom_call_target="tpu_custom_call" | custom-call | flops 2415919104 | bytes 8388608 | tf_op jit(solution)/shard_map/attn_bwd1/pallas_call | solution.py:1134
  299.3 0.0 copy-start.26
  299.3 1.1 fusion.2
  300.5 0.7 copy-done.42
  301.2 0.7 fusion.4
  301.9 53.6 %ffn_bwd0.1 = (f32[96,1536]{1,0:T(8,128)S(1)}, f32[1,1536]{1,0:T(1,128)S(1)}, bf16[2,4,96,1536]{3,2,1,0:T(8,128)(2,1)}, bf16[2,4,96,1024]{3,2,1,0:T(8,128)(2,1)S...) custom-call(bf16[96,1536]{1,0:T(8,128)(2,1)S(1)} %get-tuple-element., ...), custom_call_target="tpu_custom_call" | custom-call | flops 3623878656 | bytes 16777216 | tf_op jit(solution)/shard_map/ffn_bwd0/pallas_call | solution.py:1134
  355.5 0.0 copy-start.18
  355.5 4.0 bitcast_convert_fusion
  359.5 0.0 copy-start.11
  359.6 0.0 copy-start.31
  359.6 2.6 fusion.1
  362.2 62.1 %attn_bwd0.1 = (bf16[96,1536]{1,0:T(8,128)(2,1)}, bf16[96,1536]{1,0:T(8,128)(2,1)S(1)}, f32[1,1536]{1,0:T(1,128)S(1)}, bf16[2,4,96,1536]{3,2,1,0:T(8,128)(2,1)},...) custom-call(f32[96,1536]{1,0:T(8,128)S(1)} %get-tuple-element.110.re, ...), custom_call_target="tpu_custom_call" | custom-call | flops 2415919104 | bytes 8388608 | tf_op jit(solution)/shard_map/attn_bwd0/pallas_call | solution.py:1134
  424.3 0.0 copy-start.30
  424.3 0.0 copy-start.36
  424.3 2.1 fusion.3
  426.4 0.2 copy-done.40
  426.6 0.3 copy-done.47
  426.9 1.5 fusion.5
  428.4 75.0 %tail.1 = (f32[4,1536]{1,0:T(4,128)}, bf16[2,96,1536]{2,1,0:T(8,128)(2,1)}, bf16[2,96,1536]{2,1,0:T(8,128)(2,1)}, bf16[3,2,2,2,192,1024]{5,4,3,2,1,0:T(8,128)(2,...) custom-call(f32[1,1536]{1,0:T(1,128)} %copy-done.36, ...), custom_call_target="tpu_custom_call", output_to_operand_aliasing={{3}: (12, {}), {4}: (13, {}), {5}: (14, {}), {6}: (15, {})} | custom-call | flops 1048576 | bytes 16777216 | tf_op jit(solution)/shard_map/tail/pallas_call | solution.py:1134
  503.5 0.8 slice_select_fusion
  504.3 0.6 fusion.12
  504.9 13.4 %widen.1 = (f32[1536,1024]{1,0:T(8,128)}, f32[1536,1024]{1,0:T(8,128)}, f32[1024,1536]{1,0:T(8,128)}, f32[1536,384]{1,0:T(8,128)}, f32[192,1536]{1,0:T(8,128)}, ...) custom-call(bf16[3,1536,1024]{2,1,0:T(8,128)(2,1)} %bitcast.105, bf16[3,512,1536]{2,1,0:T(8,128)(2,1)} %bitcast.106, ...), custom_call_target="tpu_custom_call" | custom-call | tf_op jit(solution)/shard_map/widen/pallas_call | solution.py:1568
  518.3 0.8 copy.53
  519.1 0.8 copy.54
  (73 shorter events, 0.2 us)
Async XLA Ops:
  1.4 6.7 %collective-permute-start = (bf16[2,1536]{1,0:T(2,128)(2,1)S(1)}, bf16[2,1536]{1,0:T(2,128)(2,1)S(1)}, u32[]{:S(2)}, u32[]{:S(2)}) collective-permute-start(bf16[2,1536]{1,0:T(2,128)(2,1)S(1)} %pad_maximum_fusion), channel_id=1, source_target_pairs={{0,16},{16,0},{1,17},{17,1},{2,18},{18,2},{3,19},{19,3},{4,20},{20... | collective-permute-start | bytes 18440 | tf_op jit(solution)/shard_map/ppermute | solution.py:1582
  57.4 1.1 copy-start.24
  58.5 46.3 %copy-start = (bf16[1,1536,384]{2,1,0:T(8,128)(2,1)S(1)}, bf16[1,1536,384]{2,1,0:T(8,128)(2,1)}, u32[]{:S(2)}) copy-start(bf16[1,1536,384]{2,1,0:T(8,128)(2,1)} %refs_8_.3) | copy-start | bytes 3538948
  58.5 46.3 %copy-start.1 = (bf16[1,384,1536]{2,1,0:T(8,128)(2,1)S(1)}, bf16[1,384,1536]{2,1,0:T(8,128)(2,1)}, u32[]{:S(2)}) copy-start(bf16[1,384,1536]{2,1,0:T(8,128)(2,1)} %refs_11_.5) | copy-start | bytes 3538948
  58.5 46.3 %copy-start.2 = (bf16[1,1536,384]{2,1,0:T(8,128)(2,1)S(1)}, bf16[1,1536,384]{2,1,0:T(8,128)(2,1)}, u32[]{:S(2)}) copy-start(bf16[1,1536,384]{2,1,0:T(8,128)(2,1)} %get-tuple-element.85.refs_11_.refs_12_) | copy-start | bytes 3538948
  58.5 46.3 %copy-start.3 = (bf16[1,1536,192]{1,2,0:T(8,128)(2,1)S(1)}, bf16[1,1536,192]{1,2,0:T(8,128)(2,1)}, u32[]{:S(2)}) copy-start(bf16[1,1536,192]{1,2,0:T(8,128)(2,1)} %param.17) | copy-start | bytes 1769476
  58.5 46.3 %copy-start.4 = (bf16[1,1536,192]{1,2,0:T(8,128)(2,1)S(1)}, bf16[1,1536,192]{1,2,0:T(8,128)(2,1)}, u32[]{:S(2)}) copy-start(bf16[1,1536,192]{1,2,0:T(8,128)(2,1)} %param.18) | copy-start | bytes 1769476
  58.5 46.3 %copy-start.5 = (bf16[1,192,1536]{2,1,0:T(8,128)(2,1)S(1)}, bf16[1,192,1536]{2,1,0:T(8,128)(2,1)}, u32[]{:S(2)}) copy-start(bf16[1,192,1536]{2,1,0:T(8,128)(2,1)} %get-tuple-element.86.refs_12_.refs_13_) | copy-start | bytes 1769476
  58.5 46.3 %copy-start.6 = (bf16[1,192,1536]{2,1,0:T(8,128)(2,1)S(1)}, bf16[1,192,1536]{2,1,0:T(8,128)(2,1)}, u32[]{:S(2)}) copy-start(bf16[1,192,1536]{2,1,0:T(8,128)(2,1)} %get-tuple-element.87.refs_13_.refs_14_) | copy-start | bytes 1769476
  58.5 46.3 %copy-start.7 = (s32[384,1]{1,0:T(8,128)S(1)}, s32[384,1]{1,0:T(8,128)}, u32[]{:S(2)}) copy-start(s32[384,1]{1,0:T(8,128)} %compare_select_fusion.refs_4_.refs_5_) | copy-start | bytes 4612
  58.5 46.3 %copy-start.8 = (f32[4,96,128]{2,1,0:T(8,128)S(1)}, f32[4,96,128]{2,1,0:T(8,128)}, u32[]{:S(2)}) copy-start(f32[4,96,128]{2,1,0:T(8,128)} %get-tuple-element.157.refs_3_.refs_4_) | copy-start | bytes 589828
  58.6 46.3 %copy-start.9 = (f32[4,96,128]{2,1,0:T(8,128)S(1)}, f32[4,96,128]{2,1,0:T(8,128)}, u32[]{:S(2)}) copy-start(f32[4,96,128]{2,1,0:T(8,128)} %get-tuple-element.158.refs_2_.refs_3_) | copy-start | bytes 589828
  58.6 46.3 %copy-start.10 = (bf16[2,96,1536]{2,1,0:T(8,128)(2,1)S(1)}, bf16[2,96,1536]{2,1,0:T(8,128)(2,1)}, u32[]{:S(2)}) copy-start(bf16[2,96,1536]{2,1,0:T(8,128)(2,1)} %refs_0_.3) | copy-start | bytes 1769476
  58.6 46.3 %copy-start.32 = (s32[1,384]{1,0:T(1,128)S(1)}, s32[1,384]{1,0:T(1,128)}, u32[]{:S(2)}) copy-start(s32[1,384]{1,0:T(1,128)} %compare_select_fusion.1.refs_5_.refs_6_) | copy-start | bytes 4612
  104.7 54.7 %copy-start.17 = (bf16[2,4,96,512]{3,2,1,0:T(8,128)(2,1)}, bf16[2,4,96,512]{3,2,1,0:T(8,128)(2,1)S(1)}, u32[]{:S(2)}) copy-start(bf16[2,4,96,512]{3,2,1,0:T(8,128)(2,1)S(1)} %get-tuple-element.114) | copy-start | bytes 2359300
  104.8 54.7 %copy-start.37 = (bf16[2,4,96,1536]{3,2,1,0:T(8,128)(2,1)}, bf16[2,4,96,1536]{3,2,1,0:T(8,128)(2,1)S(1)}, u32[]{:S(2)}) copy-start(bf16[2,4,96,1536]{3,2,1,0:T(8,128)(2,1)S(1)} %get-tuple-element.112) | copy-start | bytes 7077892
  104.8 137.8 %copy-start.14 = (bf16[96,1536]{1,0:T(8,128)(2,1)}, bf16[96,1536]{1,0:T(8,128)(2,1)S(1)}, u32[]{:S(2)}) copy-start(bf16[96,1536]{1,0:T(8,128)(2,1)S(1)} %get-tuple-element.96.refs_1_.refs_4_) | copy-start | bytes 884740
  159.4 0.9 copy-start.19
  160.3 0.8 copy-start.22
  161.1 0.7 copy-start.25
  161.9 42.9 %copy-start.39 = (bf16[2,4,96,1536]{3,2,1,0:T(8,128)(2,1)S(1)}, bf16[2,4,96,1536]{3,2,1,0:T(8,128)(2,1)}, u32[]{:S(2)}) copy-start(bf16[2,4,96,1536]{3,2,1,0:T(8,128)(2,1)} %get-tuple-element.93.refs_11_) | copy-start | bytes 7077892
  203.6 1.1 copy-start.12
  204.7 1.4 copy-start.28
  204.7 1.5 copy-start.13
  204.7 1.6 copy-start.23
  238.5 4.1 copy-start.33
  238.5 4.1 copy-start.20
  242.6 56.7 %copy-start.44 = (bf16[2,4,96,1536]{3,2,1,0:T(8,128)(2,1)S(1)}, bf16[2,4,96,1536]{3,2,1,0:T(8,128)(2,1)}, u32[]{:S(2)}) copy-start(bf16[2,4,96,1536]{3,2,1,0:T(8,128)(2,1)} %get-tuple-element.106) | copy-start | bytes 7077892
  299.3 2.6 copy-start.29
  299.3 2.6 copy-start.34
  299.3 1.2 copy-start.26
  299.3 1.9 copy-start.42
  300.4 1.4 copy-start.21
  301.9 53.6 %copy-start.38 = (bf16[2,4,96,1536]{3,2,1,0:T(8,128)(2,1)S(1)}, bf16[2,4,96,1536]{3,2,1,0:T(8,128)(2,1)}, u32[]{:S(2)}) copy-start(bf16[2,4,96,1536]{3,2,1,0:T(8,128)(2,1)} %copy-done.37) | copy-start | bytes 7077892
  355.4 4.1 copy-start.35
  355.5 4.1 copy-start.18
  355.5 4.1 copy-start.41
  359.5 2.6 copy-start.11
  359.6 2.6 copy-start.15
  359.6 2.6 copy-start.31
  362.2 62.2 %copy-start.43 = (bf16[2,4,96,1536]{3,2,1,0:T(8,128)(2,1)S(1)}, bf16[2,4,96,1536]{3,2,1,0:T(8,128)(2,1)}, u32[]{:S(2)}) copy-start(bf16[2,4,96,1536]{3,2,1,0:T(8,128)(2,1)} %get-tuple-element.128) | copy-start | bytes 7077892
  424.2 4.2 copy-start.16
  424.2 4.2 copy-start.27
  424.3 4.1 copy-start.30
  424.3 4.1 copy-start.36
  424.3 2.3 copy-start.40
  424.3 2.6 copy-start.47
  504.9 13.4 %copy-start.46 = (bf16[2,96,1536]{2,1,0:T(8,128)(2,1)S(1)}, bf16[2,96,1536]{2,1,0:T(8,128)(2,1)}, u32[]{:S(2)}) copy-start(bf16[2,96,1536]{2,1,0:T(8,128)(2,1)} %get-tuple-element.135) | copy-start | bytes 1769476
  504.9 14.2 %copy-start.45 = (bf16[2,96,1536]{2,1,0:T(8,128)(2,1)S(1)}, bf16[2,96,1536]{2,1,0:T(8,128)(2,1)}, u32[]{:S(2)}) copy-start(bf16[2,96,1536]{2,1,0:T(8,128)(2,1)} %get-tuple-element.136) | copy-start | bytes 1769476
